TPU v7x, 256 devices: a whole 4x4x8 slice. The times are simulated.
256 devices in a mesh: blk: 16 (over z, y_lo), grp: 16 (over x, y_hi, core).
Axes of the slice: x: 4, y: 4 (y_hi: 2, y_lo: 2; y = y_hi * 2 + y_lo), z: 8, core: 2. Of those that a mesh axis runs over, the one named last changes fastest.
Arguments:
- frames: bfloat16 [16, 4096, 1024], P('grp', 'blk'), may hold values from -16 to 16
- utt_lengths: int32 [8], replicated, may hold values from 1 to 16384, 65536 in all
- attn_gain: float32 [1024], replicated, may hold values from 0.25 to 1.75
- w_qkv: bfloat16 [1024, 3072], P(None, 'grp'), may hold values from -4 to 4
- w_out: bfloat16 [1024, 1024], replicated, may hold values from -0.375 to 0.375
- conv_gain: float32 [1024], replicated, may hold values from 0.25 to 1.75
- w_glu: bfloat16 [1024, 2048], replicated, may hold values from -0.1875 to 0.1875
- w_depth: float32 [31, 1024], replicated, may hold values from -1 to 1
- depth_gain: float32 [1024], replicated, may hold values from 0.25 to 1.75
- w_proj: bfloat16 [1024, 1024], replicated, may hold values from -0.1875 to 0.1875
Outputs:
- block_out: bfloat16 [16, 4096, 1024], P('grp', 'blk')
Inputs may be any that keep to these rules, and one draw needn't show every extreme that they name: `utt_lengths`: they sum to 65536 and the longest is exactly 16384.
All inputs are finite; a program needn't handle non-finite values.
Results may differ from a plain program's by a relative error of at most 0.0095.
Values may be sent and summed in bfloat16 or wider, within the bound.
No kernel may reach another device: no remote copies, remote signals or barrier semaphores. Data moves between devices by JAX's collectives and lax.ppermute only.
A program may use at most 192 MiB of HBM per device.

v0:
```python
import jax
import jax.numpy as jnp
from jax import lax
from jax.experimental import pallas as pl
from jax.experimental.pallas import tpu as pltpu
from jax.sharding import PartitionSpec as P


HEAD = 64
LANES = 128
KEY_CHUNK = 512
QUERY_PARTS = 2
OFFSETS = (0, 1, 3, 2)
LOG2E = 1.4426950408889634

epsilon = 1e-05
big_negative = -1e30


VMEM = pl.BlockSpec(memory_space=pltpu.VMEM)
SMEM = pl.BlockSpec(memory_space=pltpu.SMEM)


def coords(index):
    b, g = divmod(index, 16)
    return g // 4, (g // 2) % 2, g % 2, b // 2, b % 2


def flat(x, yh, core, z, yl):
    return ((z % 8) * 2 + yl) * 16 + (x % 4) * 4 + yh * 2 + core


def send(value, target):
    pairs = []
    for source in range(256):
        to = target(*coords(source))
        if to is not None:
            pairs.append((source, to if isinstance(to, int) else flat(*to)))
    return lax.ppermute(value, ("blk", "grp"), pairs)


def normalize(values, row_gain):
    center = values - jnp.mean(values, axis=-1, keepdims=True)
    spread = jnp.mean(center * center, axis=-1, keepdims=True)
    return center * lax.rsqrt(spread + epsilon) * row_gain


def segment_of(utt_lengths, positions):
    starts = jnp.cumsum(utt_lengths) - utt_lengths
    started = (starts[None, :] <= positions[:, None]).astype(jnp.int32)
    return jnp.sum(started, axis=1) - 1


def low_lanes(rows):
    return lax.broadcasted_iota(jnp.int32, (rows, LANES), 1) < HEAD


def swap_lanes(values):
    return pltpu.roll(values, HEAD, 1)


def project(normed, slot_ref, shards, weights, scale):
    near, far = shards[:4], shards[4]
    for i in range(4):
        weights[pl.ds(pl.multiple_of(slot_ref[i] * HEAD, HEAD), HEAD), :] = near[i][...]
        weights[pl.ds(pl.multiple_of(slot_ref[4 + i] * HEAD, HEAD), HEAD), :] = far[i * HEAD : (i + 1) * HEAD]
    rows = normed.shape[0] // 2
    low = low_lanes(rows)
    for pair in range(4):
        both = lax.dot_general(
            normed[...],
            weights[pair * LANES : (pair + 1) * LANES, :],
            (((1,), (1,)), ((), ())),
            preferred_element_type=jnp.float32,
        )
        if scale is not None:
            both = both * scale
        own, other = both[:rows], both[rows:]
        yield 2 * pair, jnp.where(low, own, swap_lanes(other)).astype(jnp.bfloat16)
        yield 2 * pair + 1, jnp.where(low, swap_lanes(own), other).astype(jnp.bfloat16)


def first_kernel(slot_ref, own_ref, other_ref, gain_ref, *refs):
    shards, (out, normed), weights = refs[:5], refs[5:7], refs[7]
    rows = own_ref.shape[0]
    gain = gain_ref[0:1, :]
    normed[:rows] = normalize(own_ref[...].astype(jnp.float32), gain).astype(jnp.bfloat16)
    normed[rows:] = normalize(other_ref[...].astype(jnp.float32), gain).astype(jnp.bfloat16)
    for head, packed in project(normed, slot_ref, shards, weights, None):
        out[head] = packed


def project_first(slots, own, other, gain, shards):
    rows, width = own.shape
    return pl.pallas_call(
        first_kernel,
        out_shape=[
            jax.ShapeDtypeStruct((8, rows, LANES), jnp.bfloat16),
            jax.ShapeDtypeStruct((2 * rows, width), jnp.bfloat16),
        ],
        in_specs=[SMEM] + [VMEM] * 8,
        out_specs=[VMEM] * 2,
        scratch_shapes=[pltpu.VMEM((8 * HEAD, width), jnp.bfloat16)],
        compiler_params=pltpu.CompilerParams(vmem_limit_bytes=24 * 1024 * 1024),
    )(slots, own, other, gain, *shards)


def next_kernel(parts, scale):
    def kernel(slot_ref, normed, *refs):
        shards, outs, weights = refs[:5], refs[5:-1], refs[-1]
        step = outs[0].shape[1]
        for head, packed in project(normed, slot_ref, shards, weights, scale):
            for i in range(parts):
                outs[i][head] = packed[i * step : (i + 1) * step]

    return kernel


def project_next(slots, normed, shards, parts, scale):
    rows, width = normed.shape[0] // 2, normed.shape[1]
    return pl.pallas_call(
        next_kernel(parts, scale),
        out_shape=[jax.ShapeDtypeStruct((8, rows // parts, LANES), jnp.bfloat16)] * parts,
        in_specs=[SMEM] + [VMEM] * 6,
        out_specs=[VMEM] * parts,
        scratch_shapes=[pltpu.VMEM((8 * HEAD, width), jnp.bfloat16)],
        compiler_params=pltpu.CompilerParams(vmem_limit_bytes=24 * 1024 * 1024),
    )(slots, normed, *shards)


def attend_kernel(base_ref, lo_ref, hi_ref, q_ref, k_ref, v_ref, out_ref, *scratch):
    keys, values, queries, scores_a, scores_b, max_a, max_b = scratch
    sources, half, _ = k_ref.shape
    part = q_ref.shape[1]
    block = 2 * part
    lo, hi = lo_ref[0:1, :], hi_ref[0:1, :]

    def inside(rows, base):
        position = lax.broadcasted_iota(jnp.int32, (rows, LANES), 0) + base
        return (position >= lo) & (position < hi)

    low_half, low_part, low_quarter = low_lanes(half), low_lanes(part), low_lanes(part // 2)

    def prepare(s, carry):
        key, value, query = (ref[s].astype(jnp.float32) for ref in (k_ref, v_ref, q_ref))
        for side in range(2):
            base = base_ref[side] + s * (2 * half)
            at = pl.ds(pl.multiple_of(s * (2 * half) + side * half, half), half)
            mask = jnp.where(inside(half, base), 0.0, big_negative)
            keys[at, :] = jnp.where(low_half, swap_lanes(key) if side else key, mask).astype(jnp.bfloat16)
            values[at, :] = jnp.where(low_half, 1.0, value if side else swap_lanes(value)).astype(jnp.bfloat16)
            at = pl.ds(pl.multiple_of(s * block + side * part, part), part)
            mark = jnp.where(inside(part, base + base_ref[2]), 1.0, 0.0)
            queries[at, :] = jnp.where(low_part, swap_lanes(query) if side else query, mark).astype(jnp.bfloat16)
        return carry

    lax.fori_loop(0, sources, prepare, 0)
    window = keys.shape[0]
    chunks = window // KEY_CHUNK

    def score(query, j, scores, best):
        part = lax.dot_general(
            query,
            keys[j * KEY_CHUNK : (j + 1) * KEY_CHUNK, :],
            (((1,), (1,)), ((), ())),
            preferred_element_type=jnp.float32,
        )
        scores[:, j * KEY_CHUNK : (j + 1) * KEY_CHUNK] = part
        for t in range(KEY_CHUNK // LANES):
            piece = part[:, t * LANES : (t + 1) * LANES]
            best = piece if best is None else jnp.maximum(best, piece)
        return best

    def weigh(j, scores, row_max, total):
        probs = jnp.exp2(scores[:, j * KEY_CHUNK : (j + 1) * KEY_CHUNK] - row_max)
        part = jnp.dot(
            probs.astype(jnp.bfloat16),
            values[j * KEY_CHUNK : (j + 1) * KEY_CHUNK, :],
            preferred_element_type=jnp.float32,
        )
        return part if total is None else total + part

    def finish(total, source):
        mixed = total / swap_lanes(total)
        for side in range(2):
            upper = swap_lanes(mixed[side * part : side * part + part // 2])
            lower = mixed[side * part + part // 2 : (side + 1) * part]
            out_ref[2 * source + base_ref[3 + side]] = jnp.where(low_quarter, upper, lower).astype(jnp.bfloat16)

    def both(i, new, old, i_old):
        query = queries[pl.ds(pl.multiple_of(i * block, block), block), :]
        row_max = old[1][:, 0:1]
        best, total = None, None
        for j in range(chunks):
            best = score(query, j, new[0], best)
            total = weigh(j, old[0], row_max, total)
        new[1][...] = jnp.broadcast_to(jnp.max(best, axis=1, keepdims=True), (block, LANES))
        finish(total, i_old)

    buffer_a, buffer_b = (scores_a, max_a), (scores_b, max_b)

    def step(i, carry):
        both(2 * i, buffer_a, buffer_b, jnp.maximum(2 * i - 1, 0))
        both(2 * i + 1, buffer_b, buffer_a, 2 * i)
        return carry

    lax.fori_loop(0, sources // 2, step, 0)
    total = None
    for j in range(chunks):
        total = weigh(j, scores_b, max_b[:, 0:1], total)
    finish(total, sources - 1)


def attend(bases, lo, hi, query, key, value):
    sources, half, _ = key.shape
    part = query.shape[1]
    window = 2 * half * sources
    return pl.pallas_call(
        attend_kernel,
        out_shape=jax.ShapeDtypeStruct((2 * sources, part // 2, LANES), jnp.bfloat16),
        in_specs=[SMEM] + [VMEM] * 5,
        out_specs=VMEM,
        scratch_shapes=[pltpu.VMEM((window, LANES), jnp.bfloat16)] * 2
        + [pltpu.VMEM((2 * part * sources, LANES), jnp.bfloat16)]
        + [pltpu.VMEM((2 * part, window), jnp.float32)] * 2
        + [pltpu.VMEM((2 * part, LANES), jnp.float32)] * 2,
        compiler_params=pltpu.CompilerParams(vmem_limit_bytes=24 * 1024 * 1024),
    )(bases, lo, hi, query, key, value)


def gate_kernel(*refs):
    parts = refs[:QUERY_PARTS]
    frames, gain, w_out_hbm, w_glu_hbm, residual_ref, gated_ref = refs[QUERY_PARTS:-5]
    w_out, w_glu, attended, out_sem, glu_sem = refs[-5:]
    out_copy = pltpu.make_async_copy(w_out_hbm, w_out, out_sem)
    glu_copy = pltpu.make_async_copy(w_glu_hbm, w_glu, glu_sem)
    out_copy.start()
    glu_copy.start()
    heads, quarter, _ = parts[0].shape
    low = low_lanes(quarter)
    for i in range(QUERY_PARTS):
        for pair in range(heads // 2):
            even = parts[i][2 * pair].astype(jnp.float32)
            odd = parts[i][2 * pair + 1].astype(jnp.float32)
            upper = jnp.where(low, even, swap_lanes(odd)).astype(jnp.bfloat16)
            lower = jnp.where(low, swap_lanes(even), odd).astype(jnp.bfloat16)
            at = slice(pair * LANES, (pair + 1) * LANES)
            attended[2 * i * quarter : (2 * i + 1) * quarter, at] = upper
            attended[(2 * i + 1) * quarter : (2 * i + 2) * quarter, at] = lower
    out_copy.wait()
    projected = jnp.dot(attended[...], w_out[...], preferred_element_type=jnp.float32)
    residual = (frames[...].astype(jnp.float32) + projected).astype(jnp.bfloat16)
    residual_ref[...] = residual
    width = frames.shape[1]
    conv_in = normalize(residual.astype(jnp.float32), gain[0:1, :]).astype(jnp.bfloat16)
    glu_copy.wait()
    step = 256
    for j in range(0, width, step):
        a = jnp.dot(conv_in, w_glu[:, j : j + step], preferred_element_type=jnp.float32)
        b = jnp.dot(conv_in, w_glu[:, width + j : width + j + step], preferred_element_type=jnp.float32)
        gated_ref[:, j : j + step] = (a * jax.nn.sigmoid(b)).astype(jnp.bfloat16)


def gate(parts, frames, gain, w_out, w_glu):
    shape = jax.ShapeDtypeStruct(frames.shape, jnp.bfloat16)
    anywhere = pl.BlockSpec(memory_space=pl.ANY)
    return pl.pallas_call(
        gate_kernel,
        out_shape=[shape, shape],
        in_specs=[VMEM] * (QUERY_PARTS + 2) + [anywhere] * 2,
        out_specs=[VMEM] * 2,
        scratch_shapes=[
            pltpu.VMEM(w_out.shape, jnp.bfloat16),
            pltpu.VMEM(w_glu.shape, jnp.bfloat16),
            pltpu.VMEM(frames.shape, jnp.bfloat16),
            pltpu.SemaphoreType.DMA,
            pltpu.SemaphoreType.DMA,
        ],
        compiler_params=pltpu.CompilerParams(vmem_limit_bytes=24 * 1024 * 1024),
    )(*parts, frames, gain, w_out, w_glu)


def body(
    frames, utt_lengths, attn_gain, w_qkv, w_out, conv_gain, w_glu, w_depth, depth_gain, w_proj
):
    frame_rows = frames.shape[1]
    width = frames.shape[2]
    kernel_half = (w_depth.shape[0] - 1) // 2
    block_index = lax.axis_index("blk")
    group_index = lax.axis_index("grp")
    yl = block_index % 2
    x, core = group_index // 4, group_index % 2
    window_start = group_index * (16 * frame_rows)
    first_frame = window_start + block_index * frame_rows
    local_frames = frames[0]

    other_frames = send(local_frames, lambda x, yh, c, z, yl: (x, yh, c, z, 1 - yl))
    shard = w_qkv.T

    def route(offset):
        return lambda x, yh, c, z, yl: (
            (x - offset, yh, yh, z, c) if yl == c else (x - offset, 1 - yh, yh, z, c)
        )

    def collect(part):
        own = shard[part * HEAD : (part + 1) * HEAD]
        near = [send(own, route(offset)) for offset in OFFSETS]
        swap = lambda x, yh, c, z, yl: (x, yh, 1 - c, z, yl)
        far = send(jnp.concatenate(near, axis=0), swap)
        return near + [far]

    slots = jnp.stack([2 * ((x + offset) % 4) + c for c in (core, 1 - core) for offset in OFFSETS])
    key_shards, value_shards, query_shards = collect(1), collect(2), collect(0)
    key, normed = project_first(slots, local_frames, other_frames, attn_gain[None, :], key_shards)
    (value,) = project_next(slots, normed, value_shards, 1, None)
    queries = project_next(slots, normed, query_shards, QUERY_PARTS, HEAD**-0.5 * LOG2E)

    def along_z(packed):
        groups = [[2 * z + yl for z in range(8)] for yl in range(2)]
        return lax.all_to_all(packed, "blk", 0, 0, axis_index_groups=groups, tiled=True)

    key, value = along_z(key), along_z(value)
    queries = [along_z(queries[i]) for i in range(QUERY_PARTS)]
    ends = jnp.cumsum(utt_lengths)
    pad = (HEAD, HEAD - utt_lengths.shape[0])
    lo = jnp.pad(ends - utt_lengths, pad)[None, :]
    hi = jnp.pad(ends, pad)[None, :]
    mixed = []
    for i in range(QUERY_PARTS):
        base = window_start + jnp.stack([yl, 1 - yl]) * frame_rows
        bases = jnp.concatenate([base, jnp.stack([i * (frame_rows // QUERY_PARTS) + 0 * yl, yl, 1 - yl])])
        part = attend(bases.astype(jnp.int32), lo, hi, queries[i], key, value)
        mixed.append(lax.all_to_all(part, "blk", 0, 0, tiled=True))
    residual, gated = gate(mixed, local_frames, conv_gain[None, :], w_out, w_glu)

    def neighbour(step):
        def target(x, yh, c, z, yl):
            place = (x * 4 + yh * 2 + c) * 16 + z * 2 + yl + step
            return (place % 16) * 16 + place // 16 if 0 <= place < 256 else None

        return target

    rim = kernel_half + 1
    left = send(gated[frame_rows - rim :], neighbour(1))
    right = send(gated[:rim], neighbour(-1))
    local_seg = segment_of(utt_lengths, first_frame + jnp.arange(frame_rows, dtype=jnp.int32))
    extended = jnp.concatenate([left[1:], gated, right[:-1]], axis=0).astype(jnp.float32)
    extended_seg = segment_of(
        utt_lengths,
        first_frame - kernel_half + jnp.arange(frame_rows + 2 * kernel_half, dtype=jnp.int32),
    )
    mixed_conv = jnp.zeros((frame_rows, width), jnp.float32)
    for offset in range(2 * kernel_half + 1):
        same_seg = (extended_seg[offset : offset + frame_rows] == local_seg)[:, None]
        mixed_conv = mixed_conv + jnp.where(
            same_seg, extended[offset : offset + frame_rows] * w_depth[offset], 0.0
        )
    normed_conv = normalize(mixed_conv, depth_gain)
    activated = (normed_conv * jax.nn.sigmoid(normed_conv)).astype(jnp.bfloat16)
    result = (
        residual.astype(jnp.float32)
        + jnp.dot(activated, w_proj, preferred_element_type=jnp.float32)
    ).astype(jnp.bfloat16)
    return result[None]


def solution(mesh):
    in_specs = (P("grp", "blk", None), P(), P(), P(None, "grp"), P(), P(), P(), P(), P(), P())
    out_specs = P("grp", "blk", None)
    return jax.shard_map(body, mesh=mesh, in_specs=in_specs, out_specs=out_specs, check_vma=False)
```

profile of v0, /device:TPU:16, one launch (start us, length us, event | category | flops | bytes accessed | tf_op | source)
XLA Modules:
  0.0 212.8 jit_solution(1115682807944040943)
XLA Ops:
  1.2 1.9 collective-permute-start.1
  3.1 2.4 %collective-permute-start.2 = (bf16[64,1024]{1,0:T(8,128)(2,1)S(1)}, bf16[64,1024]{1,0:T(8,128)(2,1)S(1)}, u32[]{:S(2)}, u32[]{:S(2)}) collective-permute-start(bf16[64,1024]{1,0:T(8,128)(2,1)S(1)} %get-tuple-element.23), channel_id=1, source_target_pairs={{0,12},{1,30},{2,15},{3,29},{4,0},{5,18},{6,3},{7,17},{8,4},{9,22}... | collective-permute-start | bytes 393224 | tf_op jit(solution)/shard_map/ppermute | solution.py:39
  5.6 3.6 %collective-permute-start.4 = (bf16[64,1024]{1,0:T(8,128)(2,1)S(1)}, bf16[64,1024]{1,0:T(8,128)(2,1)S(1)}, u32[]{:S(2)}, u32[]{:S(2)}) collective-permute-start(bf16[64,1024]{1,0:T(8,128)(2,1)S(1)} %get-tuple-element.23), channel_id=1, source_target_pairs={{0,8},{1,26},{2,11},{3,25},{4,12},{5,30},{6,15},{7,29},{8,0},{9,18... | collective-permute-start | bytes 393224 | tf_op jit(solution)/shard_map/ppermute | solution.py:39
  9.2 1.9 collective-permute-start.6
  12.7 4.1 %collective-permute-done.3.refs_2_ = bf16[64,1024]{1,0:T(8,128)(2,1)S(1)} collective-permute-done((bf16[64,1024]{1,0:T(8,128)(2,1)S(1)}, bf16[64,1024]{1,0:T(8,128)(2,1)S(1)}, u32[]{:S(2)}, u32[]{:S(2)}) %collective-permute-start.3) | collective-permute-done | bytes 131104 | tf_op jit(solution)/shard_map/ppermute | solution.py:39
  16.8 5.7 %collective-permute-start = (bf16[256,1024]{1,0:T(8,128)(2,1)}, bf16[256,1024]{1,0:T(8,128)(2,1)S(1)}, u32[]{:S(2)}, u32[]{:S(2)}) collective-permute-start(bf16[256,1024]{1,0:T(8,128)(2,1)} %bitcast.56), channel_id=1, source_target_pairs={{0,16},{1,17},{2,18},{3,19},{4,20},{5,21},{6,22},{7,23},{8,24},{9,... | collective-permute-start | bytes 1572872 | tf_op jit(solution)/shard_map/ppermute | solution.py:39
  23.5 1.8 collective-permute-done.9.refs_3_
  26.8 2.4 %collective-permute-start.11 = (bf16[64,1024]{1,0:T(8,128)(2,1)S(1)}, bf16[64,1024]{1,0:T(8,128)(2,1)S(1)}, u32[]{:S(2)}, u32[]{:S(2)}) collective-permute-start(bf16[64,1024]{1,0:T(8,128)(2,1)S(1)} %get-tuple-element.21), channel_id=1, source_target_pairs={{0,0},{1,18},{2,3},{3,17},{4,4},{5,22},{6,7},{7,21},{8,8},{9,26},{... | collective-permute-start | bytes 393224 | tf_op jit(solution)/shard_map/ppermute | solution.py:39
  29.2 1.9 collective-permute-start.12
  31.2 2.5 %collective-permute-done.11.refs_0_ = bf16[64,1024]{1,0:T(8,128)(2,1)S(1)} collective-permute-done((bf16[64,1024]{1,0:T(8,128)(2,1)S(1)}, bf16[64,1024]{1,0:T(8,128)(2,1)S(1)}, u32[]{:S(2)}, u32[]{:S(2)}) %collective-permute-start.11) | collective-permute-done | bytes 131104 | tf_op jit(solution)/shard_map/ppermute | solution.py:39
  33.7 2.4 %collective-permute-done.12.refs_1_ = bf16[64,1024]{1,0:T(8,128)(2,1)S(1)} collective-permute-done((bf16[64,1024]{1,0:T(8,128)(2,1)S(1)}, bf16[64,1024]{1,0:T(8,128)(2,1)S(1)}, u32[]{:S(2)}, u32[]{:S(2)}) %collective-permute-start.12) | collective-permute-done | bytes 131104 | tf_op jit(solution)/shard_map/ppermute | solution.py:39
  36.4 4.3 %collective-permute-done.13.refs_2_ = bf16[64,1024]{1,0:T(8,128)(2,1)S(1)} collective-permute-done((bf16[64,1024]{1,0:T(8,128)(2,1)S(1)}, bf16[64,1024]{1,0:T(8,128)(2,1)S(1)}, u32[]{:S(2)}, u32[]{:S(2)}) %collective-permute-start.13) | collective-permute-done | bytes 131104 | tf_op jit(solution)/shard_map/ppermute | solution.py:39
  40.7 3.8 %collective-permute-done.14.refs_3_ = bf16[64,1024]{1,0:T(8,128)(2,1)S(1)} collective-permute-done((bf16[64,1024]{1,0:T(8,128)(2,1)S(1)}, bf16[64,1024]{1,0:T(8,128)(2,1)S(1)}, u32[]{:S(2)}, u32[]{:S(2)}) %collective-permute-start.14) | collective-permute-done | bytes 131104 | tf_op jit(solution)/shard_map/ppermute | solution.py:39
  52.7 2.3 %shard_map.100 = (bf16[8,256,128]{2,1,0:T(8,128)(2,1)S(1)}, bf16[512,1024]{1,0:T(8,128)(2,1)S(1)}) custom-call(s32[8]{0:T(128)S(1)} %stack.54.slot_ref, bf16[256,1024]{1,0:T(8,128)(2,1)S(1)} %bitcast.57, bf16[256,1024]{1,0:T(8,128)(2,1)S(1)} %copy-done.9, f32[1,1024]{1,0:T(1,128)S(1)} %bitcast.59, bf16[64,1024]{1,0:T(8,128)(2,1)S(1)} %collective-permute-done.1.refs_0_, ...), custom_call_target="tpu_custom_call" | custom-call | tf_op jit(solution)/shard_map/pallas_call | solution.py:95
  55.9 2.4 %shard_map.101 = (bf16[8,128,128]{2,1,0:T(8,128)(2,1)S(1)}, bf16[8,128,128]{2,1,0:T(8,128)(2,1)S(1)}) custom-call(s32[8]{0:T(128)S(1)} %stack.54.slot_ref, bf16[512,1024]{1,0:T(8,128)(2,1)S(1)} %get-tuple-element.11.normed, bf16[64,1024]{1,0:T(8,128)(2,1)S(1)} %collective-permute-done.6.refs_0_, bf16[64,1024]{1,0:T(8,128)(2,1)S(1)} %copy-done.18, ...), custom_call_target="tpu_custom_call" | custom-call | tf_op jit(solution)/shard_map/pallas_call | solution.py:121
  59.8 8.5 %all-to-all-start.4 = ((bf16[8,128,128]{2,1,0:T(8,128)(2,1)}), bf16[8,128,128]{2,1,0:T(8,128)(2,1)S(1)}, u32[]{:S(2)}, u32[]{:S(2)}) async-start(bf16[8,128,128]{2,1,0:T(8,128)(2,1)} %copy-done.32), calls=%async_computation.4 | async-start | bytes 524288 | tf_op jit(solution)/shard_map/all_to_all | solution.py:320
  71.9 2.4 %shard_map.102 = bf16[8,256,128]{2,1,0:T(8,128)(2,1)S(1)} custom-call(s32[8]{0:T(128)S(1)} %stack.54.slot_ref, bf16[512,1024]{1,0:T(8,128)(2,1)S(1)} %get-tuple-element.11.normed, bf16[64,1024]{1,0:T(8,128)(2,1)S(1)} %copy-done.24, bf16[64,1024]{1,0:T(8,128)(2,1)S(1)} %copy-done.26, bf16[64,1024]{1,0:T(8,128)(2,1)S(1)} %copy-done.28, ...), custom_call_target="tpu_custom_call" | custom-call | tf_op jit(solution)/shard_map/pallas_call | solution.py:121
  75.1 5.6 %all-to-all-done.4.q_ref = bf16[8,128,128]{2,1,0:T(8,128)(2,1)S(1)} async-done(((bf16[8,128,128]{2,1,0:T(8,128)(2,1)}), bf16[8,128,128]{2,1,0:T(8,128)(2,1)S(1)}, u32[]{:S(2)}, u32[]{:S(2)}) %all-to-all-start.4) | async-done | bytes 262176 | tf_op jit(solution)/shard_map/all_to_all | solution.py:320
  80.7 21.3 %all_to_all.30.v_ref = bf16[8,256,128]{2,1,0:T(8,128)(2,1)S(1)} all-to-all(bf16[8,256,128]{2,1,0:T(8,128)(2,1)} %copy-done.5), channel_id=1, replica_groups={{0,32,64,96,128,160,192,224},{16,48,80,112,144,176,208,240},{1,33,65,97..., dimensions={0} | all-to-all | bytes 1048576 | tf_op jit(solution)/shard_map/all_to_all | solution.py:320
  102.0 3.5 %all-to-all-start.1 = ((bf16[8,256,128]{2,1,0:T(8,128)(2,1)}), bf16[8,256,128]{2,1,0:T(8,128)(2,1)S(1)}, u32[]{:S(2)}, u32[]{:S(2)}) async-start(bf16[8,256,128]{2,1,0:T(8,128)(2,1)} %copy-done.12), calls=%async_computation.1 | async-start | bytes 1048576 | tf_op jit(solution)/shard_map/all_to_all | solution.py:320
  105.7 17.1 %all-to-all-done.1.k_ref = bf16[8,256,128]{2,1,0:T(8,128)(2,1)S(1)} async-done(((bf16[8,256,128]{2,1,0:T(8,128)(2,1)}), bf16[8,256,128]{2,1,0:T(8,128)(2,1)S(1)}, u32[]{:S(2)}, u32[]{:S(2)}) %all-to-all-start.1) | async-done | bytes 524320 | tf_op jit(solution)/shard_map/all_to_all | solution.py:320
  122.8 4.0 %all-to-all-start = ((bf16[8,128,128]{2,1,0:T(8,128)(2,1)}), bf16[8,128,128]{2,1,0:T(8,128)(2,1)}, u32[]{:S(2)}, u32[]{:S(2)}) async-start(bf16[8,128,128]{2,1,0:T(8,128)(2,1)} %copy-done.31), calls=%async_computation | async-start | bytes 524288 | tf_op jit(solution)/shard_map/all_to_all | solution.py:320
  127.1 13.0 %shard_map.104 = bf16[16,64,128]{2,1,0:T(8,128)(2,1)S(1)} custom-call(s32[5]{0:T(128)S(1)} %get-tuple-element.86.base_ref, s32[1,128]{1,0:T(1,128)S(1)} %get-tuple-element.89.lo_ref, s32[1,128]{1,0:T(1,128)S(1)} %get-tuple-element.88.hi_ref, bf16[8,128,128]{2,1,0:T(8,128)(2,1)S(1)} %all-to-all-done.4.q_ref, bf16[8,256,128]{2,1,0:T(8,128)(2,1)S(1)} %all-to-all-done.1.k_ref, ...), custom_call_target="tpu_custom_call" | custom-call | tf_op jit(solution)/shard_map/pallas_call | solution.py:218
  140.9 12.4 %all-to-all-start.5 = ((bf16[16,64,128]{2,1,0:T(8,128)(2,1)}), bf16[16,64,128]{2,1,0:T(8,128)(2,1)S(1)}, u32[]{:S(2)}, u32[]{:S(2)}) async-start(bf16[16,64,128]{2,1,0:T(8,128)(2,1)} %copy-done.7), calls=%async_computation.5 | async-start | bytes 524288 | tf_op jit(solution)/shard_map/all_to_all | solution.py:333
  153.5 13.4 %shard_map.103 = bf16[16,64,128]{2,1,0:T(8,128)(2,1)S(1)} custom-call(s32[5]{0:T(128)S(1)} %get-tuple-element.87.base_ref, s32[1,128]{1,0:T(1,128)S(1)} %get-tuple-element.89.lo_ref, s32[1,128]{1,0:T(1,128)S(1)} %get-tuple-element.88.hi_ref, bf16[8,128,128]{2,1,0:T(8,128)(2,1)} %all-to-all-done.q_ref, bf16[8,256,128]{2,1,0:T(8,128)(2,1)S(1)} %all-to-all-done.1.k_ref, ...), custom_call_target="tpu_custom_call" | custom-call | tf_op jit(solution)/shard_map/pallas_call | solution.py:218
  167.6 8.1 %all-to-all-start.3 = ((bf16[16,64,128]{2,1,0:T(8,128)(2,1)}), bf16[16,64,128]{2,1,0:T(8,128)(2,1)S(1)}, u32[]{:S(2)}, u32[]{:S(2)}) async-start(bf16[16,64,128]{2,1,0:T(8,128)(2,1)} %copy-done.6), calls=%async_computation.3 | async-start | bytes 524288 | tf_op jit(solution)/shard_map/all_to_all | solution.py:333
  178.4 8.9 %all-to-all-done.3.refs_0_ = bf16[16,64,128]{2,1,0:T(8,128)(2,1)S(1)} async-done(((bf16[16,64,128]{2,1,0:T(8,128)(2,1)}), bf16[16,64,128]{2,1,0:T(8,128)(2,1)S(1)}, u32[]{:S(2)}, u32[]{:S(2)}) %all-to-all-start.3) | async-done | bytes 262176 | tf_op jit(solution)/shard_map/all_to_all | solution.py:333
  187.3 2.2 %copy-done.1 = bf16[1024,2048]{1,0:T(8,128)(2,1)S(1)} copy-done((bf16[1024,2048]{1,0:T(8,128)(2,1)S(1)}, bf16[1024,2048]{1,0:T(8,128)(2,1)}, u32[]{:S(2)}) %copy-start.1) | copy-done | bytes 4194328
  192.1 3.0 %shard_map.105 = (bf16[256,1024]{1,0:T(8,128)(2,1)S(1)}, bf16[256,1024]{1,0:T(8,128)(2,1)S(1)}) custom-call(bf16[16,64,128]{2,1,0:T(8,128)(2,1)S(1)} %all-to-all-done.3.refs_0_, bf16[16,64,128]{2,1,0:T(8,128)(2,1)S(1)} %all-to-all-done.5.refs_1_, bf16[256,1024]{1,0:T(8,128)(2,1)S(1)} %bitcast.58, f32[1,1024]{1,0:T(1,128)S(1)} %bitcast.60, ...), custom_call_target="tpu_custom_call" | custom-call | tf_op jit(solution)/shard_map/pallas_call | solution.py:267
  195.1 2.4 %collective-permute-start.16 = (bf16[16,1024]{1,0:T(8,128)(2,1)S(1)}, bf16[16,1024]{1,0:T(8,128)(2,1)S(1)}, u32[]{:S(2)}, u32[]{:S(2)}) collective-permute-start(bf16[16,1024]{1,0:T(8,128)(2,1)S(1)} %get-tuple-element.19), channel_id=1, source_target_pairs={{0,16},{1,17},{2,18},{3,19},{4,20},{5,21},{6,22},{7,23},{8,24},{9,... | collective-permute-start | bytes 98312 | tf_op jit(solution)/shard_map/ppermute | solution.py:39
  197.5 5.3 %collective-permute-start.17 = (bf16[16,1024]{1,0:T(8,128)(2,1)S(1)}, bf16[16,1024]{1,0:T(8,128)(2,1)S(1)}, u32[]{:S(2)}, u32[]{:S(2)}) collective-permute-start(bf16[16,1024]{1,0:T(8,128)(2,1)S(1)} %get-tuple-element.20), channel_id=1, source_target_pairs={{1,240},{2,241},{3,242},{4,243},{5,244},{6,245},{7,246},{8,247},{9... | collective-permute-start | bytes 98312 | tf_op jit(solution)/shard_map/ppermute | solution.py:39
  204.6 6.3 %fusion.69 = (f32[256]{0:T(256)S(1)}, f32[256,1024]{1,0:T(8,128)S(1)}) fusion(f32[1024]{0:T(1024)S(1)} %bitcast.73, f32[286,1024]{1,0:T(8,128)S(1)} %maximum_convert_fusion, pred[256]{0:T(512)(128)(4,1)S(1)} %get-tuple-element.56, f32[1024]{0:T(1024)S(1)} %bitcast.74, pred[256]{0:T(512)(128)(4,1)S(1)} %get-tuple-element.57, f32[1024]{0:T(1024)S(1)} %bitcast.76, ...), kind=kLoop, calls=%fused_computation.152 | loop fusion | flops 24379136 | bytes 33690368 | tf_op jit(solution)/shard_map/reduce_sum | solution.py:43
  (122 shorter events, 31.3 us)
Async XLA Ops:
  0.0 211.1 %copy-start = (bf16[1024,1024]{1,0:T(8,128)(2,1)S(1)}, bf16[1024,1024]{1,0:T(8,128)(2,1)}, u32[]{:S(2)}) copy-start(bf16[1024,1024]{1,0:T(8,128)(2,1)} %param.19) | copy-start | bytes 6291460
  1.2 9.9 %collective-permute-start.1 = (bf16[64,1024]{1,0:T(8,128)(2,1)S(1)}, bf16[64,1024]{1,0:T(8,128)(2,1)S(1)}, u32[]{:S(2)}, u32[]{:S(2)}) collective-permute-start(bf16[64,1024]{1,0:T(8,128)(2,1)S(1)} %get-tuple-element.23), channel_id=1, source_target_pairs={{0,0},{1,18},{2,3},{3,17},{4,4},{5,22},{6,7},{7,21},{8,8},{9,26},{... | collective-permute-start | bytes 393224 | tf_op jit(solution)/shard_map/ppermute | solution.py:39
  3.1 9.0 %collective-permute-start.2 = (bf16[64,1024]{1,0:T(8,128)(2,1)S(1)}, bf16[64,1024]{1,0:T(8,128)(2,1)S(1)}, u32[]{:S(2)}, u32[]{:S(2)}) collective-permute-start(bf16[64,1024]{1,0:T(8,128)(2,1)S(1)} %get-tuple-element.23), channel_id=1, source_target_pairs={{0,12},{1,30},{2,15},{3,29},{4,0},{5,18},{6,3},{7,17},{8,4},{9,22}... | collective-permute-start | bytes 393224 | tf_op jit(solution)/shard_map/ppermute | solution.py:39
  5.6 11.2 %collective-permute-start.3 = (bf16[64,1024]{1,0:T(8,128)(2,1)S(1)}, bf16[64,1024]{1,0:T(8,128)(2,1)S(1)}, u32[]{:S(2)}, u32[]{:S(2)}) collective-permute-start(bf16[64,1024]{1,0:T(8,128)(2,1)S(1)} %get-tuple-element.23), channel_id=1, source_target_pairs={{0,4},{1,22},{2,7},{3,21},{4,8},{5,26},{6,11},{7,25},{8,12},{9,30}... | collective-permute-start | bytes 393224 | tf_op jit(solution)/shard_map/ppermute | solution.py:39
  5.6 11.3 %collective-permute-start.4 = (bf16[64,1024]{1,0:T(8,128)(2,1)S(1)}, bf16[64,1024]{1,0:T(8,128)(2,1)S(1)}, u32[]{:S(2)}, u32[]{:S(2)}) collective-permute-start(bf16[64,1024]{1,0:T(8,128)(2,1)S(1)} %get-tuple-element.23), channel_id=1, source_target_pairs={{0,8},{1,26},{2,11},{3,25},{4,12},{5,30},{6,15},{7,29},{8,0},{9,18... | collective-permute-start | bytes 393224 | tf_op jit(solution)/shard_map/ppermute | solution.py:39
  9.2 14.2 %collective-permute-start.6 = (bf16[64,1024]{1,0:T(8,128)(2,1)S(1)}, bf16[64,1024]{1,0:T(8,128)(2,1)S(1)}, u32[]{:S(2)}, u32[]{:S(2)}) collective-permute-start(bf16[64,1024]{1,0:T(8,128)(2,1)S(1)} %get-tuple-element.22), channel_id=1, source_target_pairs={{0,0},{1,18},{2,3},{3,17},{4,4},{5,22},{6,7},{7,21},{8,8},{9,26},{... | collective-permute-start | bytes 393224 | tf_op jit(solution)/shard_map/ppermute | solution.py:39
  11.1 12.4 %collective-permute-start.7 = (bf16[64,1024]{1,0:T(8,128)(2,1)S(1)}, bf16[64,1024]{1,0:T(8,128)(2,1)S(1)}, u32[]{:S(2)}, u32[]{:S(2)}) collective-permute-start(bf16[64,1024]{1,0:T(8,128)(2,1)S(1)} %get-tuple-element.22), channel_id=1, source_target_pairs={{0,12},{1,30},{2,15},{3,29},{4,0},{5,18},{6,3},{7,17},{8,4},{9,22}... | collective-permute-start | bytes 393224 | tf_op jit(solution)/shard_map/ppermute | solution.py:39
  12.1 11.4 %collective-permute-start.8 = (bf16[64,1024]{1,0:T(8,128)(2,1)S(1)}, bf16[64,1024]{1,0:T(8,128)(2,1)S(1)}, u32[]{:S(2)}, u32[]{:S(2)}) collective-permute-start(bf16[64,1024]{1,0:T(8,128)(2,1)S(1)} %get-tuple-element.22), channel_id=1, source_target_pairs={{0,4},{1,22},{2,7},{3,21},{4,8},{5,26},{6,11},{7,25},{8,12},{9,30}... | collective-permute-start | bytes 393224 | tf_op jit(solution)/shard_map/ppermute | solution.py:39
  16.8 6.5 %copy-start.13 = (bf16[64,1024]{1,0:T(8,128)(2,1)}, bf16[64,1024]{1,0:T(8,128)(2,1)S(1)}, u32[]{:S(2)}) copy-start(bf16[64,1024]{1,0:T(8,128)(2,1)S(1)} %collective-permute-done.3.refs_2_) | copy-start | bytes 393220
  16.8 8.4 %collective-permute-start.9 = (bf16[64,1024]{1,0:T(8,128)(2,1)S(1)}, bf16[64,1024]{1,0:T(8,128)(2,1)S(1)}, u32[]{:S(2)}, u32[]{:S(2)}) collective-permute-start(bf16[64,1024]{1,0:T(8,128)(2,1)S(1)} %get-tuple-element.22), channel_id=1, source_target_pairs={{0,8},{1,26},{2,11},{3,25},{4,12},{5,30},{6,15},{7,29},{8,0},{9,18... | collective-permute-start | bytes 393224 | tf_op jit(solution)/shard_map/ppermute | solution.py:39
  16.8 6.5 %copy-start.15 = (bf16[64,1024]{1,0:T(8,128)(2,1)}, bf16[64,1024]{1,0:T(8,128)(2,1)S(1)}, u32[]{:S(2)}) copy-start(bf16[64,1024]{1,0:T(8,128)(2,1)S(1)} %collective-permute-done.4.refs_3_) | copy-start | bytes 393220
  16.8 29.3 %collective-permute-start = (bf16[256,1024]{1,0:T(8,128)(2,1)}, bf16[256,1024]{1,0:T(8,128)(2,1)S(1)}, u32[]{:S(2)}, u32[]{:S(2)}) collective-permute-start(bf16[256,1024]{1,0:T(8,128)(2,1)} %bitcast.56), channel_id=1, source_target_pairs={{0,16},{1,17},{2,18},{3,19},{4,20},{5,21},{6,22},{7,23},{8,24},{9,... | collective-permute-start | bytes 1572872 | tf_op jit(solution)/shard_map/ppermute | solution.py:39
  23.4 24.4 %copy-start.33 = (f32[1024]{0:T(1024)S(1)}, f32[1024]{0:T(1024)}, u32[]{:S(2)}) copy-start(f32[1024]{0:T(1024)} %param.12) | copy-start | bytes 12292
  23.4 23.6 %collective-permute-start.5 = (bf16[256,1024]{1,0:T(8,128)(2,1)}, bf16[256,1024]{1,0:T(8,128)(2,1)S(1)}, u32[]{:S(2)}, u32[]{:S(2)}) collective-permute-start(bf16[256,1024]{1,0:T(8,128)(2,1)} %pad_maximum_fusion), channel_id=1, source_target_pairs={{0,1},{1,0},{2,3},{3,2},{4,5},{5,4},{6,7},{7,6},{8,9},{9,8},{10,11... | collective-permute-start | bytes 1572872 | tf_op jit(solution)/shard_map/ppermute | solution.py:39
  26.8 29.1 %collective-permute-start.10 = (bf16[256,1024]{1,0:T(8,128)(2,1)}, bf16[256,1024]{1,0:T(8,128)(2,1)}, u32[]{:S(2)}, u32[]{:S(2)}) collective-permute-start(bf16[256,1024]{1,0:T(8,128)(2,1)} %pad_maximum_fusion.1), channel_id=1, source_target_pairs={{0,1},{1,0},{2,3},{3,2},{4,5},{5,4},{6,7},{7,6},{8,9},{9,8},{10,11... | collective-permute-start | bytes 1572872 | tf_op jit(solution)/shard_map/ppermute | solution.py:39
  26.8 6.9 %collective-permute-start.11 = (bf16[64,1024]{1,0:T(8,128)(2,1)S(1)}, bf16[64,1024]{1,0:T(8,128)(2,1)S(1)}, u32[]{:S(2)}, u32[]{:S(2)}) collective-permute-start(bf16[64,1024]{1,0:T(8,128)(2,1)S(1)} %get-tuple-element.21), channel_id=1, source_target_pairs={{0,0},{1,18},{2,3},{3,17},{4,4},{5,22},{6,7},{7,21},{8,8},{9,26},{... | collective-permute-start | bytes 393224 | tf_op jit(solution)/shard_map/ppermute | solution.py:39
  29.2 6.8 %collective-permute-start.12 = (bf16[64,1024]{1,0:T(8,128)(2,1)S(1)}, bf16[64,1024]{1,0:T(8,128)(2,1)S(1)}, u32[]{:S(2)}, u32[]{:S(2)}) collective-permute-start(bf16[64,1024]{1,0:T(8,128)(2,1)S(1)} %get-tuple-element.21), channel_id=1, source_target_pairs={{0,12},{1,30},{2,15},{3,29},{4,0},{5,18},{6,3},{7,17},{8,4},{9,22}... | collective-permute-start | bytes 393224 | tf_op jit(solution)/shard_map/ppermute | solution.py:39
  33.7 7.1 %collective-permute-start.13 = (bf16[64,1024]{1,0:T(8,128)(2,1)S(1)}, bf16[64,1024]{1,0:T(8,128)(2,1)S(1)}, u32[]{:S(2)}, u32[]{:S(2)}) collective-permute-start(bf16[64,1024]{1,0:T(8,128)(2,1)S(1)} %get-tuple-element.21), channel_id=1, source_target_pairs={{0,4},{1,22},{2,7},{3,21},{4,8},{5,26},{6,11},{7,25},{8,12},{9,30}... | collective-permute-start | bytes 393224 | tf_op jit(solution)/shard_map/ppermute | solution.py:39
  36.0 9.3 %copy-start.25 = (bf16[64,1024]{1,0:T(8,128)(2,1)}, bf16[64,1024]{1,0:T(8,128)(2,1)S(1)}, u32[]{:S(2)}) copy-start(bf16[64,1024]{1,0:T(8,128)(2,1)S(1)} %collective-permute-done.12.refs_1_) | copy-start | bytes 393220
  36.0 8.4 %collective-permute-start.14 = (bf16[64,1024]{1,0:T(8,128)(2,1)S(1)}, bf16[64,1024]{1,0:T(8,128)(2,1)S(1)}, u32[]{:S(2)}, u32[]{:S(2)}) collective-permute-start(bf16[64,1024]{1,0:T(8,128)(2,1)S(1)} %get-tuple-element.21), channel_id=1, source_target_pairs={{0,8},{1,26},{2,11},{3,25},{4,12},{5,30},{6,15},{7,29},{8,0},{9,18... | collective-permute-start | bytes 393224 | tf_op jit(solution)/shard_map/ppermute | solution.py:39
  40.7 5.3 %copy-start.27 = (bf16[64,1024]{1,0:T(8,128)(2,1)}, bf16[64,1024]{1,0:T(8,128)(2,1)S(1)}, u32[]{:S(2)}) copy-start(bf16[64,1024]{1,0:T(8,128)(2,1)S(1)} %collective-permute-done.13.refs_2_) | copy-start | bytes 393220
  46.0 22.2 %collective-permute-start.15 = (bf16[256,1024]{1,0:T(8,128)(2,1)}, bf16[256,1024]{1,0:T(8,128)(2,1)}, u32[]{:S(2)}, u32[]{:S(2)}) collective-permute-start(bf16[256,1024]{1,0:T(8,128)(2,1)} %pad_maximum_fusion.2), channel_id=1, source_target_pairs={{0,1},{1,0},{2,3},{3,2},{4,5},{5,4},{6,7},{7,6},{8,9},{9,8},{10,11... | collective-permute-start | bytes 1572872 | tf_op jit(solution)/shard_map/ppermute | solution.py:39
  59.8 20.9 %all-to-all-start.4 = ((bf16[8,128,128]{2,1,0:T(8,128)(2,1)}), bf16[8,128,128]{2,1,0:T(8,128)(2,1)S(1)}, u32[]{:S(2)}, u32[]{:S(2)}) async-start(bf16[8,128,128]{2,1,0:T(8,128)(2,1)} %copy-done.32), calls=%async_computation.4 | async-start | bytes 524288 | tf_op jit(solution)/shard_map/all_to_all | solution.py:320
  75.1 30.4 %copy-start.36 = (s32[8]{0:T(128)S(1)}, s32[8]{0:T(128)}, u32[]{:S(2)}) copy-start(s32[8]{0:T(128)} %param.11) | copy-start | bytes 100
  102.0 20.8 %all-to-all-start.1 = ((bf16[8,256,128]{2,1,0:T(8,128)(2,1)}), bf16[8,256,128]{2,1,0:T(8,128)(2,1)S(1)}, u32[]{:S(2)}, u32[]{:S(2)}) async-start(bf16[8,256,128]{2,1,0:T(8,128)(2,1)} %copy-done.12), calls=%async_computation.1 | async-start | bytes 1048576 | tf_op jit(solution)/shard_map/all_to_all | solution.py:320
  122.8 18.1 %all-to-all-start = ((bf16[8,128,128]{2,1,0:T(8,128)(2,1)}), bf16[8,128,128]{2,1,0:T(8,128)(2,1)}, u32[]{:S(2)}, u32[]{:S(2)}) async-start(bf16[8,128,128]{2,1,0:T(8,128)(2,1)} %copy-done.31), calls=%async_computation | async-start | bytes 524288 | tf_op jit(solution)/shard_map/all_to_all | solution.py:320
  140.9 26.7 %all-to-all-start.5 = ((bf16[16,64,128]{2,1,0:T(8,128)(2,1)}), bf16[16,64,128]{2,1,0:T(8,128)(2,1)S(1)}, u32[]{:S(2)}, u32[]{:S(2)}) async-start(bf16[16,64,128]{2,1,0:T(8,128)(2,1)} %copy-done.7), calls=%async_computation.5 | async-start | bytes 524288 | tf_op jit(solution)/shard_map/all_to_all | solution.py:333
  153.5 33.8 %copy-start.34 = (f32[1024]{0:T(1024)S(1)}, f32[1024]{0:T(1024)}, u32[]{:S(2)}) copy-start(f32[1024]{0:T(1024)} %param.15) | copy-start | bytes 12292
  167.6 19.7 %all-to-all-start.3 = ((bf16[16,64,128]{2,1,0:T(8,128)(2,1)}), bf16[16,64,128]{2,1,0:T(8,128)(2,1)S(1)}, u32[]{:S(2)}, u32[]{:S(2)}) async-start(bf16[16,64,128]{2,1,0:T(8,128)(2,1)} %copy-done.6), calls=%async_computation.3 | async-start | bytes 524288 | tf_op jit(solution)/shard_map/all_to_all | solution.py:333
  195.1 7.8 %collective-permute-start.16 = (bf16[16,1024]{1,0:T(8,128)(2,1)S(1)}, bf16[16,1024]{1,0:T(8,128)(2,1)S(1)}, u32[]{:S(2)}, u32[]{:S(2)}) collective-permute-start(bf16[16,1024]{1,0:T(8,128)(2,1)S(1)} %get-tuple-element.19), channel_id=1, source_target_pairs={{0,16},{1,17},{2,18},{3,19},{4,20},{5,21},{6,22},{7,23},{8,24},{9,... | collective-permute-start | bytes 98312 | tf_op jit(solution)/shard_map/ppermute | solution.py:39
  197.5 6.9 %collective-permute-start.17 = (bf16[16,1024]{1,0:T(8,128)(2,1)S(1)}, bf16[16,1024]{1,0:T(8,128)(2,1)S(1)}, u32[]{:S(2)}, u32[]{:S(2)}) collective-permute-start(bf16[16,1024]{1,0:T(8,128)(2,1)S(1)} %get-tuple-element.20), channel_id=1, source_target_pairs={{1,240},{2,241},{3,242},{4,243},{5,244},{6,245},{7,246},{8,247},{9... | collective-permute-start | bytes 98312 | tf_op jit(solution)/shard_map/ppermute | solution.py:39
  204.5 6.6 %copy-start.35 = (f32[1024]{0:T(1024)S(1)}, f32[1024]{0:T(1024)}, u32[]{:S(2)}) copy-start(f32[1024]{0:T(1024)} %param.18) | copy-start | bytes 12292
  (28 other events, 35.9 us)
where the time goes:
time: 214 us; the launch traced here: 213 us
  starting transfers between devices  66.2 us (31%)
  waiting for transfers between devices  51.9 us (24%)
  Pallas kernels  36.6 us (17%)
  local copies, waits for them, and re-layouts  24.6 us (11%)
  blocking collectives  21.3 us (10%)
  other arithmetic  9.89 us (5%)
    ppermute x18, starting transfers between devices, send(): return lax.ppermute(value, ('blk', 'grp'), pairs)  29.7 us
    pallas_call x2, Pallas kernels, attend(): pl.pallas_call(attend_kernel, out_shape=jax.ShapeDtypeStruct((2 * sources...  26.4 us
    all_to_all x3, waiting for transfers between devices, along_z(): lax.all_to_all(packed, 'blk', 0, 0, axis_index_groups=groups, tiled=True)  22.7 us
    all_to_all x1, blocking collectives, along_z(): lax.all_to_all(packed, 'blk', 0, 0, axis_index_groups=groups, tiled=True)  21.3 us
    unnamed x74, local copies, waits for them, and re-layouts  20.7 us
    all_to_all x2, starting transfers between devices, body(): mixed.append(lax.all_to_all(part, 'blk', 0, 0, tiled=True))  20.5 us
    ppermute x18, waiting for transfers between devices, send(): return lax.ppermute(value, ('blk', 'grp'), pairs)  20.3 us
    all_to_all x3, starting transfers between devices, along_z(): lax.all_to_all(packed, 'blk', 0, 0, axis_index_groups=groups, tiled=True)  16 us
  transfers between devices with their start and end apart: 23, of which 10 were waited for; matrix products, arithmetic and copies ran while one was open for 3% of the time, Pallas kernels for 16%

commit v1 on v0

v1 whole, which is shorter than its diff:
```python
import jax
import jax.numpy as jnp
from jax import lax
from jax.experimental import pallas as pl
from jax.experimental.pallas import tpu as pltpu
from jax.sharding import PartitionSpec as P


HEAD = 64
LANES = 128
KEY_CHUNK = 512
RIM = 16
ROWS = 16
OFFSETS = (0, 1, 3, 2)
LOG2E = 1.4426950408889634

epsilon = 1e-05
big_negative = -1e30


VMEM = pl.BlockSpec(memory_space=pltpu.VMEM)
SMEM = pl.BlockSpec(memory_space=pltpu.SMEM)
HBM = pl.BlockSpec(memory_space=pltpu.HBM)


def coords(index):
    b, g = divmod(index, 16)
    return g // 4, (g // 2) % 2, g % 2, b // 2, b % 2


def flat(x, yh, core, z, yl):
    return ((z % 8) * 2 + yl) * 16 + (x % 4) * 4 + yh * 2 + core


def send(value, target):
    pairs = []
    for source in range(256):
        to = target(*coords(source))
        if to is not None:
            pairs.append((source, to if isinstance(to, int) else flat(*to)))
    return lax.ppermute(value, ("blk", "grp"), pairs)


def normalize(values, row_gain):
    center = values - jnp.mean(values, axis=-1, keepdims=True)
    spread = jnp.mean(center * center, axis=-1, keepdims=True)
    return center * lax.rsqrt(spread + epsilon) * row_gain


def low_lanes(rows):
    return lax.broadcasted_iota(jnp.int32, (rows, LANES), 1) < HEAD


def swap_lanes(values):
    return pltpu.roll(values, HEAD, 1)


def project_kernel(slot_ref, own_ref, other_ref, gain_ref, *refs):
    shards, out, weights, normed, sems = refs[:8], refs[8], refs[9], refs[10], refs[11]
    copies = []
    for i, shard in enumerate(shards):
        at = pl.ds(pl.multiple_of(slot_ref[i] * HEAD, HEAD), HEAD)
        for j in range(3):
            copies.append(
                pltpu.make_async_copy(
                    shard.at[pl.ds(j * HEAD, HEAD)], weights.at[(j + 2) % 3, at], sems.at[3 * i + j]
                )
            )
            copies[-1].start()
    rows = own_ref.shape[0]
    gain = gain_ref[0:1, :]
    normed[:rows] = normalize(own_ref[...].astype(jnp.float32), gain).astype(jnp.bfloat16)
    normed[rows:] = normalize(other_ref[...].astype(jnp.float32), gain).astype(jnp.bfloat16)
    for copy in copies:
        copy.wait()
    low = low_lanes(rows)
    for part in range(3):
        at = slice(part * rows, (part + 1) * rows)
        for pair in range(4):
            both = lax.dot_general(
                normed[...],
                weights[part, pair * LANES : (pair + 1) * LANES, :],
                (((1,), (1,)), ((), ())),
                preferred_element_type=jnp.float32,
            )
            if part == 2:
                both = both * (HEAD**-0.5 * LOG2E)
            own, other = both[:rows], both[rows:]
            out[2 * pair, at] = jnp.where(low, own, swap_lanes(other)).astype(jnp.bfloat16)
            out[2 * pair + 1, at] = jnp.where(low, swap_lanes(own), other).astype(jnp.bfloat16)


def project_qkv(slots, own, other, gain, shards):
    rows, width = own.shape
    return pl.pallas_call(
        project_kernel,
        out_shape=jax.ShapeDtypeStruct((8, 3 * rows, LANES), jnp.bfloat16),
        in_specs=[SMEM] + [VMEM] * 3 + [HBM] * 8,
        out_specs=VMEM,
        scratch_shapes=[
            pltpu.VMEM((3, 8 * HEAD, width), jnp.bfloat16),
            pltpu.VMEM((2 * rows, width), jnp.bfloat16),
            pltpu.SemaphoreType.DMA((24,)),
        ],
        compiler_params=pltpu.CompilerParams(vmem_limit_bytes=24 * 1024 * 1024),
    )(slots, own, other, gain, *shards)


def attend_kernel(base_ref, lo_ref, hi_ref, in_ref, out_ref, *scratch):
    keys, values, queries, scores_a, scores_b, max_a, max_b = scratch
    sources = in_ref.shape[0]
    block = in_ref.shape[1] // 3
    lo, hi = lo_ref[0:1, :], hi_ref[0:1, :]
    low = low_lanes(block)
    row = lax.broadcasted_iota(jnp.int32, (block, LANES), 0)

    def prepare(s, carry):
        key, value, query = (
            in_ref[s, i * block : (i + 1) * block].astype(jnp.float32) for i in range(3)
        )
        for side in range(2):
            position = row + (base_ref[side] + s * (2 * block))
            inside = (position >= lo) & (position < hi)
            at = pl.ds(pl.multiple_of((2 * s + side) * block, block), block)
            mask, mark = jnp.where(inside, 0.0, big_negative), jnp.where(inside, 1.0, 0.0)
            keys[at, :] = jnp.where(low, swap_lanes(key) if side else key, mask).astype(jnp.bfloat16)
            values[at, :] = jnp.where(low, 1.0, value if side else swap_lanes(value)).astype(jnp.bfloat16)
            queries[at, :] = jnp.where(low, swap_lanes(query) if side else query, mark).astype(jnp.bfloat16)
        return carry

    lax.fori_loop(0, sources, prepare, 0)
    window = keys.shape[0]
    chunks = window // KEY_CHUNK

    def score(query, j, scores, best):
        part = lax.dot_general(
            query,
            keys[j * KEY_CHUNK : (j + 1) * KEY_CHUNK, :],
            (((1,), (1,)), ((), ())),
            preferred_element_type=jnp.float32,
        )
        scores[:, j * KEY_CHUNK : (j + 1) * KEY_CHUNK] = part
        for t in range(KEY_CHUNK // LANES):
            piece = part[:, t * LANES : (t + 1) * LANES]
            best = piece if best is None else jnp.maximum(best, piece)
        return best

    def weigh(j, scores, row_max, total):
        probs = jnp.exp2(scores[:, j * KEY_CHUNK : (j + 1) * KEY_CHUNK] - row_max)
        part = jnp.dot(
            probs.astype(jnp.bfloat16),
            values[j * KEY_CHUNK : (j + 1) * KEY_CHUNK, :],
            preferred_element_type=jnp.float32,
        )
        return part if total is None else total + part

    half = block // 2

    def finish(total, source, side):
        mixed = total / swap_lanes(total)
        packed = jnp.where(low[:half], swap_lanes(mixed[:half]), mixed[half:])
        out_ref[2 * source + base_ref[2 + side]] = packed.astype(jnp.bfloat16)

    def both(i, new, old, source_old, side_old):
        query = queries[pl.ds(pl.multiple_of(i * block, block), block), :]
        row_max = old[1][:, 0:1]
        best, total = None, None
        for j in range(chunks):
            best = score(query, j, new[0], best)
            total = weigh(j, old[0], row_max, total)
        new[1][...] = jnp.broadcast_to(jnp.max(best, axis=1, keepdims=True), (block, LANES))
        finish(total, source_old, side_old)

    buffer_a, buffer_b = (scores_a, max_a), (scores_b, max_b)

    def step(i, carry):
        both(2 * i, buffer_a, buffer_b, jnp.maximum(i - 1, 0), 1)
        both(2 * i + 1, buffer_b, buffer_a, i, 0)
        return carry

    lax.fori_loop(0, sources, step, 0)
    total = None
    for j in range(chunks):
        total = weigh(j, scores_b, max_b[:, 0:1], total)
    finish(total, sources - 1, 1)


def attend(bases, lo, hi, parts):
    sources, block = parts.shape[0], parts.shape[1] // 3
    window = 2 * block * sources
    return pl.pallas_call(
        attend_kernel,
        out_shape=jax.ShapeDtypeStruct((2 * sources, block // 2, LANES), jnp.bfloat16),
        in_specs=[SMEM] + [VMEM] * 3,
        out_specs=VMEM,
        scratch_shapes=[pltpu.VMEM((window, LANES), jnp.bfloat16)] * 3
        + [pltpu.VMEM((block, window), jnp.float32)] * 2
        + [pltpu.VMEM((block, LANES), jnp.float32)] * 2,
        compiler_params=pltpu.CompilerParams(vmem_limit_bytes=24 * 1024 * 1024),
    )(bases, lo, hi, parts)


def gate_kernel(mixed, frames, gain, w_out_hbm, w_glu_hbm, residual_ref, gated_ref, *scratch):
    w_out, w_glu, attended, out_sem, glu_sem = scratch
    out_copy = pltpu.make_async_copy(w_out_hbm, w_out, out_sem)
    glu_copy = pltpu.make_async_copy(w_glu_hbm, w_glu, glu_sem)
    out_copy.start()
    glu_copy.start()
    heads, half, _ = mixed.shape
    low = low_lanes(half)
    for pair in range(heads // 2):
        even, odd = mixed[2 * pair].astype(jnp.float32), mixed[2 * pair + 1].astype(jnp.float32)
        at = slice(pair * LANES, (pair + 1) * LANES)
        attended[:half, at] = jnp.where(low, even, swap_lanes(odd)).astype(jnp.bfloat16)
        attended[half:, at] = jnp.where(low, swap_lanes(even), odd).astype(jnp.bfloat16)
    out_copy.wait()
    projected = jnp.dot(attended[...], w_out[...], preferred_element_type=jnp.float32)
    residual = (frames[...].astype(jnp.float32) + projected).astype(jnp.bfloat16)
    residual_ref[...] = residual
    width = frames.shape[1]
    conv_in = normalize(residual.astype(jnp.float32), gain[0:1, :]).astype(jnp.bfloat16)
    glu_copy.wait()
    step = 256
    for j in range(0, width, step):
        a = jnp.dot(conv_in, w_glu[:, j : j + step], preferred_element_type=jnp.float32)
        b = jnp.dot(conv_in, w_glu[:, width + j : width + j + step], preferred_element_type=jnp.float32)
        gated_ref[:, j : j + step] = (a * jax.nn.sigmoid(b)).astype(jnp.bfloat16)


def gate(mixed, frames, gain, w_out, w_glu):
    shape = jax.ShapeDtypeStruct(frames.shape, jnp.bfloat16)
    return pl.pallas_call(
        gate_kernel,
        out_shape=[shape, shape],
        in_specs=[VMEM] * 3 + [HBM] * 2,
        out_specs=[VMEM] * 2,
        scratch_shapes=[
            pltpu.VMEM(w_out.shape, jnp.bfloat16),
            pltpu.VMEM(w_glu.shape, jnp.bfloat16),
            pltpu.VMEM(frames.shape, jnp.bfloat16),
            pltpu.SemaphoreType.DMA,
            pltpu.SemaphoreType.DMA,
        ],
        compiler_params=pltpu.CompilerParams(vmem_limit_bytes=24 * 1024 * 1024),
    )(mixed, frames, gain, w_out, w_glu)


def convolve(source, row, weights, t_first, t_last, position, start_ref, end_ref, masked):
    place = lax.broadcasted_iota(jnp.int32, (ROWS, LANES), 0) + position
    lo, hi = jnp.zeros_like(place), jnp.zeros_like(place)
    if masked:
        for u in range(start_ref.shape[0]):
            inside = (place >= start_ref[u]) & (place < end_ref[u])
            lo, hi = jnp.where(inside, start_ref[u], lo), jnp.where(inside, end_ref[u], hi)
        lo, hi = lo - place, hi - place
    tiles = source.shape[0]
    totals = [None] * tiles
    for t in range(t_first, t_last):
        same = (lo <= t - RIM + 1) & (hi > t - RIM + 1) if masked else None
        for c in range(tiles):
            term = source[c, pl.ds(row + t + 1, ROWS), :] * weights[t : t + 1, c * LANES : (c + 1) * LANES]
            term = jnp.where(same, term, 0.0) if masked else term
            totals[c] = term if totals[c] is None else totals[c] + term
    return totals


def inner_kernel(first_ref, start_ref, end_ref, gated, weights, out, padded):
    rows, width = gated.shape
    for c in range(width // LANES):
        padded[c, :RIM] = jnp.zeros((RIM, LANES), jnp.float32)
        padded[c, RIM : RIM + rows] = gated[:, c * LANES : (c + 1) * LANES].astype(jnp.float32)
        padded[c, RIM + rows :] = jnp.zeros((RIM, LANES), jnp.float32)

    def step(i, carry):
        row = pl.multiple_of(i * ROWS, ROWS)
        position = first_ref[0] + row
        crossed = False
        for u in range(1, start_ref.shape[0]):
            crossed |= (start_ref[u] > position - RIM) & (start_ref[u] < position + ROWS + RIM)

        def run(masked):
            totals = convolve(
                padded, row, weights, 0, weights.shape[0], position, start_ref, end_ref, masked
            )
            for c, total in enumerate(totals):
                out[pl.ds(row, ROWS), c * LANES : (c + 1) * LANES] = total

        pl.when(crossed)(lambda: run(True))
        pl.when(jnp.logical_not(crossed))(lambda: run(False))
        return carry

    lax.fori_loop(0, rows // ROWS, step, 0)


def convolve_inner(first, starts, ends, gated, weights):
    rows, width = gated.shape
    return pl.pallas_call(
        inner_kernel,
        out_shape=jax.ShapeDtypeStruct(gated.shape, jnp.float32),
        in_specs=[SMEM] * 3 + [VMEM] * 2,
        out_specs=VMEM,
        scratch_shapes=[pltpu.VMEM((width // LANES, rows + 2 * RIM, LANES), jnp.float32)],
        compiler_params=pltpu.CompilerParams(vmem_limit_bytes=16 * 1024 * 1024),
    )(first, starts, ends, gated, weights)


def last_kernel(
    first_ref, start_ref, end_ref, inner, left, right, residual, weights, gain, w_proj_hbm, out, *scratch
):
    w_proj, total, edge, sem = scratch
    copy = pltpu.make_async_copy(w_proj_hbm, w_proj, sem)
    copy.start()
    rows, width = inner.shape
    total[...] = inner[...]
    count = weights.shape[0]
    for side, rim in enumerate((left, right)):
        at = 0 if side == 0 else 2 * RIM
        row = 0 if side == 0 else rows - ROWS
        for c in range(width // LANES):
            edge[c] = jnp.zeros(edge.shape[1:], jnp.float32)
            edge[c, at : at + RIM] = rim[:, c * LANES : (c + 1) * LANES].astype(jnp.float32)
        span = (0, RIM - 1) if side == 0 else (RIM, count)
        parts = convolve(
            edge, 0, weights, *span, first_ref[0] + row, start_ref, end_ref, True
        )
        for c, part in enumerate(parts):
            lanes = slice(c * LANES, (c + 1) * LANES)
            total[row : row + ROWS, lanes] = total[row : row + ROWS, lanes] + part
    normed = normalize(total[...], gain[0:1, :])
    activated = (normed * jax.nn.sigmoid(normed)).astype(jnp.bfloat16)
    copy.wait()
    projected = jnp.dot(activated, w_proj[...], preferred_element_type=jnp.float32)
    out[...] = (residual[...].astype(jnp.float32) + projected).astype(jnp.bfloat16)


def finish_block(first, starts, ends, inner, left, right, residual, weights, gain, w_proj):
    _, width = inner.shape
    return pl.pallas_call(
        last_kernel,
        out_shape=jax.ShapeDtypeStruct(residual.shape, jnp.bfloat16),
        in_specs=[SMEM] * 3 + [VMEM] * 6 + [HBM],
        out_specs=VMEM,
        scratch_shapes=[
            pltpu.VMEM(w_proj.shape, jnp.bfloat16),
            pltpu.VMEM(inner.shape, jnp.float32),
            pltpu.VMEM((width // LANES, 3 * RIM, LANES), jnp.float32),
            pltpu.SemaphoreType.DMA,
        ],
        compiler_params=pltpu.CompilerParams(vmem_limit_bytes=24 * 1024 * 1024),
    )(first, starts, ends, inner, left, right, residual, weights, gain, w_proj)


def body(
    frames, utt_lengths, attn_gain, w_qkv, w_out, conv_gain, w_glu, w_depth, depth_gain, w_proj
):
    frame_rows = frames.shape[1]
    block_index = lax.axis_index("blk")
    group_index = lax.axis_index("grp")
    yl = block_index % 2
    x, core = group_index // 4, group_index % 2
    window_start = group_index * (16 * frame_rows)
    first_frame = window_start + block_index * frame_rows
    local_frames = frames[0]

    other_frames = send(local_frames, lambda x, yh, c, z, yl: (x, yh, c, z, 1 - yl))
    shard = w_qkv.T

    def route(offset):
        return lambda x, yh, c, z, yl: (
            (x - offset, yh, yh, z, c) if yl == c else (x - offset, 1 - yh, yh, z, c)
        )

    near = [send(shard, route(offset)) for offset in OFFSETS]
    swap = lambda x, yh, c, z, yl: (x, yh, 1 - c, z, yl)
    far = [send(piece, swap) for piece in near]
    slots = jnp.stack([2 * ((x + offset) % 4) + c for c in (core, 1 - core) for offset in OFFSETS])
    parts = project_qkv(slots, local_frames, other_frames, attn_gain[None, :], near + far)
    groups = [[2 * z + yl for z in range(8)] for yl in range(2)]
    parts = lax.all_to_all(parts, "blk", 0, 0, axis_index_groups=groups, tiled=True)
    ends = jnp.cumsum(utt_lengths)
    starts = ends - utt_lengths
    pad = (HEAD, HEAD - utt_lengths.shape[0])
    sides = jnp.stack([yl, 1 - yl])
    bases = jnp.concatenate([window_start + sides * frame_rows, sides])
    mixed = attend(bases, jnp.pad(starts, pad)[None, :], jnp.pad(ends, pad)[None, :], parts)
    mixed = lax.all_to_all(mixed, "blk", 0, 0, tiled=True)
    residual, gated = gate(mixed, local_frames, conv_gain[None, :], w_out, w_glu)

    def neighbour(step):
        def target(x, yh, c, z, yl):
            place = (x * 4 + yh * 2 + c) * 16 + z * 2 + yl + step
            return (place % 16) * 16 + place // 16 if 0 <= place < 256 else None

        return target

    left = send(gated[frame_rows - RIM :], neighbour(1))
    right = send(gated[:RIM], neighbour(-1))
    where = (first_frame[None], starts, ends)
    inner = convolve_inner(*where, gated, w_depth)
    result = finish_block(*where, inner, left, right, residual, w_depth, depth_gain[None, :], w_proj)
    return result[None]


def solution(mesh):
    in_specs = (P("grp", "blk", None), P(), P(), P(None, "grp"), P(), P(), P(), P(), P(), P())
    out_specs = P("grp", "blk", None)
    return jax.shard_map(body, mesh=mesh, in_specs=in_specs, out_specs=out_specs, check_vma=False)
```

time: 214 us -> 154 us (0.72)
  the two profiles are of different devices: /device:TPU:16 before, /device:TPU:1 now
where the time goes in v1:
time: 154 us; the launch traced here: 153 us
  waiting for transfers between devices  59.2 us (38%)
  Pallas kernels  42.9 us (28%)
  starting transfers between devices  26.5 us (17%)
  blocking collectives  18.5 us (12%)
  local copies, waits for them, and re-layouts  4.9 us (3%)
    all_to_all x1, waiting for transfers between devices, body(): lax.all_to_all(parts, 'blk', 0, 0, axis_index_groups=groups, tiled=True)  40 us
    pallas_call x1, Pallas kernels, attend(): pl.pallas_call(attend_kernel, out_shape=jax.ShapeDtypeStruct((2 * sources...  23.4 us
    ppermute x11, waiting for transfers between devices, send(): return lax.ppermute(value, ('blk', 'grp'), pairs)  19.2 us
    all_to_all x1, blocking collectives, body(): mixed = lax.all_to_all(mixed, 'blk', 0, 0, tiled=True)  18.5 us
    ppermute x11, starting transfers between devices, send(): return lax.ppermute(value, ('blk', 'grp'), pairs)  18.3 us
    pallas_call x1, Pallas kernels, project_qkv(): pl.pallas_call(project_kernel, out_shape=jax.ShapeDtypeStruct((8, 3 * row...  10.1 us
    all_to_all x1, starting transfers between devices, body(): lax.all_to_all(parts, 'blk', 0, 0, axis_index_groups=groups, tiled=True)  8.2 us
    unnamed x24, local copies, waits for them, and re-layouts  4.73 us
  transfers between devices with their start and end apart: 12, of which 7 were waited for; matrix products, arithmetic and copies ran while one was open for 0% of the time, Pallas kernels for 2%

profile of v1, /device:TPU:1, one launch (start us, length us, event | category | flops | bytes accessed | tf_op | source)
XLA Modules:
  0.0 152.7 jit_solution(11986130576671026299)
XLA Ops:
  0.0 6.0 %collective-permute-start.1 = (bf16[192,1024]{1,0:T(8,128)(2,1)}, bf16[192,1024]{1,0:T(8,128)(2,1)S(1)}, u32[]{:S(2)}, u32[]{:S(2)}) collective-permute-start(bf16[192,1024]{1,0:T(8,128)(2,1)} %bitcast.33), channel_id=1, source_target_pairs={{0,0},{1,18},{2,3},{3,17},{4,4},{5,22},{6,7},{7,21},{8,8},{9,26},{... | collective-permute-start | bytes 1179656 | tf_op jit(solution)/shard_map/ppermute | solution.py:41
  6.0 2.3 %collective-permute-start.2 = (bf16[192,1024]{1,0:T(8,128)(2,1)}, bf16[192,1024]{1,0:T(8,128)(2,1)S(1)}, u32[]{:S(2)}, u32[]{:S(2)}) collective-permute-start(bf16[192,1024]{1,0:T(8,128)(2,1)} %bitcast.34), channel_id=1, source_target_pairs={{0,12},{1,30},{2,15},{3,29},{4,0},{5,18},{6,3},{7,17},{8,4},{9,22}... | collective-permute-start | bytes 1179656 | tf_op jit(solution)/shard_map/ppermute | solution.py:41
  8.3 1.6 %collective-permute-start.3 = (bf16[192,1024]{1,0:T(8,128)(2,1)}, bf16[192,1024]{1,0:T(8,128)(2,1)S(1)}, u32[]{:S(2)}, u32[]{:S(2)}) collective-permute-start(bf16[192,1024]{1,0:T(8,128)(2,1)} %bitcast.35), channel_id=1, source_target_pairs={{0,4},{1,22},{2,7},{3,21},{4,8},{5,26},{6,11},{7,25},{8,12},{9,30}... | collective-permute-start | bytes 1179656 | tf_op jit(solution)/shard_map/ppermute | solution.py:41
  10.0 2.5 %collective-permute-start.4 = (bf16[192,1024]{1,0:T(8,128)(2,1)}, bf16[192,1024]{1,0:T(8,128)(2,1)S(1)}, u32[]{:S(2)}, u32[]{:S(2)}) collective-permute-start(bf16[192,1024]{1,0:T(8,128)(2,1)} %bitcast.36), channel_id=1, source_target_pairs={{0,8},{1,26},{2,11},{3,25},{4,12},{5,30},{6,15},{7,29},{8,0},{9,18... | collective-permute-start | bytes 1179656 | tf_op jit(solution)/shard_map/ppermute | solution.py:41
  12.4 1.6 %collective-permute-done.1.refs_0_ = bf16[192,1024]{1,0:T(8,128)(2,1)S(1)} collective-permute-done((bf16[192,1024]{1,0:T(8,128)(2,1)}, bf16[192,1024]{1,0:T(8,128)(2,1)S(1)}, u32[]{:S(2)}, u32[]{:S(2)}) %collective-permute-start.1) | collective-permute-done | bytes 393248 | tf_op jit(solution)/shard_map/ppermute | solution.py:41
  14.1 6.1 %collective-permute-done.2.refs_1_ = bf16[192,1024]{1,0:T(8,128)(2,1)S(1)} collective-permute-done((bf16[192,1024]{1,0:T(8,128)(2,1)}, bf16[192,1024]{1,0:T(8,128)(2,1)S(1)}, u32[]{:S(2)}, u32[]{:S(2)}) %collective-permute-start.2) | collective-permute-done | bytes 393248 | tf_op jit(solution)/shard_map/ppermute | solution.py:41
  20.1 8.0 %collective-permute-done.3.refs_2_ = bf16[192,1024]{1,0:T(8,128)(2,1)S(1)} collective-permute-done((bf16[192,1024]{1,0:T(8,128)(2,1)}, bf16[192,1024]{1,0:T(8,128)(2,1)S(1)}, u32[]{:S(2)}, u32[]{:S(2)}) %collective-permute-start.3) | collective-permute-done | bytes 393248 | tf_op jit(solution)/shard_map/ppermute | solution.py:41
  28.1 0.5 collective-permute-start.8
  28.6 0.1 stack.47.slot_ref
  28.7 1.1 collective-permute-done.7.refs_6_
  29.8 0.7 collective-permute-done.8.refs_7_
  30.5 1.0 copy-done.3
  31.5 0.7 copy-done.9
  32.2 10.1 %shard_map.100 = bf16[8,768,128]{2,1,0:T(8,128)(2,1)} custom-call(s32[8]{0:T(128)S(1)} %stack.47.slot_ref, bf16[256,1024]{1,0:T(8,128)(2,1)S(1)} %bitcast.25, bf16[256,1024]{1,0:T(8,128)(2,1)S(1)} %collective-permute-done.other_ref, f32[1,1024]{1,0:T(1,128)S(1)} %bitcast.31, bf16[192,1024]{1,0:T(8,128)(2,1)S(1)} %collective-permute-done.1.refs_0_, ...), custom_call_target="tpu_custom_call" | custom-call | tf_op jit(solution)/shard_map/pallas_call | solution.py:95
  42.3 8.2 %all-to-all-start = ((bf16[8,768,128]{2,1,0:T(8,128)(2,1)}), bf16[8,768,128]{2,1,0:T(8,128)(2,1)S(1)}, u32[]{:S(2)}, u32[]{:S(2)}) async-start(bf16[8,768,128]{2,1,0:T(8,128)(2,1)} %shard_map.100), calls=%async_computation | async-start | bytes 3145728 | tf_op jit(solution)/shard_map/all_to_all | solution.py:379
  50.6 0.2 reduce-window.9
  50.7 0.1 fusion
  50.8 0.1 pad_add_fusion.base_ref
  50.9 0.1 pad_bitcast_fusion
  51.0 40.0 %all-to-all-done.in_ref = bf16[8,768,128]{2,1,0:T(8,128)(2,1)S(1)} async-done(((bf16[8,768,128]{2,1,0:T(8,128)(2,1)}), bf16[8,768,128]{2,1,0:T(8,128)(2,1)S(1)}, u32[]{:S(2)}, u32[]{:S(2)}) %all-to-all-start) | async-done | bytes 1572896 | tf_op jit(solution)/shard_map/all_to_all | solution.py:379
  91.0 23.4 %shard_map.101 = bf16[16,128,128]{2,1,0:T(8,128)(2,1)S(1)} custom-call(s32[4]{0:T(128)S(1)} %pad_add_fusion.base_ref, s32[1,128]{1,0:T(1,128)S(1)} %get-tuple-element.12.lo_ref, s32[1,128]{1,0:T(1,128)S(1)} %get-tuple-element.11.hi_ref, bf16[8,768,128]{2,1,0:T(8,128)(2,1)S(1)} %all-to-all-done.in_ref), custom_call_target="tpu_custom_call" | custom-call | tf_op jit(solution)/shard_map/pallas_call | solution.py:191
  114.4 18.5 %all_to_all.10.mixed = bf16[16,128,128]{2,1,0:T(8,128)(2,1)S(1)} all-to-all(bf16[16,128,128]{2,1,0:T(8,128)(2,1)S(1)} %shard_map.101), channel_id=1, replica_groups=mesh['blk'=16,'grp'=16] {'blk'}, dimensions={0} | all-to-all | bytes 1048576 | tf_op jit(solution)/shard_map/all_to_all | solution.py:386
  132.9 0.0 copy-start
  132.9 2.2 %copy-done = bf16[1024,2048]{1,0:T(8,128)(2,1)S(1)} copy-done((bf16[1024,2048]{1,0:T(8,128)(2,1)S(1)}, bf16[1024,2048]{1,0:T(8,128)(2,1)}, u32[]{:S(2)}) %copy-start) | copy-done | bytes 4194328
  135.1 3.0 %shard_map.102 = (bf16[256,1024]{1,0:T(8,128)(2,1)S(1)}, bf16[256,1024]{1,0:T(8,128)(2,1)S(1)}) custom-call(bf16[16,128,128]{2,1,0:T(8,128)(2,1)S(1)} %all_to_all.10.mixed, bf16[256,1024]{1,0:T(8,128)(2,1)S(1)} %bitcast.26, f32[1,1024]{1,0:T(1,128)S(1)} %bitcast.30, bf16[1024,1024]{1,0:T(8,128)(2,1)S(1)} %copy-done.1, bf16[1024,2048]{1,0:T(8,128)(2,1)S(1)} %copy-done), custom_call_target="tpu_custom_call" | custom-call | tf_op jit(solution)/shard_map/pallas_call | solution.py:232
  138.1 0.0 copy-start.5
  138.1 0.8 copy-done.5
  138.9 3.5 %collective-permute-start.10 = (bf16[16,1024]{1,0:T(8,128)(2,1)S(1)}, bf16[16,1024]{1,0:T(8,128)(2,1)S(1)}, u32[]{:S(2)}, u32[]{:S(2)}) collective-permute-start(bf16[16,1024]{1,0:T(8,128)(2,1)S(1)} %get-tuple-element.9), channel_id=1, source_target_pairs={{1,240},{2,241},{3,242},{4,243},{5,244},{6,245},{7,246},{8,247},{9... | collective-permute-start | bytes 98312 | tf_op jit(solution)/shard_map/ppermute | solution.py:41
  142.3 1.9 %collective-permute-start.9 = (bf16[16,1024]{1,0:T(8,128)(2,1)S(1)}, bf16[16,1024]{1,0:T(8,128)(2,1)S(1)}, u32[]{:S(2)}, u32[]{:S(2)}) collective-permute-start(bf16[16,1024]{1,0:T(8,128)(2,1)S(1)} %get-tuple-element.10), channel_id=1, source_target_pairs={{0,16},{1,17},{2,18},{3,19},{4,20},{5,21},{6,22},{7,23},{8,24},{9,... | collective-permute-start | bytes 98312 | tf_op jit(solution)/shard_map/ppermute | solution.py:41
  144.3 3.6 %shard_map.103.inner = f32[256,1024]{1,0:T(8,128)S(1)} custom-call(s32[1]{0:T(128)} %bitcast.first_ref, s32[8]{0:T(128)S(1)} %bitcast_subtract_fusion.start_ref, s32[8]{0:T(128)S(1)} %bitcast.28, bf16[256,1024]{1,0:T(8,128)(2,1)S(1)} %get-tuple-element.7.gated, f32[31,1024]{1,0:T(8,128)S(1)} %copy-done.7), custom_call_target="tpu_custom_call" | custom-call | tf_op jit(solution)/shard_map/pallas_call | solution.py:297
  147.9 1.8 %collective-permute-done.9.left = bf16[16,1024]{1,0:T(8,128)(2,1)S(1)} collective-permute-done((bf16[16,1024]{1,0:T(8,128)(2,1)S(1)}, bf16[16,1024]{1,0:T(8,128)(2,1)S(1)}, u32[]{:S(2)}, u32[]{:S(2)}) %collective-permute-start.9) | collective-permute-done | bytes 32800 | tf_op jit(solution)/shard_map/ppermute | solution.py:41
  149.7 2.9 %shard_map.104 = bf16[256,1024]{1,0:T(8,128)(2,1)} custom-call(s32[1]{0:T(128)} %bitcast.first_ref, s32[8]{0:T(128)S(1)} %bitcast_subtract_fusion.start_ref, s32[8]{0:T(128)S(1)} %bitcast.29, f32[256,1024]{1,0:T(8,128)S(1)} %shard_map.103.inner, bf16[16,1024]{1,0:T(8,128)(2,1)S(1)} %collective-permute-done.9.left, ...), custom_call_target="tpu_custom_call" | custom-call | tf_op jit(solution)/shard_map/pallas_call | solution.py:338
  (29 shorter events, 0.1 us)
Async XLA Ops:
  0.0 14.1 %collective-permute-start.1 = (bf16[192,1024]{1,0:T(8,128)(2,1)}, bf16[192,1024]{1,0:T(8,128)(2,1)S(1)}, u32[]{:S(2)}, u32[]{:S(2)}) collective-permute-start(bf16[192,1024]{1,0:T(8,128)(2,1)} %bitcast.33), channel_id=1, source_target_pairs={{0,0},{1,18},{2,3},{3,17},{4,4},{5,22},{6,7},{7,21},{8,8},{9,26},{... | collective-permute-start | bytes 1179656 | tf_op jit(solution)/shard_map/ppermute | solution.py:41
  6.0 14.1 %collective-permute-start.2 = (bf16[192,1024]{1,0:T(8,128)(2,1)}, bf16[192,1024]{1,0:T(8,128)(2,1)S(1)}, u32[]{:S(2)}, u32[]{:S(2)}) collective-permute-start(bf16[192,1024]{1,0:T(8,128)(2,1)} %bitcast.34), channel_id=1, source_target_pairs={{0,12},{1,30},{2,15},{3,29},{4,0},{5,18},{6,3},{7,17},{8,4},{9,22}... | collective-permute-start | bytes 1179656 | tf_op jit(solution)/shard_map/ppermute | solution.py:41
  8.3 19.8 %collective-permute-start.3 = (bf16[192,1024]{1,0:T(8,128)(2,1)}, bf16[192,1024]{1,0:T(8,128)(2,1)S(1)}, u32[]{:S(2)}, u32[]{:S(2)}) collective-permute-start(bf16[192,1024]{1,0:T(8,128)(2,1)} %bitcast.35), channel_id=1, source_target_pairs={{0,4},{1,22},{2,7},{3,21},{4,8},{5,26},{6,11},{7,25},{8,12},{9,30}... | collective-permute-start | bytes 1179656 | tf_op jit(solution)/shard_map/ppermute | solution.py:41
  10.0 18.1 %collective-permute-start.4 = (bf16[192,1024]{1,0:T(8,128)(2,1)}, bf16[192,1024]{1,0:T(8,128)(2,1)S(1)}, u32[]{:S(2)}, u32[]{:S(2)}) collective-permute-start(bf16[192,1024]{1,0:T(8,128)(2,1)} %bitcast.36), channel_id=1, source_target_pairs={{0,8},{1,26},{2,11},{3,25},{4,12},{5,30},{6,15},{7,29},{8,0},{9,18... | collective-permute-start | bytes 1179656 | tf_op jit(solution)/shard_map/ppermute | solution.py:41
  12.4 16.3 %collective-permute-start = (bf16[256,1024]{1,0:T(8,128)(2,1)}, bf16[256,1024]{1,0:T(8,128)(2,1)S(1)}, u32[]{:S(2)}, u32[]{:S(2)}) collective-permute-start(bf16[256,1024]{1,0:T(8,128)(2,1)} %bitcast.24), channel_id=1, source_target_pairs={{0,16},{1,17},{2,18},{3,19},{4,20},{5,21},{6,22},{7,23},{8,24},{9,... | collective-permute-start | bytes 1572872 | tf_op jit(solution)/shard_map/ppermute | solution.py:41
  14.1 14.6 %collective-permute-start.5 = (bf16[192,1024]{1,0:T(8,128)(2,1)S(1)}, bf16[192,1024]{1,0:T(8,128)(2,1)S(1)}, u32[]{:S(2)}, u32[]{:S(2)}) collective-permute-start(bf16[192,1024]{1,0:T(8,128)(2,1)S(1)} %collective-permute-done.1.refs_0_), channel_id=1, source_target_pairs={{0,1},{1,0},{2,3},{3,2},{4,5},{5,4},{6,7},{7,6},{8,9},{9,8},{10,11... | collective-permute-start | bytes 1179656 | tf_op jit(solution)/shard_map/ppermute | solution.py:41
  20.1 8.6 %collective-permute-start.6 = (bf16[192,1024]{1,0:T(8,128)(2,1)S(1)}, bf16[192,1024]{1,0:T(8,128)(2,1)S(1)}, u32[]{:S(2)}, u32[]{:S(2)}) collective-permute-start(bf16[192,1024]{1,0:T(8,128)(2,1)S(1)} %collective-permute-done.2.refs_1_), channel_id=1, source_target_pairs={{0,1},{1,0},{2,3},{3,2},{4,5},{5,4},{6,7},{7,6},{8,9},{9,8},{10,11... | collective-permute-start | bytes 1179656 | tf_op jit(solution)/shard_map/ppermute | solution.py:41
  28.1 1.7 %collective-permute-start.7 = (bf16[192,1024]{1,0:T(8,128)(2,1)S(1)}, bf16[192,1024]{1,0:T(8,128)(2,1)S(1)}, u32[]{:S(2)}, u32[]{:S(2)}) collective-permute-start(bf16[192,1024]{1,0:T(8,128)(2,1)S(1)} %collective-permute-done.3.refs_2_), channel_id=1, source_target_pairs={{0,1},{1,0},{2,3},{3,2},{4,5},{5,4},{6,7},{7,6},{8,9},{9,8},{10,11... | collective-permute-start | bytes 1179656 | tf_op jit(solution)/shard_map/ppermute | solution.py:41
  28.1 2.4 %collective-permute-start.8 = (bf16[192,1024]{1,0:T(8,128)(2,1)S(1)}, bf16[192,1024]{1,0:T(8,128)(2,1)}, u32[]{:S(2)}, u32[]{:S(2)}) collective-permute-start(bf16[192,1024]{1,0:T(8,128)(2,1)S(1)} %collective-permute-done.4.refs_3_), channel_id=1, source_target_pairs={{0,1},{1,0},{2,3},{3,2},{4,5},{5,4},{6,7},{7,6},{8,9},{9,8},{10,11... | collective-permute-start | bytes 1179656 | tf_op jit(solution)/shard_map/ppermute | solution.py:41
  30.5 1.0 copy-start.3
  31.5 0.7 copy-start.9
  42.3 8.2 %copy-start.11 = (s32[8]{0:T(128)S(1)}, s32[8]{0:T(128)}, u32[]{:S(2)}) copy-start(s32[8]{0:T(128)} %param.11) | copy-start | bytes 100
  42.3 48.6 %all-to-all-start = ((bf16[8,768,128]{2,1,0:T(8,128)(2,1)}), bf16[8,768,128]{2,1,0:T(8,128)(2,1)S(1)}, u32[]{:S(2)}, u32[]{:S(2)}) async-start(bf16[8,768,128]{2,1,0:T(8,128)(2,1)} %shard_map.100), calls=%async_computation | async-start | bytes 3145728 | tf_op jit(solution)/shard_map/all_to_all | solution.py:379
  50.5 82.4 %copy-start.4 = (bf16[1,256,1024]{2,1,0:T(8,128)(2,1)S(1)}, bf16[1,256,1024]{2,1,0:T(8,128)(2,1)}, u32[]{:S(2)}) copy-start(bf16[1,256,1024]{2,1,0:T(8,128)(2,1)} %param.10) | copy-start | bytes 1572868
  50.5 82.4 %copy-start.8 = (f32[1024]{0:T(1024)S(1)}, f32[1024]{0:T(1024)}, u32[]{:S(2)}) copy-start(f32[1024]{0:T(1024)} %param.15) | copy-start | bytes 12292
  91.0 41.9 %copy-start.1 = (bf16[1024,1024]{1,0:T(8,128)(2,1)S(1)}, bf16[1024,1024]{1,0:T(8,128)(2,1)}, u32[]{:S(2)}) copy-start(bf16[1024,1024]{1,0:T(8,128)(2,1)} %w_out_hbm.1) | copy-start | bytes 6291460
  132.9 2.2 %copy-start = (bf16[1024,2048]{1,0:T(8,128)(2,1)S(1)}, bf16[1024,2048]{1,0:T(8,128)(2,1)}, u32[]{:S(2)}) copy-start(bf16[1024,2048]{1,0:T(8,128)(2,1)} %w_glu_hbm.1) | copy-start | bytes 12582916
  135.1 9.2 %copy-start.7 = (f32[31,1024]{1,0:T(8,128)S(1)}, f32[31,1024]{1,0:T(8,128)}, u32[]{:S(2)}) copy-start(f32[31,1024]{1,0:T(8,128)} %weights.3) | copy-start | bytes 380932
  135.1 14.6 %copy-start.2 = (bf16[1024,1024]{1,0:T(8,128)(2,1)S(1)}, bf16[1024,1024]{1,0:T(8,128)(2,1)}, u32[]{:S(2)}) copy-start(bf16[1024,1024]{1,0:T(8,128)(2,1)} %w_proj_hbm.1) | copy-start | bytes 6291460
  135.1 14.6 %copy-start.10 = (f32[1024]{0:T(1024)S(1)}, f32[1024]{0:T(1024)}, u32[]{:S(2)}) copy-start(f32[1024]{0:T(1024)} %param.18) | copy-start | bytes 12292
  138.1 0.8 copy-start.5
  138.8 10.9 %copy-start.6 = (bf16[256,1024]{1,0:T(8,128)(2,1)S(1)}, bf16[256,1024]{1,0:T(8,128)(2,1)}, u32[]{:S(2)}) copy-start(bf16[256,1024]{1,0:T(8,128)(2,1)} %copy-done.5) | copy-start | bytes 1572868
  138.9 9.1 %collective-permute-start.10 = (bf16[16,1024]{1,0:T(8,128)(2,1)S(1)}, bf16[16,1024]{1,0:T(8,128)(2,1)S(1)}, u32[]{:S(2)}, u32[]{:S(2)}) collective-permute-start(bf16[16,1024]{1,0:T(8,128)(2,1)S(1)} %get-tuple-element.9), channel_id=1, source_target_pairs={{1,240},{2,241},{3,242},{4,243},{5,244},{6,245},{7,246},{8,247},{9... | collective-permute-start | bytes 98312 | tf_op jit(solution)/shard_map/ppermute | solution.py:41
  142.3 7.3 %collective-permute-start.9 = (bf16[16,1024]{1,0:T(8,128)(2,1)S(1)}, bf16[16,1024]{1,0:T(8,128)(2,1)S(1)}, u32[]{:S(2)}, u32[]{:S(2)}) collective-permute-start(bf16[16,1024]{1,0:T(8,128)(2,1)S(1)} %get-tuple-element.10), channel_id=1, source_target_pairs={{0,16},{1,17},{2,18},{3,19},{4,20},{5,21},{6,22},{7,23},{8,24},{9,... | collective-permute-start | bytes 98312 | tf_op jit(solution)/shard_map/ppermute | solution.py:41

commit v2 on v1

--- a/solution.py
+++ b/solution.py
@@ -56,38 +56,32 @@
 
 
 def project_kernel(slot_ref, own_ref, other_ref, gain_ref, *refs):
-    shards, out, weights, normed, sems = refs[:8], refs[8], refs[9], refs[10], refs[11]
-    copies = []
-    for i, shard in enumerate(shards):
-        at = pl.ds(pl.multiple_of(slot_ref[i] * HEAD, HEAD), HEAD)
-        for j in range(3):
-            copies.append(
-                pltpu.make_async_copy(
-                    shard.at[pl.ds(j * HEAD, HEAD)], weights.at[(j + 2) % 3, at], sems.at[3 * i + j]
-                )
-            )
-            copies[-1].start()
+    shards, out, normed = refs[:8], refs[8], refs[9]
     rows = own_ref.shape[0]
     gain = gain_ref[0:1, :]
     normed[:rows] = normalize(own_ref[...].astype(jnp.float32), gain).astype(jnp.bfloat16)
     normed[rows:] = normalize(other_ref[...].astype(jnp.float32), gain).astype(jnp.bfloat16)
-    for copy in copies:
-        copy.wait()
     low = low_lanes(rows)
-    for part in range(3):
-        at = slice(part * rows, (part + 1) * rows)
-        for pair in range(4):
-            both = lax.dot_general(
-                normed[...],
-                weights[part, pair * LANES : (pair + 1) * LANES, :],
-                (((1,), (1,)), ((), ())),
-                preferred_element_type=jnp.float32,
+    contract = (((1,), (1,)), ((), ()))
+    for pair in range(4):
+        weights = jnp.concatenate(
+            [shards[i][HEAD : 2 * HEAD, :] for i in (2 * pair, 2 * pair + 1)], axis=0
+        )
+        both = lax.dot_general(normed[...], weights, contract, preferred_element_type=jnp.float32)
+        own, other = both[:rows], both[rows:]
+        out[slot_ref[2 * pair], :rows] = jnp.where(low, own, swap_lanes(other)).astype(jnp.bfloat16)
+        out[slot_ref[2 * pair + 1], :rows] = jnp.where(low, swap_lanes(own), other).astype(jnp.bfloat16)
+        for i in (2 * pair, 2 * pair + 1):
+            weights = jnp.concatenate([shards[i][2 * HEAD :, :], shards[i][:HEAD, :]], axis=0)
+            flipped = lax.dot_general(
+                weights, normed[...], contract, preferred_element_type=jnp.float32
             )
-            if part == 2:
-                both = both * (HEAD**-0.5 * LOG2E)
-            own, other = both[:rows], both[rows:]
-            out[2 * pair, at] = jnp.where(low, own, swap_lanes(other)).astype(jnp.bfloat16)
-            out[2 * pair + 1, at] = jnp.where(low, swap_lanes(own), other).astype(jnp.bfloat16)
+            value = flipped[:HEAD].astype(jnp.bfloat16)
+            query = (flipped[HEAD:] * (HEAD**-0.5 * LOG2E)).astype(jnp.bfloat16)
+            for part, flat_part in enumerate((value, query)):
+                for j in range(2 * rows // LANES):
+                    at = (part + 1) * rows + j * HEAD
+                    out[slot_ref[i], at : at + HEAD] = flat_part[:, j * LANES : (j + 1) * LANES]
 
 
 def project_qkv(slots, own, other, gain, shards):
@@ -95,109 +89,105 @@
     return pl.pallas_call(
         project_kernel,
         out_shape=jax.ShapeDtypeStruct((8, 3 * rows, LANES), jnp.bfloat16),
-        in_specs=[SMEM] + [VMEM] * 3 + [HBM] * 8,
+        in_specs=[SMEM] + [VMEM] * 11,
         out_specs=VMEM,
-        scratch_shapes=[
-            pltpu.VMEM((3, 8 * HEAD, width), jnp.bfloat16),
-            pltpu.VMEM((2 * rows, width), jnp.bfloat16),
-            pltpu.SemaphoreType.DMA((24,)),
-        ],
+        scratch_shapes=[pltpu.VMEM((2 * rows, width), jnp.bfloat16)],
         compiler_params=pltpu.CompilerParams(vmem_limit_bytes=24 * 1024 * 1024),
     )(slots, own, other, gain, *shards)
 
 
-def attend_kernel(base_ref, lo_ref, hi_ref, in_ref, out_ref, *scratch):
-    keys, values, queries, scores_a, scores_b, max_a, max_b = scratch
+def attend_kernel(base_ref, lo_ref, hi_ref, start_ref, end_ref, in_ref, out_ref, *scratch):
+    keys, values, queries, scores, most_ref = scratch
     sources = in_ref.shape[0]
     block = in_ref.shape[1] // 3
     lo, hi = lo_ref[0:1, :], hi_ref[0:1, :]
     low = low_lanes(block)
     row = lax.broadcasted_iota(jnp.int32, (block, LANES), 0)
+    place = lax.broadcasted_iota(jnp.int32, (16, block), 0)
+    column = lax.broadcasted_iota(jnp.int32, (16, block), 1)
+    start, end = jnp.zeros_like(place), jnp.zeros_like(place)
+    for u in range(start_ref.shape[0]):
+        start, end = jnp.where(place == u, start_ref[u], start), jnp.where(place == u, end_ref[u], end)
+    window = keys.shape[0]
+    extra = values.shape[1] - HEAD
+    top = lax.broadcasted_iota(jnp.int32, (extra, KEY_CHUNK), 0) == 0
+    for j in range(values.shape[0]):
+        values[j, HEAD:] = jnp.where(top, 1.0, 0.0).astype(jnp.bfloat16)
 
     def prepare(s, carry):
-        key, value, query = (
-            in_ref[s, i * block : (i + 1) * block].astype(jnp.float32) for i in range(3)
-        )
+        key = in_ref[s, :block].astype(jnp.float32)
         for side in range(2):
-            position = row + (base_ref[side] + s * (2 * block))
-            inside = (position >= lo) & (position < hi)
+            base = base_ref[side] + s * (2 * block)
+            inside = (row + base >= lo) & (row + base < hi)
             at = pl.ds(pl.multiple_of((2 * s + side) * block, block), block)
-            mask, mark = jnp.where(inside, 0.0, big_negative), jnp.where(inside, 1.0, 0.0)
+            mask = jnp.where(inside, 0.0, big_negative)
             keys[at, :] = jnp.where(low, swap_lanes(key) if side else key, mask).astype(jnp.bfloat16)
-            values[at, :] = jnp.where(low, 1.0, value if side else swap_lanes(value)).astype(jnp.bfloat16)
-            queries[at, :] = jnp.where(low, swap_lanes(query) if side else query, mark).astype(jnp.bfloat16)
+            mark = jnp.where((column + base >= start) & (column + base < end), 1.0, 0.0)
+            queries[2 * s + side, HEAD : HEAD + 16] = mark.astype(jnp.bfloat16)
+            queries[2 * s + side, HEAD + 16 :] = jnp.zeros((HEAD - 16, block), jnp.bfloat16)
+        for i in range(2 * block // LANES):
+            at = block + i * HEAD
+            values[s, :HEAD, i * LANES : (i + 1) * LANES] = in_ref[s, at : at + HEAD]
+            side, part = divmod(i * LANES, block)
+            at += block
+            queries[2 * s + side, :HEAD, part : part + LANES] = in_ref[s, at : at + HEAD]
         return carry
 
     lax.fori_loop(0, sources, prepare, 0)
-    window = keys.shape[0]
     chunks = window // KEY_CHUNK
 
-    def score(query, j, scores, best):
-        part = lax.dot_general(
-            query,
-            keys[j * KEY_CHUNK : (j + 1) * KEY_CHUNK, :],
-            (((1,), (1,)), ((), ())),
-            preferred_element_type=jnp.float32,
-        )
-        scores[:, j * KEY_CHUNK : (j + 1) * KEY_CHUNK] = part
-        for t in range(KEY_CHUNK // LANES):
-            piece = part[:, t * LANES : (t + 1) * LANES]
-            best = piece if best is None else jnp.maximum(best, piece)
-        return best
-
-    def weigh(j, scores, row_max, total):
-        probs = jnp.exp2(scores[:, j * KEY_CHUNK : (j + 1) * KEY_CHUNK] - row_max)
-        part = jnp.dot(
-            probs.astype(jnp.bfloat16),
-            values[j * KEY_CHUNK : (j + 1) * KEY_CHUNK, :],
-            preferred_element_type=jnp.float32,
-        )
-        return part if total is None else total + part
-
-    half = block // 2
-
-    def finish(total, source, side):
-        mixed = total / swap_lanes(total)
-        packed = jnp.where(low[:half], swap_lanes(mixed[:half]), mixed[half:])
-        out_ref[2 * source + base_ref[2 + side]] = packed.astype(jnp.bfloat16)
-
-    def both(i, new, old, source_old, side_old):
-        query = queries[pl.ds(pl.multiple_of(i * block, block), block), :]
-        row_max = old[1][:, 0:1]
+    def score(query, j):
+        at = slice(j * KEY_CHUNK, (j + 1) * KEY_CHUNK)
+        return jnp.dot(keys[at, :], query, preferred_element_type=jnp.float32)
+
+    def weigh(j, most):
+        probs = jnp.exp2(scores[j * KEY_CHUNK : (j + 1) * KEY_CHUNK, :] - most)
+        return jnp.dot(values[j], probs.astype(jnp.bfloat16), preferred_element_type=jnp.float32)
+
+    def finish(total, i):
+        mixed = total[:HEAD] / total[HEAD : HEAD + 1]
+        side = lax.rem(i, 2)
+        out_ref[i - side + base_ref[2 + side]] = mixed.astype(jnp.bfloat16)
+
+    def step(i, carry):
+        query = queries[i]
+        most = most_ref[0:1, :]
         best, total = None, None
         for j in range(chunks):
-            best = score(query, j, new[0], best)
-            total = weigh(j, old[0], row_max, total)
-        new[1][...] = jnp.broadcast_to(jnp.max(best, axis=1, keepdims=True), (block, LANES))
-        finish(total, source_old, side_old)
-
-    buffer_a, buffer_b = (scores_a, max_a), (scores_b, max_b)
-
-    def step(i, carry):
-        both(2 * i, buffer_a, buffer_b, jnp.maximum(i - 1, 0), 1)
-        both(2 * i + 1, buffer_b, buffer_a, i, 0)
+            part = weigh(j, most)
+            total = part if total is None else total + part
+            part = score(query, j)
+            scores[j * KEY_CHUNK : (j + 1) * KEY_CHUNK, :] = part
+            part = jnp.max(part.reshape(KEY_CHUNK // 8, 8, block), axis=0)
+            best = part if best is None else jnp.maximum(best, part)
+        most_ref[...] = jnp.broadcast_to(jnp.max(best, axis=0, keepdims=True), (8, block))
+        finish(total, jnp.maximum(i - 1, 0))
         return carry
 
-    lax.fori_loop(0, sources, step, 0)
+    lax.fori_loop(0, 2 * sources, step, 0)
     total = None
     for j in range(chunks):
-        total = weigh(j, scores_b, max_b[:, 0:1], total)
-    finish(total, sources - 1, 1)
-
-
-def attend(bases, lo, hi, parts):
+        part = weigh(j, most_ref[0:1, :])
+        total = part if total is None else total + part
+    finish(total, 2 * sources - 1)
+
+
+def attend(bases, lo, hi, starts, ends, parts):
     sources, block = parts.shape[0], parts.shape[1] // 3
     window = 2 * block * sources
     return pl.pallas_call(
         attend_kernel,
-        out_shape=jax.ShapeDtypeStruct((2 * sources, block // 2, LANES), jnp.bfloat16),
-        in_specs=[SMEM] + [VMEM] * 3,
+        out_shape=jax.ShapeDtypeStruct((2 * sources, HEAD, block), jnp.bfloat16),
+        in_specs=[SMEM] + [VMEM] * 2 + [SMEM] * 2 + [VMEM],
         out_specs=VMEM,
-        scratch_shapes=[pltpu.VMEM((window, LANES), jnp.bfloat16)] * 3
-        + [pltpu.VMEM((block, window), jnp.float32)] * 2
-        + [pltpu.VMEM((block, LANES), jnp.float32)] * 2,
+        scratch_shapes=[
+            pltpu.VMEM((window, LANES), jnp.bfloat16),
+            pltpu.VMEM((window // KEY_CHUNK, HEAD + 16, KEY_CHUNK), jnp.bfloat16),
+            pltpu.VMEM((2 * sources, LANES, block), jnp.bfloat16),
+        ]
+        + [pltpu.VMEM((window, block), jnp.float32), pltpu.VMEM((8, block), jnp.float32)],
         compiler_params=pltpu.CompilerParams(vmem_limit_bytes=24 * 1024 * 1024),
-    )(bases, lo, hi, parts)
+    )(bases, lo, hi, starts, ends, parts)
 
 
 def gate_kernel(mixed, frames, gain, w_out_hbm, w_glu_hbm, residual_ref, gated_ref, *scratch):
@@ -206,13 +196,10 @@
     glu_copy = pltpu.make_async_copy(w_glu_hbm, w_glu, glu_sem)
     out_copy.start()
     glu_copy.start()
-    heads, half, _ = mixed.shape
-    low = low_lanes(half)
+    heads = mixed.shape[0]
     for pair in range(heads // 2):
-        even, odd = mixed[2 * pair].astype(jnp.float32), mixed[2 * pair + 1].astype(jnp.float32)
-        at = slice(pair * LANES, (pair + 1) * LANES)
-        attended[:half, at] = jnp.where(low, even, swap_lanes(odd)).astype(jnp.bfloat16)
-        attended[half:, at] = jnp.where(low, swap_lanes(even), odd).astype(jnp.bfloat16)
+        flipped = jnp.concatenate([mixed[2 * pair], mixed[2 * pair + 1]], axis=0).astype(jnp.float32)
+        attended[:, pair * LANES : (pair + 1) * LANES] = flipped.T.astype(jnp.bfloat16)
     out_copy.wait()
     projected = jnp.dot(attended[...], w_out[...], preferred_element_type=jnp.float32)
     residual = (frames[...].astype(jnp.float32) + projected).astype(jnp.bfloat16)
@@ -382,7 +369,8 @@
     pad = (HEAD, HEAD - utt_lengths.shape[0])
     sides = jnp.stack([yl, 1 - yl])
     bases = jnp.concatenate([window_start + sides * frame_rows, sides])
-    mixed = attend(bases, jnp.pad(starts, pad)[None, :], jnp.pad(ends, pad)[None, :], parts)
+    lo, hi = jnp.pad(starts, pad)[None, :], jnp.pad(ends, pad)[None, :]
+    mixed = attend(bases, lo, hi, starts, ends, parts)
     mixed = lax.all_to_all(mixed, "blk", 0, 0, tiled=True)
     residual, gated = gate(mixed, local_frames, conv_gain[None, :], w_out, w_glu)
 

time: 154 us -> 146 us (0.948)
  Pallas kernels: 42.9 us -> 34 us
    pallas_call x1, Pallas kernels: 23.4 us -> 18.4 us  [attend(): pl.pallas_call(attend_kernel, out_shape=jax.ShapeDtypeStruct((2 * sources...]
    pallas_call x1, Pallas kernels: 10.1 us -> 6.24 us  [project_qkv(): pl.pallas_call(project_kernel, out_shape=jax.ShapeDtypeStruct((8, 3 * row...]
  transfers between devices with their start and end apart: 12 -> 12, of which waited for: 7 -> 7; matrix products, arithmetic and copies ran while one was open for 0% -> 0% of each run, Pallas kernels for 2% -> 3%
where the time goes in v2:
time: 146 us; the launch traced here: 144 us
  waiting for transfers between devices  59.2 us (41%)
  Pallas kernels  34 us (23%)
  starting transfers between devices  26.8 us (18%)
  blocking collectives  18.3 us (13%)
  local copies, waits for them, and re-layouts  4.9 us (3%)
    all_to_all x1, waiting for transfers between devices, body(): lax.all_to_all(parts, 'blk', 0, 0, axis_index_groups=groups, tiled=True)  40 us
    ppermute x11, waiting for transfers between devices, send(): return lax.ppermute(value, ('blk', 'grp'), pairs)  19.2 us
    ppermute x11, starting transfers between devices, send(): return lax.ppermute(value, ('blk', 'grp'), pairs)  18.5 us
    pallas_call x1, Pallas kernels, attend(): pl.pallas_call(attend_kernel, out_shape=jax.ShapeDtypeStruct((2 * sources...  18.4 us
    all_to_all x1, blocking collectives, body(): mixed = lax.all_to_all(mixed, 'blk', 0, 0, tiled=True)  18.3 us
    all_to_all x1, starting transfers between devices, body(): lax.all_to_all(parts, 'blk', 0, 0, axis_index_groups=groups, tiled=True)  8.32 us
    pallas_call x1, Pallas kernels, project_qkv(): pl.pallas_call(project_kernel, out_shape=jax.ShapeDtypeStruct((8, 3 * row...  6.24 us
    unnamed x24, local copies, waits for them, and re-layouts  4.73 us
  transfers between devices with their start and end apart: 12, of which 7 were waited for; matrix products, arithmetic and copies ran while one was open for 0% of the time, Pallas kernels for 3%

profile of v2, /device:TPU:1, one launch (start us, length us, event | category | flops | bytes accessed | tf_op | source)
XLA Modules:
  0.0 143.9 jit_solution(8229682441272011470)
XLA Ops:
  0.0 6.0 %collective-permute-start.1 = (bf16[192,1024]{1,0:T(8,128)(2,1)}, bf16[192,1024]{1,0:T(8,128)(2,1)S(1)}, u32[]{:S(2)}, u32[]{:S(2)}) collective-permute-start(bf16[192,1024]{1,0:T(8,128)(2,1)} %bitcast.34), channel_id=1, source_target_pairs={{0,0},{1,18},{2,3},{3,17},{4,4},{5,22},{6,7},{7,21},{8,8},{9,26},{... | collective-permute-start | bytes 1179656 | tf_op jit(solution)/shard_map/ppermute | solution.py:41
  6.0 2.3 %collective-permute-start.2 = (bf16[192,1024]{1,0:T(8,128)(2,1)}, bf16[192,1024]{1,0:T(8,128)(2,1)S(1)}, u32[]{:S(2)}, u32[]{:S(2)}) collective-permute-start(bf16[192,1024]{1,0:T(8,128)(2,1)} %bitcast.35), channel_id=1, source_target_pairs={{0,12},{1,30},{2,15},{3,29},{4,0},{5,18},{6,3},{7,17},{8,4},{9,22}... | collective-permute-start | bytes 1179656 | tf_op jit(solution)/shard_map/ppermute | solution.py:41
  8.3 1.6 %collective-permute-start.3 = (bf16[192,1024]{1,0:T(8,128)(2,1)}, bf16[192,1024]{1,0:T(8,128)(2,1)S(1)}, u32[]{:S(2)}, u32[]{:S(2)}) collective-permute-start(bf16[192,1024]{1,0:T(8,128)(2,1)} %bitcast.36), channel_id=1, source_target_pairs={{0,4},{1,22},{2,7},{3,21},{4,8},{5,26},{6,11},{7,25},{8,12},{9,30}... | collective-permute-start | bytes 1179656 | tf_op jit(solution)/shard_map/ppermute | solution.py:41
  10.0 2.5 %collective-permute-start.4 = (bf16[192,1024]{1,0:T(8,128)(2,1)}, bf16[192,1024]{1,0:T(8,128)(2,1)S(1)}, u32[]{:S(2)}, u32[]{:S(2)}) collective-permute-start(bf16[192,1024]{1,0:T(8,128)(2,1)} %bitcast.37), channel_id=1, source_target_pairs={{0,8},{1,26},{2,11},{3,25},{4,12},{5,30},{6,15},{7,29},{8,0},{9,18... | collective-permute-start | bytes 1179656 | tf_op jit(solution)/shard_map/ppermute | solution.py:41
  12.4 1.6 %collective-permute-done.1.refs_0_ = bf16[192,1024]{1,0:T(8,128)(2,1)S(1)} collective-permute-done((bf16[192,1024]{1,0:T(8,128)(2,1)}, bf16[192,1024]{1,0:T(8,128)(2,1)S(1)}, u32[]{:S(2)}, u32[]{:S(2)}) %collective-permute-start.1) | collective-permute-done | bytes 393248 | tf_op jit(solution)/shard_map/ppermute | solution.py:41
  14.1 6.1 %collective-permute-done.2.refs_1_ = bf16[192,1024]{1,0:T(8,128)(2,1)S(1)} collective-permute-done((bf16[192,1024]{1,0:T(8,128)(2,1)}, bf16[192,1024]{1,0:T(8,128)(2,1)S(1)}, u32[]{:S(2)}, u32[]{:S(2)}) %collective-permute-start.2) | collective-permute-done | bytes 393248 | tf_op jit(solution)/shard_map/ppermute | solution.py:41
  20.1 8.0 %collective-permute-done.3.refs_2_ = bf16[192,1024]{1,0:T(8,128)(2,1)S(1)} collective-permute-done((bf16[192,1024]{1,0:T(8,128)(2,1)}, bf16[192,1024]{1,0:T(8,128)(2,1)S(1)}, u32[]{:S(2)}, u32[]{:S(2)}) %collective-permute-start.3) | collective-permute-done | bytes 393248 | tf_op jit(solution)/shard_map/ppermute | solution.py:41
  28.1 0.5 collective-permute-start.8
  28.6 0.1 stack.47.slot_ref
  28.7 1.1 collective-permute-done.7.refs_6_
  29.8 0.7 collective-permute-done.8.refs_7_
  30.5 1.0 copy-done.3
  31.5 0.7 copy-done.9
  32.2 6.2 %shard_map.100 = bf16[8,768,128]{2,1,0:T(8,128)(2,1)} custom-call(s32[8]{0:T(128)S(1)} %stack.47.slot_ref, bf16[256,1024]{1,0:T(8,128)(2,1)S(1)} %bitcast.25, bf16[256,1024]{1,0:T(8,128)(2,1)S(1)} %collective-permute-done.other_ref, f32[1,1024]{1,0:T(1,128)S(1)} %bitcast.32, bf16[192,1024]{1,0:T(8,128)(2,1)S(1)} %collective-permute-done.1.refs_0_, ...), custom_call_target="tpu_custom_call" | custom-call | tf_op jit(solution)/shard_map/pallas_call | solution.py:89
  38.5 8.3 %all-to-all-start = ((bf16[8,768,128]{2,1,0:T(8,128)(2,1)}), bf16[8,768,128]{2,1,0:T(8,128)(2,1)S(1)}, u32[]{:S(2)}, u32[]{:S(2)}) async-start(bf16[8,768,128]{2,1,0:T(8,128)(2,1)} %shard_map.100), calls=%async_computation | async-start | bytes 3145728 | tf_op jit(solution)/shard_map/all_to_all | solution.py:366
  46.8 0.2 reduce-window.9
  47.0 0.1 fusion
  47.1 0.1 pad_add_fusion.base_ref
  47.2 0.1 pad_bitcast_fusion
  47.2 40.0 %all-to-all-done.in_ref = bf16[8,768,128]{2,1,0:T(8,128)(2,1)S(1)} async-done(((bf16[8,768,128]{2,1,0:T(8,128)(2,1)}), bf16[8,768,128]{2,1,0:T(8,128)(2,1)S(1)}, u32[]{:S(2)}, u32[]{:S(2)}) %all-to-all-start) | async-done | bytes 1572896 | tf_op jit(solution)/shard_map/all_to_all | solution.py:366
  87.2 18.4 %shard_map.101 = bf16[16,64,256]{2,1,0:T(8,128)(2,1)S(1)} custom-call(s32[4]{0:T(128)S(1)} %pad_add_fusion.base_ref, s32[1,128]{1,0:T(1,128)S(1)} %get-tuple-element.12.lo_ref, s32[1,128]{1,0:T(1,128)S(1)} %get-tuple-element.11.hi_ref, s32[8]{0:T(128)S(1)} %bitcast_subtract_fusion.start_ref, s32[8]{0:T(128)S(1)} %bitcast.28, ...), custom_call_target="tpu_custom_call" | custom-call | tf_op jit(solution)/shard_map/pallas_call | solution.py:178
  105.6 18.3 %all_to_all.10.mixed = bf16[16,64,256]{2,1,0:T(8,128)(2,1)S(1)} all-to-all(bf16[16,64,256]{2,1,0:T(8,128)(2,1)S(1)} %shard_map.101), channel_id=1, replica_groups=mesh['blk'=16,'grp'=16] {'blk'}, dimensions={0} | all-to-all | bytes 1048576 | tf_op jit(solution)/shard_map/all_to_all | solution.py:374
  124.0 0.0 copy-start
  124.0 2.2 %copy-done = bf16[1024,2048]{1,0:T(8,128)(2,1)S(1)} copy-done((bf16[1024,2048]{1,0:T(8,128)(2,1)S(1)}, bf16[1024,2048]{1,0:T(8,128)(2,1)}, u32[]{:S(2)}) %copy-start) | copy-done | bytes 4194328
  126.2 2.9 %shard_map.102 = (bf16[256,1024]{1,0:T(8,128)(2,1)S(1)}, bf16[256,1024]{1,0:T(8,128)(2,1)S(1)}) custom-call(bf16[16,64,256]{2,1,0:T(8,128)(2,1)S(1)} %all_to_all.10.mixed, bf16[256,1024]{1,0:T(8,128)(2,1)S(1)} %bitcast.26, f32[1,1024]{1,0:T(1,128)S(1)} %bitcast.31, bf16[1024,1024]{1,0:T(8,128)(2,1)S(1)} %copy-done.1, bf16[1024,2048]{1,0:T(8,128)(2,1)S(1)} %copy-done), custom_call_target="tpu_custom_call" | custom-call | tf_op jit(solution)/shard_map/pallas_call | solution.py:219
  129.1 0.0 copy-start.5
  129.1 0.8 copy-done.5
  129.9 3.6 %collective-permute-start.10 = (bf16[16,1024]{1,0:T(8,128)(2,1)S(1)}, bf16[16,1024]{1,0:T(8,128)(2,1)S(1)}, u32[]{:S(2)}, u32[]{:S(2)}) collective-permute-start(bf16[16,1024]{1,0:T(8,128)(2,1)S(1)} %get-tuple-element.9), channel_id=1, source_target_pairs={{1,240},{2,241},{3,242},{4,243},{5,244},{6,245},{7,246},{8,247},{9... | collective-permute-start | bytes 98312 | tf_op jit(solution)/shard_map/ppermute | solution.py:41
  133.5 1.9 %collective-permute-start.9 = (bf16[16,1024]{1,0:T(8,128)(2,1)S(1)}, bf16[16,1024]{1,0:T(8,128)(2,1)S(1)}, u32[]{:S(2)}, u32[]{:S(2)}) collective-permute-start(bf16[16,1024]{1,0:T(8,128)(2,1)S(1)} %get-tuple-element.10), channel_id=1, source_target_pairs={{0,16},{1,17},{2,18},{3,19},{4,20},{5,21},{6,22},{7,23},{8,24},{9,... | collective-permute-start | bytes 98312 | tf_op jit(solution)/shard_map/ppermute | solution.py:41
  135.5 3.6 %shard_map.103.inner = f32[256,1024]{1,0:T(8,128)S(1)} custom-call(s32[1]{0:T(128)} %bitcast.first_ref, s32[8]{0:T(128)S(1)} %bitcast_subtract_fusion.start_ref, s32[8]{0:T(128)S(1)} %bitcast.29, bf16[256,1024]{1,0:T(8,128)(2,1)S(1)} %get-tuple-element.7.gated, f32[31,1024]{1,0:T(8,128)S(1)} %copy-done.7), custom_call_target="tpu_custom_call" | custom-call | tf_op jit(solution)/shard_map/pallas_call | solution.py:284
  139.1 1.8 %collective-permute-done.9.left = bf16[16,1024]{1,0:T(8,128)(2,1)S(1)} collective-permute-done((bf16[16,1024]{1,0:T(8,128)(2,1)S(1)}, bf16[16,1024]{1,0:T(8,128)(2,1)S(1)}, u32[]{:S(2)}, u32[]{:S(2)}) %collective-permute-start.9) | collective-permute-done | bytes 32800 | tf_op jit(solution)/shard_map/ppermute | solution.py:41
  140.9 2.9 %shard_map.104 = bf16[256,1024]{1,0:T(8,128)(2,1)} custom-call(s32[1]{0:T(128)} %bitcast.first_ref, s32[8]{0:T(128)S(1)} %bitcast_subtract_fusion.start_ref, s32[8]{0:T(128)S(1)} %bitcast.30, f32[256,1024]{1,0:T(8,128)S(1)} %shard_map.103.inner, bf16[16,1024]{1,0:T(8,128)(2,1)S(1)} %collective-permute-done.9.left, ...), custom_call_target="tpu_custom_call" | custom-call | tf_op jit(solution)/shard_map/pallas_call | solution.py:325
  (29 shorter events, 0.1 us)
Async XLA Ops:
  0.0 14.1 %collective-permute-start.1 = (bf16[192,1024]{1,0:T(8,128)(2,1)}, bf16[192,1024]{1,0:T(8,128)(2,1)S(1)}, u32[]{:S(2)}, u32[]{:S(2)}) collective-permute-start(bf16[192,1024]{1,0:T(8,128)(2,1)} %bitcast.34), channel_id=1, source_target_pairs={{0,0},{1,18},{2,3},{3,17},{4,4},{5,22},{6,7},{7,21},{8,8},{9,26},{... | collective-permute-start | bytes 1179656 | tf_op jit(solution)/shard_map/ppermute | solution.py:41
  6.0 14.1 %collective-permute-start.2 = (bf16[192,1024]{1,0:T(8,128)(2,1)}, bf16[192,1024]{1,0:T(8,128)(2,1)S(1)}, u32[]{:S(2)}, u32[]{:S(2)}) collective-permute-start(bf16[192,1024]{1,0:T(8,128)(2,1)} %bitcast.35), channel_id=1, source_target_pairs={{0,12},{1,30},{2,15},{3,29},{4,0},{5,18},{6,3},{7,17},{8,4},{9,22}... | collective-permute-start | bytes 1179656 | tf_op jit(solution)/shard_map/ppermute | solution.py:41
  8.3 19.8 %collective-permute-start.3 = (bf16[192,1024]{1,0:T(8,128)(2,1)}, bf16[192,1024]{1,0:T(8,128)(2,1)S(1)}, u32[]{:S(2)}, u32[]{:S(2)}) collective-permute-start(bf16[192,1024]{1,0:T(8,128)(2,1)} %bitcast.36), channel_id=1, source_target_pairs={{0,4},{1,22},{2,7},{3,21},{4,8},{5,26},{6,11},{7,25},{8,12},{9,30}... | collective-permute-start | bytes 1179656 | tf_op jit(solution)/shard_map/ppermute | solution.py:41
  10.0 18.1 %collective-permute-start.4 = (bf16[192,1024]{1,0:T(8,128)(2,1)}, bf16[192,1024]{1,0:T(8,128)(2,1)S(1)}, u32[]{:S(2)}, u32[]{:S(2)}) collective-permute-start(bf16[192,1024]{1,0:T(8,128)(2,1)} %bitcast.37), channel_id=1, source_target_pairs={{0,8},{1,26},{2,11},{3,25},{4,12},{5,30},{6,15},{7,29},{8,0},{9,18... | collective-permute-start | bytes 1179656 | tf_op jit(solution)/shard_map/ppermute | solution.py:41
  12.4 16.3 %collective-permute-start = (bf16[256,1024]{1,0:T(8,128)(2,1)}, bf16[256,1024]{1,0:T(8,128)(2,1)S(1)}, u32[]{:S(2)}, u32[]{:S(2)}) collective-permute-start(bf16[256,1024]{1,0:T(8,128)(2,1)} %bitcast.24), channel_id=1, source_target_pairs={{0,16},{1,17},{2,18},{3,19},{4,20},{5,21},{6,22},{7,23},{8,24},{9,... | collective-permute-start | bytes 1572872 | tf_op jit(solution)/shard_map/ppermute | solution.py:41
  14.1 14.6 %collective-permute-start.5 = (bf16[192,1024]{1,0:T(8,128)(2,1)S(1)}, bf16[192,1024]{1,0:T(8,128)(2,1)S(1)}, u32[]{:S(2)}, u32[]{:S(2)}) collective-permute-start(bf16[192,1024]{1,0:T(8,128)(2,1)S(1)} %collective-permute-done.1.refs_0_), channel_id=1, source_target_pairs={{0,1},{1,0},{2,3},{3,2},{4,5},{5,4},{6,7},{7,6},{8,9},{9,8},{10,11... | collective-permute-start | bytes 1179656 | tf_op jit(solution)/shard_map/ppermute | solution.py:41
  20.1 8.6 %collective-permute-start.6 = (bf16[192,1024]{1,0:T(8,128)(2,1)S(1)}, bf16[192,1024]{1,0:T(8,128)(2,1)S(1)}, u32[]{:S(2)}, u32[]{:S(2)}) collective-permute-start(bf16[192,1024]{1,0:T(8,128)(2,1)S(1)} %collective-permute-done.2.refs_1_), channel_id=1, source_target_pairs={{0,1},{1,0},{2,3},{3,2},{4,5},{5,4},{6,7},{7,6},{8,9},{9,8},{10,11... | collective-permute-start | bytes 1179656 | tf_op jit(solution)/shard_map/ppermute | solution.py:41
  28.1 1.7 %collective-permute-start.7 = (bf16[192,1024]{1,0:T(8,128)(2,1)S(1)}, bf16[192,1024]{1,0:T(8,128)(2,1)S(1)}, u32[]{:S(2)}, u32[]{:S(2)}) collective-permute-start(bf16[192,1024]{1,0:T(8,128)(2,1)S(1)} %collective-permute-done.3.refs_2_), channel_id=1, source_target_pairs={{0,1},{1,0},{2,3},{3,2},{4,5},{5,4},{6,7},{7,6},{8,9},{9,8},{10,11... | collective-permute-start | bytes 1179656 | tf_op jit(solution)/shard_map/ppermute | solution.py:41
  28.1 2.4 %collective-permute-start.8 = (bf16[192,1024]{1,0:T(8,128)(2,1)S(1)}, bf16[192,1024]{1,0:T(8,128)(2,1)}, u32[]{:S(2)}, u32[]{:S(2)}) collective-permute-start(bf16[192,1024]{1,0:T(8,128)(2,1)S(1)} %collective-permute-done.4.refs_3_), channel_id=1, source_target_pairs={{0,1},{1,0},{2,3},{3,2},{4,5},{5,4},{6,7},{7,6},{8,9},{9,8},{10,11... | collective-permute-start | bytes 1179656 | tf_op jit(solution)/shard_map/ppermute | solution.py:41
  30.5 1.0 copy-start.3
  31.5 0.7 copy-start.9
  38.5 8.4 %copy-start.11 = (s32[8]{0:T(128)S(1)}, s32[8]{0:T(128)}, u32[]{:S(2)}) copy-start(s32[8]{0:T(128)} %param.11) | copy-start | bytes 100
  38.5 48.8 %all-to-all-start = ((bf16[8,768,128]{2,1,0:T(8,128)(2,1)}), bf16[8,768,128]{2,1,0:T(8,128)(2,1)S(1)}, u32[]{:S(2)}, u32[]{:S(2)}) async-start(bf16[8,768,128]{2,1,0:T(8,128)(2,1)} %shard_map.100), calls=%async_computation | async-start | bytes 3145728 | tf_op jit(solution)/shard_map/all_to_all | solution.py:366
  46.8 77.2 %copy-start.4 = (bf16[1,256,1024]{2,1,0:T(8,128)(2,1)S(1)}, bf16[1,256,1024]{2,1,0:T(8,128)(2,1)}, u32[]{:S(2)}) copy-start(bf16[1,256,1024]{2,1,0:T(8,128)(2,1)} %param.10) | copy-start | bytes 1572868
  46.8 77.2 %copy-start.8 = (f32[1024]{0:T(1024)S(1)}, f32[1024]{0:T(1024)}, u32[]{:S(2)}) copy-start(f32[1024]{0:T(1024)} %param.15) | copy-start | bytes 12292
  87.2 36.7 %copy-start.1 = (bf16[1024,1024]{1,0:T(8,128)(2,1)S(1)}, bf16[1024,1024]{1,0:T(8,128)(2,1)}, u32[]{:S(2)}) copy-start(bf16[1024,1024]{1,0:T(8,128)(2,1)} %w_out_hbm.1) | copy-start | bytes 6291460
  124.0 2.2 %copy-start = (bf16[1024,2048]{1,0:T(8,128)(2,1)S(1)}, bf16[1024,2048]{1,0:T(8,128)(2,1)}, u32[]{:S(2)}) copy-start(bf16[1024,2048]{1,0:T(8,128)(2,1)} %w_glu_hbm.1) | copy-start | bytes 12582916
  126.2 9.3 %copy-start.7 = (f32[31,1024]{1,0:T(8,128)S(1)}, f32[31,1024]{1,0:T(8,128)}, u32[]{:S(2)}) copy-start(f32[31,1024]{1,0:T(8,128)} %weights.3) | copy-start | bytes 380932
  126.2 14.7 %copy-start.2 = (bf16[1024,1024]{1,0:T(8,128)(2,1)S(1)}, bf16[1024,1024]{1,0:T(8,128)(2,1)}, u32[]{:S(2)}) copy-start(bf16[1024,1024]{1,0:T(8,128)(2,1)} %w_proj_hbm.1) | copy-start | bytes 6291460
  126.2 14.7 %copy-start.10 = (f32[1024]{0:T(1024)S(1)}, f32[1024]{0:T(1024)}, u32[]{:S(2)}) copy-start(f32[1024]{0:T(1024)} %param.18) | copy-start | bytes 12292
  129.1 0.8 copy-start.5
  129.9 11.0 %copy-start.6 = (bf16[256,1024]{1,0:T(8,128)(2,1)S(1)}, bf16[256,1024]{1,0:T(8,128)(2,1)}, u32[]{:S(2)}) copy-start(bf16[256,1024]{1,0:T(8,128)(2,1)} %copy-done.5) | copy-start | bytes 1572868
  129.9 9.2 %collective-permute-start.10 = (bf16[16,1024]{1,0:T(8,128)(2,1)S(1)}, bf16[16,1024]{1,0:T(8,128)(2,1)S(1)}, u32[]{:S(2)}, u32[]{:S(2)}) collective-permute-start(bf16[16,1024]{1,0:T(8,128)(2,1)S(1)} %get-tuple-element.9), channel_id=1, source_target_pairs={{1,240},{2,241},{3,242},{4,243},{5,244},{6,245},{7,246},{8,247},{9... | collective-permute-start | bytes 98312 | tf_op jit(solution)/shard_map/ppermute | solution.py:41
  133.5 7.3 %collective-permute-start.9 = (bf16[16,1024]{1,0:T(8,128)(2,1)S(1)}, bf16[16,1024]{1,0:T(8,128)(2,1)S(1)}, u32[]{:S(2)}, u32[]{:S(2)}) collective-permute-start(bf16[16,1024]{1,0:T(8,128)(2,1)S(1)} %get-tuple-element.10), channel_id=1, source_target_pairs={{0,16},{1,17},{2,18},{3,19},{4,20},{5,21},{6,22},{7,23},{8,24},{9,... | collective-permute-start | bytes 98312 | tf_op jit(solution)/shard_map/ppermute | solution.py:41

commit v3 on v2

--- a/solution.py
+++ b/solution.py
@@ -12,6 +12,7 @@
 RIM = 16
 ROWS = 16
 OFFSETS = (0, 1, 3, 2)
+SEND_ORDER = (4, 3, 5, 2, 6, 1, 7)
 LOG2E = 1.4426950408889634
 
 epsilon = 1e-05
@@ -55,84 +56,152 @@
     return pltpu.roll(values, HEAD, 1)
 
 
-def project_kernel(slot_ref, own_ref, other_ref, gain_ref, *refs):
-    shards, out, normed = refs[:8], refs[8], refs[9]
+X, CORE, Z, YL, WINDOW, FIRST = range(6)
+
+
+def shard_head(me, i):
+    core = me[CORE] if i < 4 else 1 - me[CORE]
+    return 2 * lax.rem(me[X] + OFFSETS[i % 4], 4) + core
+
+
+def inside(position, start_ref, end_ref, place):
+    start, end = jnp.zeros_like(position), jnp.zeros_like(position)
+    for u in range(start_ref.shape[0]):
+        start, end = jnp.where(place == u, start_ref[u], start), jnp.where(place == u, end_ref[u], end)
+    return (position >= start) & (position < end)
+
+
+CONTRACT = (((1,), (1,)), ((), ()))
+
+
+def transposed(out, index, start, flipped):
+    for j in range(flipped.shape[1] // LANES):
+        at = start + j * HEAD
+        out[index, at : at + HEAD] = flipped[:, j * LANES : (j + 1) * LANES].astype(jnp.bfloat16)
+
+
+def key_value_kernel(me, own_hbm, gain_hbm, other_hbm, *refs):
+    shards_hbm, out, normed = refs[:8], refs[8], refs[9]
+    own_ref, gain_ref, other_ref, shards, sems = refs[10:]
+    pairs = [(own_hbm, own_ref), (gain_hbm, gain_ref), (other_hbm, other_ref)]
+    pairs += [(shards_hbm[i], shards.at[i]) for i in range(8)]
+    copies = [pltpu.make_async_copy(a, b, sems.at[i]) for i, (a, b) in enumerate(pairs)]
+    for copy in copies:
+        copy.start()
+    copies[1].wait()
     rows = own_ref.shape[0]
     gain = gain_ref[0:1, :]
+    copies[0].wait()
     normed[:rows] = normalize(own_ref[...].astype(jnp.float32), gain).astype(jnp.bfloat16)
+    copies[2].wait()
     normed[rows:] = normalize(other_ref[...].astype(jnp.float32), gain).astype(jnp.bfloat16)
     low = low_lanes(rows)
-    contract = (((1,), (1,)), ((), ()))
-    for pair in range(4):
-        weights = jnp.concatenate(
-            [shards[i][HEAD : 2 * HEAD, :] for i in (2 * pair, 2 * pair + 1)], axis=0
-        )
-        both = lax.dot_general(normed[...], weights, contract, preferred_element_type=jnp.float32)
+    for i in range(0, 8, 2):
+        copies[3 + i].wait()
+        copies[4 + i].wait()
+        heads = shard_head(me, i), shard_head(me, i + 1)
+        weights = jnp.concatenate([shards[i, :HEAD], shards[i + 1, :HEAD]], axis=0)
+        both = lax.dot_general(normed[...], weights, CONTRACT, preferred_element_type=jnp.float32)
         own, other = both[:rows], both[rows:]
-        out[slot_ref[2 * pair], :rows] = jnp.where(low, own, swap_lanes(other)).astype(jnp.bfloat16)
-        out[slot_ref[2 * pair + 1], :rows] = jnp.where(low, swap_lanes(own), other).astype(jnp.bfloat16)
-        for i in (2 * pair, 2 * pair + 1):
-            weights = jnp.concatenate([shards[i][2 * HEAD :, :], shards[i][:HEAD, :]], axis=0)
-            flipped = lax.dot_general(
-                weights, normed[...], contract, preferred_element_type=jnp.float32
-            )
-            value = flipped[:HEAD].astype(jnp.bfloat16)
-            query = (flipped[HEAD:] * (HEAD**-0.5 * LOG2E)).astype(jnp.bfloat16)
-            for part, flat_part in enumerate((value, query)):
-                for j in range(2 * rows // LANES):
-                    at = (part + 1) * rows + j * HEAD
-                    out[slot_ref[i], at : at + HEAD] = flat_part[:, j * LANES : (j + 1) * LANES]
-
-
-def project_qkv(slots, own, other, gain, shards):
+        out[heads[0], :rows] = jnp.where(low, own, swap_lanes(other)).astype(jnp.bfloat16)
+        out[heads[1], :rows] = jnp.where(low, swap_lanes(own), other).astype(jnp.bfloat16)
+        weights = jnp.concatenate([shards[i, HEAD:], shards[i + 1, HEAD:]], axis=0)
+        both = lax.dot_general(weights, normed[...], CONTRACT, preferred_element_type=jnp.float32)
+        transposed(out, heads[0], rows, both[:HEAD])
+        transposed(out, heads[1], rows, both[HEAD:])
+
+
+def project_key_value(me, own, other, gain, shards):
     rows, width = own.shape
     return pl.pallas_call(
-        project_kernel,
-        out_shape=jax.ShapeDtypeStruct((8, 3 * rows, LANES), jnp.bfloat16),
-        in_specs=[SMEM] + [VMEM] * 11,
-        out_specs=VMEM,
-        scratch_shapes=[pltpu.VMEM((2 * rows, width), jnp.bfloat16)],
-        compiler_params=pltpu.CompilerParams(vmem_limit_bytes=24 * 1024 * 1024),
-    )(slots, own, other, gain, *shards)
-
-
-def attend_kernel(base_ref, lo_ref, hi_ref, start_ref, end_ref, in_ref, out_ref, *scratch):
-    keys, values, queries, scores, most_ref = scratch
+        key_value_kernel,
+        out_shape=[
+            jax.ShapeDtypeStruct((8, 2 * rows, LANES), jnp.bfloat16),
+            jax.ShapeDtypeStruct((2 * rows, width), jnp.bfloat16),
+        ],
+        in_specs=[SMEM] + [HBM] * 11,
+        out_specs=[VMEM] * 2,
+        scratch_shapes=[
+            pltpu.VMEM(own.shape, jnp.bfloat16),
+            pltpu.VMEM(gain.shape, jnp.float32),
+            pltpu.VMEM(own.shape, jnp.bfloat16),
+            pltpu.VMEM((8,) + shards[0].shape, jnp.bfloat16),
+            pltpu.SemaphoreType.DMA((11,)),
+        ],
+        compiler_params=pltpu.CompilerParams(vmem_limit_bytes=60 * 1024 * 1024),
+    )(me, own, gain, other, *shards)
+
+
+def query_kernel(me, normed, *refs):
+    near, far, outs, staged = refs[:4], refs[4], refs[5:13], refs[13]
+    shards = [ref[...] for ref in near] + [far[i * HEAD : (i + 1) * HEAD, :] for i in range(4)]
+    for i in range(0, 8, 2):
+        weights = jnp.concatenate([shards[i], shards[i + 1]], axis=0)
+        both = lax.dot_general(weights, normed[...], CONTRACT, preferred_element_type=jnp.float32)
+        both = both * (HEAD**-0.5 * LOG2E)
+        transposed(staged, lax.rem(shard_head(me, i) + 8 - me[Z], 8), 0, both[:HEAD])
+        transposed(staged, lax.rem(shard_head(me, i + 1) + 8 - me[Z], 8), 0, both[HEAD:])
+    for d in range(8):
+        outs[d][...] = staged[d]
+
+
+def project_query(me, normed, shards):
+    shape = (normed.shape[0] // 2, LANES)
+    return pl.pallas_call(
+        query_kernel,
+        out_shape=[jax.ShapeDtypeStruct(shape, jnp.bfloat16)] * 8,
+        in_specs=[SMEM] + [VMEM] * 6,
+        out_specs=[VMEM] * 8,
+        scratch_shapes=[pltpu.VMEM((8,) + shape, jnp.bfloat16)],
+        compiler_params=pltpu.CompilerParams(vmem_limit_bytes=16 * 1024 * 1024),
+    )(me, normed, *shards)
+
+
+def attend_kernel(me, start_ref, end_ref, in_ref, *refs):
+    parts_hbm, out_ref = refs[:8], refs[8]
+    keys, values, queries, scores, most_ref, parts_q, sems = refs[9:]
+    copies = [pltpu.make_async_copy(parts_hbm[d], parts_q.at[d], sems.at[d]) for d in range(8)]
+    for copy in copies:
+        copy.start()
     sources = in_ref.shape[0]
-    block = in_ref.shape[1] // 3
-    lo, hi = lo_ref[0:1, :], hi_ref[0:1, :]
+    block = in_ref.shape[1] // 2
     low = low_lanes(block)
     row = lax.broadcasted_iota(jnp.int32, (block, LANES), 0)
+    lane = lax.broadcasted_iota(jnp.int32, (block, LANES), 1) - HEAD
     place = lax.broadcasted_iota(jnp.int32, (16, block), 0)
     column = lax.broadcasted_iota(jnp.int32, (16, block), 1)
-    start, end = jnp.zeros_like(place), jnp.zeros_like(place)
-    for u in range(start_ref.shape[0]):
-        start, end = jnp.where(place == u, start_ref[u], start), jnp.where(place == u, end_ref[u], end)
     window = keys.shape[0]
-    extra = values.shape[1] - HEAD
-    top = lax.broadcasted_iota(jnp.int32, (extra, KEY_CHUNK), 0) == 0
+    top = lax.broadcasted_iota(jnp.int32, (values.shape[1] - HEAD, KEY_CHUNK), 0) == 0
     for j in range(values.shape[0]):
         values[j, HEAD:] = jnp.where(top, 1.0, 0.0).astype(jnp.bfloat16)
 
     def prepare(s, carry):
         key = in_ref[s, :block].astype(jnp.float32)
         for side in range(2):
-            base = base_ref[side] + s * (2 * block)
-            inside = (row + base >= lo) & (row + base < hi)
+            shard = 2 * s + (me[YL] if side == 0 else 1 - me[YL])
+            base = me[WINDOW] + shard * block
             at = pl.ds(pl.multiple_of((2 * s + side) * block, block), block)
-            mask = jnp.where(inside, 0.0, big_negative)
+            mask = jnp.where(inside(row + base, start_ref, end_ref, lane), 0.0, big_negative)
             keys[at, :] = jnp.where(low, swap_lanes(key) if side else key, mask).astype(jnp.bfloat16)
-            mark = jnp.where((column + base >= start) & (column + base < end), 1.0, 0.0)
-            queries[2 * s + side, HEAD : HEAD + 16] = mark.astype(jnp.bfloat16)
-            queries[2 * s + side, HEAD + 16 :] = jnp.zeros((HEAD - 16, block), jnp.bfloat16)
         for i in range(2 * block // LANES):
             at = block + i * HEAD
             values[s, :HEAD, i * LANES : (i + 1) * LANES] = in_ref[s, at : at + HEAD]
-            side, part = divmod(i * LANES, block)
-            at += block
-            queries[2 * s + side, :HEAD, part : part + LANES] = in_ref[s, at : at + HEAD]
         return carry
 
+    def origin(i):
+        d, side = i // 2, lax.rem(i, 2)
+        shard = jnp.where(side == 0, me[YL], 1 - me[YL])
+        return 2 * lax.rem(me[Z] + 8 - d, 8) + shard
+
+    for i in range(2 * sources):
+        if i % 2 == 0:
+            copies[i // 2].wait()
+        mark = inside(column + (me[WINDOW] + origin(i) * block), start_ref, end_ref, place)
+        queries[i, HEAD : HEAD + 16] = jnp.where(mark, 1.0, 0.0).astype(jnp.bfloat16)
+        queries[i, HEAD + 16 :] = jnp.zeros((HEAD - 16, block), jnp.bfloat16)
+        for j in range(block // LANES):
+            at = ((i % 2) * (block // LANES) + j) * HEAD
+            queries[i, :HEAD, j * LANES : (j + 1) * LANES] = parts_q[i // 2, at : at + HEAD]
     lax.fori_loop(0, sources, prepare, 0)
     chunks = window // KEY_CHUNK
 
@@ -146,8 +215,7 @@
 
     def finish(total, i):
         mixed = total[:HEAD] / total[HEAD : HEAD + 1]
-        side = lax.rem(i, 2)
-        out_ref[i - side + base_ref[2 + side]] = mixed.astype(jnp.bfloat16)
+        out_ref[origin(i)] = mixed.astype(jnp.bfloat16)
 
     def step(i, carry):
         query = queries[i]
@@ -172,22 +240,23 @@
     finish(total, 2 * sources - 1)
 
 
-def attend(bases, lo, hi, starts, ends, parts):
-    sources, block = parts.shape[0], parts.shape[1] // 3
+def attend(me, starts, ends, key_value, queries):
+    sources, block = key_value.shape[0], key_value.shape[1] // 2
     window = 2 * block * sources
     return pl.pallas_call(
         attend_kernel,
         out_shape=jax.ShapeDtypeStruct((2 * sources, HEAD, block), jnp.bfloat16),
-        in_specs=[SMEM] + [VMEM] * 2 + [SMEM] * 2 + [VMEM],
+        in_specs=[SMEM] * 3 + [VMEM] + [HBM] * 8,
         out_specs=VMEM,
         scratch_shapes=[
             pltpu.VMEM((window, LANES), jnp.bfloat16),
             pltpu.VMEM((window // KEY_CHUNK, HEAD + 16, KEY_CHUNK), jnp.bfloat16),
             pltpu.VMEM((2 * sources, LANES, block), jnp.bfloat16),
         ]
-        + [pltpu.VMEM((window, block), jnp.float32), pltpu.VMEM((8, block), jnp.float32)],
+        + [pltpu.VMEM((window, block), jnp.float32), pltpu.VMEM((8, block), jnp.float32)]
+        + [pltpu.VMEM((8, block, LANES), jnp.bfloat16), pltpu.SemaphoreType.DMA((8,))],
         compiler_params=pltpu.CompilerParams(vmem_limit_bytes=24 * 1024 * 1024),
-    )(bases, lo, hi, starts, ends, parts)
+    )(me, starts, ends, key_value, *queries)
 
 
 def gate_kernel(mixed, frames, gain, w_out_hbm, w_glu_hbm, residual_ref, gated_ref, *scratch):
@@ -228,7 +297,7 @@
             pltpu.SemaphoreType.DMA,
             pltpu.SemaphoreType.DMA,
         ],
-        compiler_params=pltpu.CompilerParams(vmem_limit_bytes=24 * 1024 * 1024),
+        compiler_params=pltpu.CompilerParams(vmem_limit_bytes=58 * 1024 * 1024),
     )(mixed, frames, gain, w_out, w_glu)
 
 
@@ -251,7 +320,7 @@
     return totals
 
 
-def inner_kernel(first_ref, start_ref, end_ref, gated, weights, out, padded):
+def inner_kernel(me, start_ref, end_ref, gated, weights, out, padded):
     rows, width = gated.shape
     for c in range(width // LANES):
         padded[c, :RIM] = jnp.zeros((RIM, LANES), jnp.float32)
@@ -260,7 +329,7 @@
 
     def step(i, carry):
         row = pl.multiple_of(i * ROWS, ROWS)
-        position = first_ref[0] + row
+        position = me[FIRST] + row
         crossed = False
         for u in range(1, start_ref.shape[0]):
             crossed |= (start_ref[u] > position - RIM) & (start_ref[u] < position + ROWS + RIM)
@@ -279,7 +348,7 @@
     lax.fori_loop(0, rows // ROWS, step, 0)
 
 
-def convolve_inner(first, starts, ends, gated, weights):
+def convolve_inner(me, starts, ends, gated, weights):
     rows, width = gated.shape
     return pl.pallas_call(
         inner_kernel,
@@ -288,11 +357,11 @@
         out_specs=VMEM,
         scratch_shapes=[pltpu.VMEM((width // LANES, rows + 2 * RIM, LANES), jnp.float32)],
         compiler_params=pltpu.CompilerParams(vmem_limit_bytes=16 * 1024 * 1024),
-    )(first, starts, ends, gated, weights)
+    )(me, starts, ends, gated, weights)
 
 
 def last_kernel(
-    first_ref, start_ref, end_ref, inner, left, right, residual, weights, gain, w_proj_hbm, out, *scratch
+    me, start_ref, end_ref, inner, left, right, residual, weights, gain, w_proj_hbm, out, *scratch
 ):
     w_proj, total, edge, sem = scratch
     copy = pltpu.make_async_copy(w_proj_hbm, w_proj, sem)
@@ -308,7 +377,7 @@
             edge[c, at : at + RIM] = rim[:, c * LANES : (c + 1) * LANES].astype(jnp.float32)
         span = (0, RIM - 1) if side == 0 else (RIM, count)
         parts = convolve(
-            edge, 0, weights, *span, first_ref[0] + row, start_ref, end_ref, True
+            edge, 0, weights, *span, me[FIRST] + row, start_ref, end_ref, True
         )
         for c, part in enumerate(parts):
             lanes = slice(c * LANES, (c + 1) * LANES)
@@ -320,7 +389,7 @@
     out[...] = (residual[...].astype(jnp.float32) + projected).astype(jnp.bfloat16)
 
 
-def finish_block(first, starts, ends, inner, left, right, residual, weights, gain, w_proj):
+def finish_block(me, starts, ends, inner, left, right, residual, weights, gain, w_proj):
     _, width = inner.shape
     return pl.pallas_call(
         last_kernel,
@@ -334,7 +403,7 @@
             pltpu.SemaphoreType.DMA,
         ],
         compiler_params=pltpu.CompilerParams(vmem_limit_bytes=24 * 1024 * 1024),
-    )(first, starts, ends, inner, left, right, residual, weights, gain, w_proj)
+    )(me, starts, ends, inner, left, right, residual, weights, gain, w_proj)
 
 
 def body(
@@ -343,13 +412,13 @@
     frame_rows = frames.shape[1]
     block_index = lax.axis_index("blk")
     group_index = lax.axis_index("grp")
-    yl = block_index % 2
+    z, yl = block_index // 2, block_index % 2
     x, core = group_index // 4, group_index % 2
     window_start = group_index * (16 * frame_rows)
     first_frame = window_start + block_index * frame_rows
     local_frames = frames[0]
-
-    other_frames = send(local_frames, lambda x, yh, c, z, yl: (x, yh, c, z, 1 - yl))
+    me = jnp.stack([x, core, z, yl, window_start, first_frame]).astype(jnp.int32)
+
     shard = w_qkv.T
 
     def route(offset):
@@ -357,20 +426,23 @@
             (x - offset, yh, yh, z, c) if yl == c else (x - offset, 1 - yh, yh, z, c)
         )
 
-    near = [send(shard, route(offset)) for offset in OFFSETS]
     swap = lambda x, yh, c, z, yl: (x, yh, 1 - c, z, yl)
+    across = lambda x, yh, c, z, yl: (x, yh, c, z, 1 - yl)
+    near = [send(shard[HEAD:], route(o)) for o in OFFSETS]
+    other_frames = send(local_frames, across)
     far = [send(piece, swap) for piece in near]
-    slots = jnp.stack([2 * ((x + offset) % 4) + c for c in (core, 1 - core) for offset in OFFSETS])
-    parts = project_qkv(slots, local_frames, other_frames, attn_gain[None, :], near + far)
+    near_q = [send(shard[:HEAD], route(o)) for o in OFFSETS]
+    far_q = send(jnp.concatenate(near_q, axis=0), swap)
+    key_value, normed = project_key_value(me, local_frames, other_frames, attn_gain[None, :], near + far)
+    queries = project_query(me, normed, near_q + [far_q])
     groups = [[2 * z + yl for z in range(8)] for yl in range(2)]
-    parts = lax.all_to_all(parts, "blk", 0, 0, axis_index_groups=groups, tiled=True)
+    key_value = lax.all_to_all(key_value, "blk", 0, 0, axis_index_groups=groups, tiled=True)
+    queries = list(queries)
+    for d in SEND_ORDER:
+        queries[d] = send(queries[d], lambda x, yh, c, z, yl: (x, yh, c, z + d, yl))
     ends = jnp.cumsum(utt_lengths)
     starts = ends - utt_lengths
-    pad = (HEAD, HEAD - utt_lengths.shape[0])
-    sides = jnp.stack([yl, 1 - yl])
-    bases = jnp.concatenate([window_start + sides * frame_rows, sides])
-    lo, hi = jnp.pad(starts, pad)[None, :], jnp.pad(ends, pad)[None, :]
-    mixed = attend(bases, lo, hi, starts, ends, parts)
+    mixed = attend(me, starts, ends, key_value, queries)
     mixed = lax.all_to_all(mixed, "blk", 0, 0, tiled=True)
     residual, gated = gate(mixed, local_frames, conv_gain[None, :], w_out, w_glu)
 
@@ -383,7 +455,7 @@
 
     left = send(gated[frame_rows - RIM :], neighbour(1))
     right = send(gated[:RIM], neighbour(-1))
-    where = (first_frame[None], starts, ends)
+    where = (me, starts, ends)
     inner = convolve_inner(*where, gated, w_depth)
     result = finish_block(*where, inner, left, right, residual, w_depth, depth_gain[None, :], w_proj)
     return result[None]

time: 146 us -> 149 us (1.021)
  the two profiles are of different devices: /device:TPU:1 before, /device:TPU:2 now
where the time goes in v3:
time: 149 us
  starting transfers between devices  69.4 us (47%)
  Pallas kernels  40.6 us (27%)
  blocking collectives  21.2 us (14%)
  waiting for transfers between devices  10.6 us (7%)
  local copies, waits for them, and re-layouts  6.19 us (4%)
    ppermute x23, starting transfers between devices, send(): return lax.ppermute(value, ('blk', 'grp'), pairs)  60.8 us
    all_to_all x1, blocking collectives, body(): mixed = lax.all_to_all(mixed, 'blk', 0, 0, tiled=True)  21.2 us
    pallas_call x1, Pallas kernels, attend(): pl.pallas_call(attend_kernel, out_shape=jax.ShapeDtypeStruct((2 * sources...  19.1 us
    ppermute x23, waiting for transfers between devices, send(): return lax.ppermute(value, ('blk', 'grp'), pairs)  10.6 us
    all_to_all x1, starting transfers between devices, body(): lax.all_to_all(key_value, 'blk', 0, 0, axis_index_groups=groups, tiled=True)  8.61 us
    pallas_call x1, Pallas kernels, project_key_value(): pl.pallas_call(key_value_kernel, out_shape=[jax.ShapeDtypeStruct((8, 2 *...  6.66 us
    pallas_call x1, Pallas kernels, gate(): pl.pallas_call(gate_kernel, out_shape=[shape, shape], in_specs=[VMEM] * 3...  6.28 us
    pallas_call x1, Pallas kernels, convolve_inner(): pl.pallas_call(inner_kernel, out_shape=jax.ShapeDtypeStruct(gated.shape,...  3.6 us
  transfers between devices with their start and end apart: 24, of which 9 were waited for; matrix products, arithmetic and copies ran while one was open for 1% of the time, Pallas kernels for 4%

profile of v3, /device:TPU:2, one launch (start us, length us, event | category | flops | bytes accessed | tf_op | source)
XLA Modules:
  0.0 148.6 jit_solution(6820677143230484735)
XLA Ops:
  1.7 2.3 %collective-permute-start.2 = (bf16[128,1024]{1,0:T(8,128)(2,1)S(1)}, bf16[128,1024]{1,0:T(8,128)(2,1)S(1)}, u32[]{:S(2)}, u32[]{:S(2)}) collective-permute-start(bf16[128,1024]{1,0:T(8,128)(2,1)S(1)} %slice.22), channel_id=1, source_target_pairs={{0,12},{1,30},{2,15},{3,29},{4,0},{5,18},{6,3},{7,17},{8,4},{9,22}... | collective-permute-start | bytes 786440 | tf_op jit(solution)/shard_map/ppermute | solution.py:42
  4.0 3.1 %collective-permute-start.4 = (bf16[128,1024]{1,0:T(8,128)(2,1)S(1)}, bf16[128,1024]{1,0:T(8,128)(2,1)S(1)}, u32[]{:S(2)}, u32[]{:S(2)}) collective-permute-start(bf16[128,1024]{1,0:T(8,128)(2,1)S(1)} %slice.22), channel_id=1, source_target_pairs={{0,8},{1,26},{2,11},{3,25},{4,12},{5,30},{6,15},{7,29},{8,0},{9,18... | collective-permute-start | bytes 786440 | tf_op jit(solution)/shard_map/ppermute | solution.py:42
  7.1 3.5 %collective-permute-start = (bf16[256,1024]{1,0:T(8,128)(2,1)}, bf16[256,1024]{1,0:T(8,128)(2,1)S(1)}, u32[]{:S(2)}, u32[]{:S(2)}) collective-permute-start(bf16[256,1024]{1,0:T(8,128)(2,1)} %bitcast.19), channel_id=1, source_target_pairs={{0,16},{1,17},{2,18},{3,19},{4,20},{5,21},{6,22},{7,23},{8,24},{9,... | collective-permute-start | bytes 1572872 | tf_op jit(solution)/shard_map/ppermute | solution.py:42
  10.6 3.0 %collective-permute-start.5 = (bf16[128,1024]{1,0:T(8,128)(2,1)S(1)}, bf16[128,1024]{1,0:T(8,128)(2,1)S(1)}, u32[]{:S(2)}, u32[]{:S(2)}) collective-permute-start(bf16[128,1024]{1,0:T(8,128)(2,1)S(1)} %collective-permute-done.1.refs_0_), channel_id=1, source_target_pairs={{0,1},{1,0},{2,3},{3,2},{4,5},{5,4},{6,7},{7,6},{8,9},{9,8},{10,11... | collective-permute-start | bytes 786440 | tf_op jit(solution)/shard_map/ppermute | solution.py:42
  13.7 3.9 %collective-permute-start.6 = (bf16[128,1024]{1,0:T(8,128)(2,1)S(1)}, bf16[128,1024]{1,0:T(8,128)(2,1)S(1)}, u32[]{:S(2)}, u32[]{:S(2)}) collective-permute-start(bf16[128,1024]{1,0:T(8,128)(2,1)S(1)} %collective-permute-done.2.refs_1_), channel_id=1, source_target_pairs={{0,1},{1,0},{2,3},{3,2},{4,5},{5,4},{6,7},{7,6},{8,9},{9,8},{10,11... | collective-permute-start | bytes 786440 | tf_op jit(solution)/shard_map/ppermute | solution.py:42
  18.6 2.1 %collective-permute-start.8 = (bf16[128,1024]{1,0:T(8,128)(2,1)S(1)}, bf16[128,1024]{1,0:T(8,128)(2,1)S(1)}, u32[]{:S(2)}, u32[]{:S(2)}) collective-permute-start(bf16[128,1024]{1,0:T(8,128)(2,1)S(1)} %collective-permute-done.4.refs_3_), channel_id=1, source_target_pairs={{0,1},{1,0},{2,3},{3,2},{4,5},{5,4},{6,7},{7,6},{8,9},{9,8},{10,11... | collective-permute-start | bytes 786440 | tf_op jit(solution)/shard_map/ppermute | solution.py:42
  22.8 6.7 %shard_map.100 = (bf16[8,512,128]{2,1,0:T(8,128)(2,1)}, bf16[512,1024]{1,0:T(8,128)(2,1)}) custom-call(s32[6]{0:T(128)} %stack.27.me, bf16[256,1024]{1,0:T(8,128)(2,1)} %bitcast.20, f32[1,1024]{1,0:T(1,128)} %bitcast.24, bf16[256,1024]{1,0:T(8,128)(2,1)} %copy-done.7, bf16[128,1024]{1,0:T(8,128)(2,1)} %copy-done.8, bf16[128,1024]{1,0:T(8,128)(2,1)} %copy-done.9, ...), custom_call_target="tpu_custom_call" | custom-call | tf_op jit(solution)/shard_map/pallas_call | solution.py:116
  29.5 8.6 %all-to-all-start = ((bf16[8,512,128]{2,1,0:T(8,128)(2,1)}), bf16[8,512,128]{2,1,0:T(8,128)(2,1)S(1)}, u32[]{:S(2)}, u32[]{:S(2)}) async-start(bf16[8,512,128]{2,1,0:T(8,128)(2,1)} %get-tuple-element.17), calls=%async_computation | async-start | bytes 2097152 | tf_op jit(solution)/shard_map/all_to_all | solution.py:439
  39.0 1.9 %collective-permute-start.10 = (bf16[64,1024]{1,0:T(8,128)(2,1)S(1)}, bf16[64,1024]{1,0:T(8,128)(2,1)S(1)}, u32[]{:S(2)}, u32[]{:S(2)}) collective-permute-start(bf16[64,1024]{1,0:T(8,128)(2,1)S(1)} %slice.23), channel_id=1, source_target_pairs={{0,12},{1,30},{2,15},{3,29},{4,0},{5,18},{6,3},{7,17},{8,4},{9,22}... | collective-permute-start | bytes 393224 | tf_op jit(solution)/shard_map/ppermute | solution.py:42
  41.1 3.2 %collective-permute-start.12 = (bf16[64,1024]{1,0:T(8,128)(2,1)S(1)}, bf16[64,1024]{1,0:T(8,128)(2,1)S(1)}, u32[]{:S(2)}, u32[]{:S(2)}) collective-permute-start(bf16[64,1024]{1,0:T(8,128)(2,1)S(1)} %slice.23), channel_id=1, source_target_pairs={{0,8},{1,26},{2,11},{3,25},{4,12},{5,30},{6,15},{7,29},{8,0},{9,18... | collective-permute-start | bytes 393224 | tf_op jit(solution)/shard_map/ppermute | solution.py:42
  45.0 1.1 collective-permute-done.11.refs_2_
  46.1 1.6 %collective-permute-done.12.refs_3_ = bf16[64,1024]{1,0:T(8,128)(2,1)S(1)} collective-permute-done((bf16[64,1024]{1,0:T(8,128)(2,1)S(1)}, bf16[64,1024]{1,0:T(8,128)(2,1)S(1)}, u32[]{:S(2)}, u32[]{:S(2)}) %collective-permute-start.12) | collective-permute-done | bytes 131104 | tf_op jit(solution)/shard_map/ppermute | solution.py:42
  47.7 8.1 %collective-permute-start.13 = (bf16[256,1024]{1,0:T(8,128)(2,1)S(1)}, bf16[256,1024]{1,0:T(8,128)(2,1)S(1)}, u32[]{:S(2)}, u32[]{:S(2)}) collective-permute-start(bf16[256,1024]{1,0:T(8,128)(2,1)S(1)} %pad_maximum_fusion), channel_id=1, source_target_pairs={{0,1},{1,0},{2,3},{3,2},{4,5},{5,4},{6,7},{7,6},{8,9},{9,8},{10,11... | collective-permute-start | bytes 1572872 | tf_op jit(solution)/shard_map/ppermute | solution.py:42
  55.8 1.5 %collective-permute-done.13.refs_4_ = bf16[256,1024]{1,0:T(8,128)(2,1)S(1)} collective-permute-done((bf16[256,1024]{1,0:T(8,128)(2,1)S(1)}, bf16[256,1024]{1,0:T(8,128)(2,1)S(1)}, u32[]{:S(2)}, u32[]{:S(2)}) %collective-permute-start.13) | collective-permute-done | bytes 524320 | tf_op jit(solution)/shard_map/ppermute | solution.py:42
  57.4 2.1 %shard_map.101 = (bf16[256,128]{1,0:T(8,128)(2,1)S(1)}, bf16[256,128]{1,0:T(8,128)(2,1)S(1)}, bf16[256,128]{1,0:T(8,128)(2,1)S(1)}, bf16[256,128]{1,0:T(8,128)(2...) custom-call(s32[6]{0:T(128)S(1)} %copy-done.5, ...), custom_call_target="tpu_custom_call" | custom-call | tf_op jit(solution)/shard_map/pallas_call | solution.py:150
  59.5 2.1 %collective-permute-start.14 = (bf16[256,128]{1,0:T(8,128)(2,1)S(1)}, bf16[256,128]{1,0:T(8,128)(2,1)S(1)}, u32[]{:S(2)}, u32[]{:S(2)}) collective-permute-start(bf16[256,128]{1,0:T(8,128)(2,1)S(1)} %get-tuple-element.20), channel_id=1, source_target_pairs={{0,32},{1,33},{2,34},{3,35},{4,36},{5,37},{6,38},{7,39},{8,40},{9,... | collective-permute-start | bytes 196616 | tf_op jit(solution)/shard_map/ppermute | solution.py:42
  61.6 2.4 %collective-permute-start.15 = (bf16[256,128]{1,0:T(8,128)(2,1)S(1)}, bf16[256,128]{1,0:T(8,128)(2,1)S(1)}, u32[]{:S(2)}, u32[]{:S(2)}) collective-permute-start(bf16[256,128]{1,0:T(8,128)(2,1)S(1)} %get-tuple-element.21), channel_id=1, source_target_pairs={{0,64},{1,65},{2,66},{3,67},{4,68},{5,69},{6,70},{7,71},{8,72},{9,... | collective-permute-start | bytes 196616 | tf_op jit(solution)/shard_map/ppermute | solution.py:42
  64.1 2.7 %collective-permute-start.16 = (bf16[256,128]{1,0:T(8,128)(2,1)S(1)}, bf16[256,128]{1,0:T(8,128)(2,1)S(1)}, u32[]{:S(2)}, u32[]{:S(2)}) collective-permute-start(bf16[256,128]{1,0:T(8,128)(2,1)S(1)} %get-tuple-element.22), channel_id=1, source_target_pairs={{0,96},{1,97},{2,98},{3,99},{4,100},{5,101},{6,102},{7,103},{8,104... | collective-permute-start | bytes 196616 | tf_op jit(solution)/shard_map/ppermute | solution.py:42
  66.8 2.3 %collective-permute-start.17 = (bf16[256,128]{1,0:T(8,128)(2,1)S(1)}, bf16[256,128]{1,0:T(8,128)(2,1)S(1)}, u32[]{:S(2)}, u32[]{:S(2)}) collective-permute-start(bf16[256,128]{1,0:T(8,128)(2,1)S(1)} %get-tuple-element.23), channel_id=1, source_target_pairs={{0,128},{1,129},{2,130},{3,131},{4,132},{5,133},{6,134},{7,135},{8... | collective-permute-start | bytes 196616 | tf_op jit(solution)/shard_map/ppermute | solution.py:42
  69.1 2.8 %collective-permute-start.18 = (bf16[256,128]{1,0:T(8,128)(2,1)S(1)}, bf16[256,128]{1,0:T(8,128)(2,1)S(1)}, u32[]{:S(2)}, u32[]{:S(2)}) collective-permute-start(bf16[256,128]{1,0:T(8,128)(2,1)S(1)} %get-tuple-element.24), channel_id=1, source_target_pairs={{0,160},{1,161},{2,162},{3,163},{4,164},{5,165},{6,166},{7,167},{8... | collective-permute-start | bytes 196616 | tf_op jit(solution)/shard_map/ppermute | solution.py:42
  71.9 3.3 %collective-permute-start.19 = (bf16[256,128]{1,0:T(8,128)(2,1)S(1)}, bf16[256,128]{1,0:T(8,128)(2,1)S(1)}, u32[]{:S(2)}, u32[]{:S(2)}) collective-permute-start(bf16[256,128]{1,0:T(8,128)(2,1)S(1)} %get-tuple-element.25), channel_id=1, source_target_pairs={{0,192},{1,193},{2,194},{3,195},{4,196},{5,197},{6,198},{7,199},{8... | collective-permute-start | bytes 196616 | tf_op jit(solution)/shard_map/ppermute | solution.py:42
  75.1 1.8 %collective-permute-start.20 = (bf16[256,128]{1,0:T(8,128)(2,1)S(1)}, bf16[256,128]{1,0:T(8,128)(2,1)S(1)}, u32[]{:S(2)}, u32[]{:S(2)}) collective-permute-start(bf16[256,128]{1,0:T(8,128)(2,1)S(1)} %get-tuple-element.26), channel_id=1, source_target_pairs={{0,224},{1,225},{2,226},{3,227},{4,228},{5,229},{6,230},{7,231},{8... | collective-permute-start | bytes 196616 | tf_op jit(solution)/shard_map/ppermute | solution.py:42
  77.4 1.1 collective-permute-done.17.refs_4_
  78.5 2.4 %collective-permute-done.18.refs_5_ = bf16[256,128]{1,0:T(8,128)(2,1)S(1)} collective-permute-done((bf16[256,128]{1,0:T(8,128)(2,1)S(1)}, bf16[256,128]{1,0:T(8,128)(2,1)S(1)}, u32[]{:S(2)}, u32[]{:S(2)}) %collective-permute-start.18) | collective-permute-done | bytes 65568 | tf_op jit(solution)/shard_map/ppermute | solution.py:42
  80.9 1.5 collective-permute-done.19.refs_6_
  82.6 19.1 %shard_map.102 = bf16[16,64,256]{2,1,0:T(8,128)(2,1)S(1)} custom-call(s32[6]{0:T(128)S(1)} %copy-done.5, s32[8]{0:T(128)S(1)} %bitcast_subtract_fusion.start_ref, s32[8]{0:T(128)S(1)} %bitcast.15, bf16[8,512,128]{2,1,0:T(8,128)(2,1)S(1)} %all-to-all-done.in_ref, bf16[256,128]{1,0:T(8,128)(2,1)S(1)} %get-tuple-element.19.refs_0_, ...), custom_call_target="tpu_custom_call" | custom-call | tf_op jit(solution)/shard_map/pallas_call | solution.py:246
  101.7 21.2 %all_to_all.10.mixed = bf16[16,64,256]{2,1,0:T(8,128)(2,1)} all-to-all(bf16[16,64,256]{2,1,0:T(8,128)(2,1)S(1)} %shard_map.102), channel_id=1, replica_groups=mesh['blk'=16,'grp'=16] {'blk'}, dimensions={0} | all-to-all | bytes 1048576 | tf_op jit(solution)/shard_map/all_to_all | solution.py:446
  122.9 6.3 %shard_map.103 = (bf16[256,1024]{1,0:T(8,128)(2,1)}, bf16[256,1024]{1,0:T(8,128)(2,1)}) custom-call(bf16[16,64,256]{2,1,0:T(8,128)(2,1)} %all_to_all.10.mixed, bf16[256,1024]{1,0:T(8,128)(2,1)} %bitcast.21, f32[1,1024]{1,0:T(1,128)} %bitcast.25, bf16[1024,1024]{1,0:T(8,128)(2,1)} %w_out_hbm.1, bf16[1024,2048]{1,0:T(8,128)(2,1)} %w_glu_hbm.1), custom_call_target="tpu_custom_call" | custom-call | tf_op jit(solution)/shard_map/pallas_call | solution.py:288
  130.0 2.4 %collective-permute-start.21 = (bf16[16,1024]{1,0:T(8,128)(2,1)S(1)}, bf16[16,1024]{1,0:T(8,128)(2,1)S(1)}, u32[]{:S(2)}, u32[]{:S(2)}) collective-permute-start(bf16[16,1024]{1,0:T(8,128)(2,1)S(1)} %get-tuple-element.30), channel_id=1, source_target_pairs={{0,16},{1,17},{2,18},{3,19},{4,20},{5,21},{6,22},{7,23},{8,24},{9,... | collective-permute-start | bytes 98312 | tf_op jit(solution)/shard_map/ppermute | solution.py:42
  132.4 7.3 %collective-permute-start.22 = (bf16[16,1024]{1,0:T(8,128)(2,1)S(1)}, bf16[16,1024]{1,0:T(8,128)(2,1)S(1)}, u32[]{:S(2)}, u32[]{:S(2)}) collective-permute-start(bf16[16,1024]{1,0:T(8,128)(2,1)S(1)} %get-tuple-element.29), channel_id=1, source_target_pairs={{1,240},{2,241},{3,242},{4,243},{5,244},{6,245},{7,246},{8,247},{9... | collective-permute-start | bytes 98312 | tf_op jit(solution)/shard_map/ppermute | solution.py:42
  140.8 3.6 %shard_map.104.inner = f32[256,1024]{1,0:T(8,128)S(1)} custom-call(s32[6]{0:T(128)S(1)} %copy-done.5, s32[8]{0:T(128)S(1)} %bitcast_subtract_fusion.start_ref, s32[8]{0:T(128)S(1)} %bitcast.16, bf16[256,1024]{1,0:T(8,128)(2,1)S(1)} %copy-done.2, f32[31,1024]{1,0:T(8,128)S(1)} %copy-done.4), custom_call_target="tpu_custom_call" | custom-call | tf_op jit(solution)/shard_map/pallas_call | solution.py:353
  145.5 2.9 %shard_map.105 = bf16[256,1024]{1,0:T(8,128)(2,1)} custom-call(s32[6]{0:T(128)S(1)} %copy-done.5, s32[8]{0:T(128)S(1)} %bitcast_subtract_fusion.start_ref, s32[8]{0:T(128)S(1)} %bitcast.17, f32[256,1024]{1,0:T(8,128)S(1)} %shard_map.104.inner, bf16[16,1024]{1,0:T(8,128)(2,1)S(1)} %collective-permute-done.21.left, ...), custom_call_target="tpu_custom_call" | custom-call | tf_op jit(solution)/shard_map/pallas_call | solution.py:394
  (64 shorter events, 10.3 us)
Async XLA Ops:
  1.0 9.7 %collective-permute-start.1 = (bf16[128,1024]{1,0:T(8,128)(2,1)S(1)}, bf16[128,1024]{1,0:T(8,128)(2,1)S(1)}, u32[]{:S(2)}, u32[]{:S(2)}) collective-permute-start(bf16[128,1024]{1,0:T(8,128)(2,1)S(1)} %slice.22), channel_id=1, source_target_pairs={{0,0},{1,18},{2,3},{3,17},{4,4},{5,22},{6,7},{7,21},{8,8},{9,26},{... | collective-permute-start | bytes 786440 | tf_op jit(solution)/shard_map/ppermute | solution.py:42
  1.7 12.0 %collective-permute-start.2 = (bf16[128,1024]{1,0:T(8,128)(2,1)S(1)}, bf16[128,1024]{1,0:T(8,128)(2,1)S(1)}, u32[]{:S(2)}, u32[]{:S(2)}) collective-permute-start(bf16[128,1024]{1,0:T(8,128)(2,1)S(1)} %slice.22), channel_id=1, source_target_pairs={{0,12},{1,30},{2,15},{3,29},{4,0},{5,18},{6,3},{7,17},{8,4},{9,22}... | collective-permute-start | bytes 786440 | tf_op jit(solution)/shard_map/ppermute | solution.py:42
  4.0 13.6 %collective-permute-start.3 = (bf16[128,1024]{1,0:T(8,128)(2,1)S(1)}, bf16[128,1024]{1,0:T(8,128)(2,1)S(1)}, u32[]{:S(2)}, u32[]{:S(2)}) collective-permute-start(bf16[128,1024]{1,0:T(8,128)(2,1)S(1)} %slice.22), channel_id=1, source_target_pairs={{0,4},{1,22},{2,7},{3,21},{4,8},{5,26},{6,11},{7,25},{8,12},{9,30}... | collective-permute-start | bytes 786440 | tf_op jit(solution)/shard_map/ppermute | solution.py:42
  4.0 14.6 %collective-permute-start.4 = (bf16[128,1024]{1,0:T(8,128)(2,1)S(1)}, bf16[128,1024]{1,0:T(8,128)(2,1)S(1)}, u32[]{:S(2)}, u32[]{:S(2)}) collective-permute-start(bf16[128,1024]{1,0:T(8,128)(2,1)S(1)} %slice.22), channel_id=1, source_target_pairs={{0,8},{1,26},{2,11},{3,25},{4,12},{5,30},{6,15},{7,29},{8,0},{9,18... | collective-permute-start | bytes 786440 | tf_op jit(solution)/shard_map/ppermute | solution.py:42
  7.1 14.8 %collective-permute-start = (bf16[256,1024]{1,0:T(8,128)(2,1)}, bf16[256,1024]{1,0:T(8,128)(2,1)S(1)}, u32[]{:S(2)}, u32[]{:S(2)}) collective-permute-start(bf16[256,1024]{1,0:T(8,128)(2,1)} %bitcast.19), channel_id=1, source_target_pairs={{0,16},{1,17},{2,18},{3,19},{4,20},{5,21},{6,22},{7,23},{8,24},{9,... | collective-permute-start | bytes 1572872 | tf_op jit(solution)/shard_map/ppermute | solution.py:42
  10.6 11.3 %copy-start.8 = (bf16[128,1024]{1,0:T(8,128)(2,1)}, bf16[128,1024]{1,0:T(8,128)(2,1)S(1)}, u32[]{:S(2)}) copy-start(bf16[128,1024]{1,0:T(8,128)(2,1)S(1)} %collective-permute-done.1.refs_0_) | copy-start | bytes 786436
  10.6 10.7 %collective-permute-start.5 = (bf16[128,1024]{1,0:T(8,128)(2,1)S(1)}, bf16[128,1024]{1,0:T(8,128)(2,1)S(1)}, u32[]{:S(2)}, u32[]{:S(2)}) collective-permute-start(bf16[128,1024]{1,0:T(8,128)(2,1)S(1)} %collective-permute-done.1.refs_0_), channel_id=1, source_target_pairs={{0,1},{1,0},{2,3},{3,2},{4,5},{5,4},{6,7},{7,6},{8,9},{9,8},{10,11... | collective-permute-start | bytes 786440 | tf_op jit(solution)/shard_map/ppermute | solution.py:42
  13.7 8.2 %copy-start.9 = (bf16[128,1024]{1,0:T(8,128)(2,1)}, bf16[128,1024]{1,0:T(8,128)(2,1)S(1)}, u32[]{:S(2)}) copy-start(bf16[128,1024]{1,0:T(8,128)(2,1)S(1)} %collective-permute-done.2.refs_1_) | copy-start | bytes 786436
  13.7 7.6 %collective-permute-start.6 = (bf16[128,1024]{1,0:T(8,128)(2,1)S(1)}, bf16[128,1024]{1,0:T(8,128)(2,1)S(1)}, u32[]{:S(2)}, u32[]{:S(2)}) collective-permute-start(bf16[128,1024]{1,0:T(8,128)(2,1)S(1)} %collective-permute-done.2.refs_1_), channel_id=1, source_target_pairs={{0,1},{1,0},{2,3},{3,2},{4,5},{5,4},{6,7},{7,6},{8,9},{9,8},{10,11... | collective-permute-start | bytes 786440 | tf_op jit(solution)/shard_map/ppermute | solution.py:42
  17.6 3.7 %collective-permute-start.7 = (bf16[128,1024]{1,0:T(8,128)(2,1)S(1)}, bf16[128,1024]{1,0:T(8,128)(2,1)S(1)}, u32[]{:S(2)}, u32[]{:S(2)}) collective-permute-start(bf16[128,1024]{1,0:T(8,128)(2,1)S(1)} %collective-permute-done.3.refs_2_), channel_id=1, source_target_pairs={{0,1},{1,0},{2,3},{3,2},{4,5},{5,4},{6,7},{7,6},{8,9},{9,8},{10,11... | collective-permute-start | bytes 786440 | tf_op jit(solution)/shard_map/ppermute | solution.py:42
  18.6 3.3 %collective-permute-start.8 = (bf16[128,1024]{1,0:T(8,128)(2,1)S(1)}, bf16[128,1024]{1,0:T(8,128)(2,1)S(1)}, u32[]{:S(2)}, u32[]{:S(2)}) collective-permute-start(bf16[128,1024]{1,0:T(8,128)(2,1)S(1)} %collective-permute-done.4.refs_3_), channel_id=1, source_target_pairs={{0,1},{1,0},{2,3},{3,2},{4,5},{5,4},{6,7},{7,6},{8,9},{9,8},{10,11... | collective-permute-start | bytes 786440 | tf_op jit(solution)/shard_map/ppermute | solution.py:42
  29.4 27.9 %copy-start.1 = (bf16[512,1024]{1,0:T(8,128)(2,1)S(1)}, bf16[512,1024]{1,0:T(8,128)(2,1)}, u32[]{:S(2)}) copy-start(bf16[512,1024]{1,0:T(8,128)(2,1)} %get-tuple-element.18.normed) | copy-start | bytes 3145732
  29.5 27.9 %copy-start.5 = (s32[6]{0:T(128)S(1)}, s32[6]{0:T(128)}, u32[]{:S(2)}) copy-start(s32[6]{0:T(128)} %stack.27.me) | copy-start | bytes 76
  29.5 53.2 %all-to-all-start = ((bf16[8,512,128]{2,1,0:T(8,128)(2,1)}), bf16[8,512,128]{2,1,0:T(8,128)(2,1)S(1)}, u32[]{:S(2)}, u32[]{:S(2)}) async-start(bf16[8,512,128]{2,1,0:T(8,128)(2,1)} %get-tuple-element.17), calls=%async_computation | async-start | bytes 2097152 | tf_op jit(solution)/shard_map/all_to_all | solution.py:439
  38.1 25.9 %copy-start.16 = (s32[8]{0:T(128)S(1)}, s32[8]{0:T(128)}, u32[]{:S(2)}) copy-start(s32[8]{0:T(128)} %param.11) | copy-start | bytes 100
  39.0 6.0 %collective-permute-start.10 = (bf16[64,1024]{1,0:T(8,128)(2,1)S(1)}, bf16[64,1024]{1,0:T(8,128)(2,1)S(1)}, u32[]{:S(2)}, u32[]{:S(2)}) collective-permute-start(bf16[64,1024]{1,0:T(8,128)(2,1)S(1)} %slice.23), channel_id=1, source_target_pairs={{0,12},{1,30},{2,15},{3,29},{4,0},{5,18},{6,3},{7,17},{8,4},{9,22}... | collective-permute-start | bytes 393224 | tf_op jit(solution)/shard_map/ppermute | solution.py:42
  40.9 5.1 %collective-permute-start.11 = (bf16[64,1024]{1,0:T(8,128)(2,1)S(1)}, bf16[64,1024]{1,0:T(8,128)(2,1)S(1)}, u32[]{:S(2)}, u32[]{:S(2)}) collective-permute-start(bf16[64,1024]{1,0:T(8,128)(2,1)S(1)} %slice.23), channel_id=1, source_target_pairs={{0,4},{1,22},{2,7},{3,21},{4,8},{5,26},{6,11},{7,25},{8,12},{9,30}... | collective-permute-start | bytes 393224 | tf_op jit(solution)/shard_map/ppermute | solution.py:42
  41.1 6.6 %collective-permute-start.12 = (bf16[64,1024]{1,0:T(8,128)(2,1)S(1)}, bf16[64,1024]{1,0:T(8,128)(2,1)S(1)}, u32[]{:S(2)}, u32[]{:S(2)}) collective-permute-start(bf16[64,1024]{1,0:T(8,128)(2,1)S(1)} %slice.23), channel_id=1, source_target_pairs={{0,8},{1,26},{2,11},{3,25},{4,12},{5,30},{6,15},{7,29},{8,0},{9,18... | collective-permute-start | bytes 393224 | tf_op jit(solution)/shard_map/ppermute | solution.py:42
  44.3 3.4 %collective-permute-start.9 = (bf16[64,1024]{1,0:T(8,128)(2,1)S(1)}, bf16[64,1024]{1,0:T(8,128)(2,1)S(1)}, u32[]{:S(2)}, u32[]{:S(2)}) collective-permute-start(bf16[64,1024]{1,0:T(8,128)(2,1)S(1)} %slice.23), channel_id=1, source_target_pairs={{0,0},{1,18},{2,3},{3,17},{4,4},{5,22},{6,7},{7,21},{8,8},{9,26},{... | collective-permute-start | bytes 393224 | tf_op jit(solution)/shard_map/ppermute | solution.py:42
  47.7 9.6 %collective-permute-start.13 = (bf16[256,1024]{1,0:T(8,128)(2,1)S(1)}, bf16[256,1024]{1,0:T(8,128)(2,1)S(1)}, u32[]{:S(2)}, u32[]{:S(2)}) collective-permute-start(bf16[256,1024]{1,0:T(8,128)(2,1)S(1)} %pad_maximum_fusion), channel_id=1, source_target_pairs={{0,1},{1,0},{2,3},{3,2},{4,5},{5,4},{6,7},{7,6},{8,9},{9,8},{10,11... | collective-permute-start | bytes 1572872 | tf_op jit(solution)/shard_map/ppermute | solution.py:42
  59.5 12.4 %collective-permute-start.14 = (bf16[256,128]{1,0:T(8,128)(2,1)S(1)}, bf16[256,128]{1,0:T(8,128)(2,1)S(1)}, u32[]{:S(2)}, u32[]{:S(2)}) collective-permute-start(bf16[256,128]{1,0:T(8,128)(2,1)S(1)} %get-tuple-element.20), channel_id=1, source_target_pairs={{0,32},{1,33},{2,34},{3,35},{4,36},{5,37},{6,38},{7,39},{8,40},{9,... | collective-permute-start | bytes 196616 | tf_op jit(solution)/shard_map/ppermute | solution.py:42
  61.6 13.6 %collective-permute-start.15 = (bf16[256,128]{1,0:T(8,128)(2,1)S(1)}, bf16[256,128]{1,0:T(8,128)(2,1)S(1)}, u32[]{:S(2)}, u32[]{:S(2)}) collective-permute-start(bf16[256,128]{1,0:T(8,128)(2,1)S(1)} %get-tuple-element.21), channel_id=1, source_target_pairs={{0,64},{1,65},{2,66},{3,67},{4,68},{5,69},{6,70},{7,71},{8,72},{9,... | collective-permute-start | bytes 196616 | tf_op jit(solution)/shard_map/ppermute | solution.py:42
  64.1 13.2 %collective-permute-start.16 = (bf16[256,128]{1,0:T(8,128)(2,1)S(1)}, bf16[256,128]{1,0:T(8,128)(2,1)S(1)}, u32[]{:S(2)}, u32[]{:S(2)}) collective-permute-start(bf16[256,128]{1,0:T(8,128)(2,1)S(1)} %get-tuple-element.22), channel_id=1, source_target_pairs={{0,96},{1,97},{2,98},{3,99},{4,100},{5,101},{6,102},{7,103},{8,104... | collective-permute-start | bytes 196616 | tf_op jit(solution)/shard_map/ppermute | solution.py:42
  66.8 11.7 %collective-permute-start.17 = (bf16[256,128]{1,0:T(8,128)(2,1)S(1)}, bf16[256,128]{1,0:T(8,128)(2,1)S(1)}, u32[]{:S(2)}, u32[]{:S(2)}) collective-permute-start(bf16[256,128]{1,0:T(8,128)(2,1)S(1)} %get-tuple-element.23), channel_id=1, source_target_pairs={{0,128},{1,129},{2,130},{3,131},{4,132},{5,133},{6,134},{7,135},{8... | collective-permute-start | bytes 196616 | tf_op jit(solution)/shard_map/ppermute | solution.py:42
  69.1 11.8 %collective-permute-start.18 = (bf16[256,128]{1,0:T(8,128)(2,1)S(1)}, bf16[256,128]{1,0:T(8,128)(2,1)S(1)}, u32[]{:S(2)}, u32[]{:S(2)}) collective-permute-start(bf16[256,128]{1,0:T(8,128)(2,1)S(1)} %get-tuple-element.24), channel_id=1, source_target_pairs={{0,160},{1,161},{2,162},{3,163},{4,164},{5,165},{6,166},{7,167},{8... | collective-permute-start | bytes 196616 | tf_op jit(solution)/shard_map/ppermute | solution.py:42
  71.9 10.5 %collective-permute-start.19 = (bf16[256,128]{1,0:T(8,128)(2,1)S(1)}, bf16[256,128]{1,0:T(8,128)(2,1)S(1)}, u32[]{:S(2)}, u32[]{:S(2)}) collective-permute-start(bf16[256,128]{1,0:T(8,128)(2,1)S(1)} %get-tuple-element.25), channel_id=1, source_target_pairs={{0,192},{1,193},{2,194},{3,195},{4,196},{5,197},{6,198},{7,199},{8... | collective-permute-start | bytes 196616 | tf_op jit(solution)/shard_map/ppermute | solution.py:42
  75.1 7.5 %collective-permute-start.20 = (bf16[256,128]{1,0:T(8,128)(2,1)S(1)}, bf16[256,128]{1,0:T(8,128)(2,1)S(1)}, u32[]{:S(2)}, u32[]{:S(2)}) collective-permute-start(bf16[256,128]{1,0:T(8,128)(2,1)S(1)} %get-tuple-element.26), channel_id=1, source_target_pairs={{0,224},{1,225},{2,226},{3,227},{4,228},{5,229},{6,230},{7,231},{8... | collective-permute-start | bytes 196616 | tf_op jit(solution)/shard_map/ppermute | solution.py:42
  122.9 16.9 %copy-start.4 = (f32[31,1024]{1,0:T(8,128)S(1)}, f32[31,1024]{1,0:T(8,128)}, u32[]{:S(2)}) copy-start(f32[31,1024]{1,0:T(8,128)} %weights.3) | copy-start | bytes 380932
  122.9 21.5 %copy-start = (bf16[1024,1024]{1,0:T(8,128)(2,1)S(1)}, bf16[1024,1024]{1,0:T(8,128)(2,1)}, u32[]{:S(2)}) copy-start(bf16[1024,1024]{1,0:T(8,128)(2,1)} %w_proj_hbm.1) | copy-start | bytes 6291460
  122.9 21.6 %copy-start.6 = (f32[1024]{0:T(1024)S(1)}, f32[1024]{0:T(1024)}, u32[]{:S(2)}) copy-start(f32[1024]{0:T(1024)} %param.18) | copy-start | bytes 12292
  130.0 14.4 %collective-permute-start.21 = (bf16[16,1024]{1,0:T(8,128)(2,1)S(1)}, bf16[16,1024]{1,0:T(8,128)(2,1)S(1)}, u32[]{:S(2)}, u32[]{:S(2)}) collective-permute-start(bf16[16,1024]{1,0:T(8,128)(2,1)S(1)} %get-tuple-element.30), channel_id=1, source_target_pairs={{0,16},{1,17},{2,18},{3,19},{4,20},{5,21},{6,22},{7,23},{8,24},{9,... | collective-permute-start | bytes 98312 | tf_op jit(solution)/shard_map/ppermute | solution.py:42
  132.4 12.0 %collective-permute-start.22 = (bf16[16,1024]{1,0:T(8,128)(2,1)S(1)}, bf16[16,1024]{1,0:T(8,128)(2,1)S(1)}, u32[]{:S(2)}, u32[]{:S(2)}) collective-permute-start(bf16[16,1024]{1,0:T(8,128)(2,1)S(1)} %get-tuple-element.29), channel_id=1, source_target_pairs={{1,240},{2,241},{3,242},{4,243},{5,244},{6,245},{7,246},{8,247},{9... | collective-permute-start | bytes 98312 | tf_op jit(solution)/shard_map/ppermute | solution.py:42
  (9 other events, 13.7 us)

commit v4 on v3

--- a/solution.py
+++ b/solution.py
@@ -1,3 +1,5 @@
+import functools
+
 import jax
 import jax.numpy as jnp
 from jax import lax
@@ -12,7 +14,8 @@
 RIM = 16
 ROWS = 16
 OFFSETS = (0, 1, 3, 2)
-SEND_ORDER = (4, 3, 5, 2, 6, 1, 7)
+SEND_ORDER = (1, 7, 2, 6, 3, 5, 4)
+PIECES = ((0, 1, 7, 2), (6, 3, 5, 4))
 LOG2E = 1.4426950408889634
 
 epsilon = 1e-05
@@ -80,89 +83,68 @@
         out[index, at : at + HEAD] = flipped[:, j * LANES : (j + 1) * LANES].astype(jnp.bfloat16)
 
 
-def key_value_kernel(me, own_hbm, gain_hbm, other_hbm, *refs):
-    shards_hbm, out, normed = refs[:8], refs[8], refs[9]
-    own_ref, gain_ref, other_ref, shards, sems = refs[10:]
-    pairs = [(own_hbm, own_ref), (gain_hbm, gain_ref), (other_hbm, other_ref)]
-    pairs += [(shards_hbm[i], shards.at[i]) for i in range(8)]
-    copies = [pltpu.make_async_copy(a, b, sems.at[i]) for i, (a, b) in enumerate(pairs)]
+def project_kernel(me, own_hbm, other_ref, gain_hbm, *refs):
+    shards, out, pieces = refs[:8], refs[8], refs[9:17]
+    normed, staged, own_ref, gain_ref, sems, in_sems = refs[17:]
+    pairs = ((gain_hbm, gain_ref), (own_hbm, own_ref))
+    copies = [pltpu.make_async_copy(a, b, in_sems.at[i]) for i, (a, b) in enumerate(pairs)]
     for copy in copies:
         copy.start()
-    copies[1].wait()
+    copies[0].wait()
     rows = own_ref.shape[0]
     gain = gain_ref[0:1, :]
-    copies[0].wait()
+    normed[rows:] = normalize(other_ref[...].astype(jnp.float32), gain).astype(jnp.bfloat16)
+    copies[1].wait()
     normed[:rows] = normalize(own_ref[...].astype(jnp.float32), gain).astype(jnp.bfloat16)
-    copies[2].wait()
-    normed[rows:] = normalize(other_ref[...].astype(jnp.float32), gain).astype(jnp.bfloat16)
     low = low_lanes(rows)
     for i in range(0, 8, 2):
-        copies[3 + i].wait()
-        copies[4 + i].wait()
         heads = shard_head(me, i), shard_head(me, i + 1)
-        weights = jnp.concatenate([shards[i, :HEAD], shards[i + 1, :HEAD]], axis=0)
+        weights = jnp.concatenate([shards[j][HEAD : 2 * HEAD, :] for j in (i, i + 1)], axis=0)
         both = lax.dot_general(normed[...], weights, CONTRACT, preferred_element_type=jnp.float32)
         own, other = both[:rows], both[rows:]
         out[heads[0], :rows] = jnp.where(low, own, swap_lanes(other)).astype(jnp.bfloat16)
         out[heads[1], :rows] = jnp.where(low, swap_lanes(own), other).astype(jnp.bfloat16)
-        weights = jnp.concatenate([shards[i, HEAD:], shards[i + 1, HEAD:]], axis=0)
-        both = lax.dot_general(weights, normed[...], CONTRACT, preferred_element_type=jnp.float32)
-        transposed(out, heads[0], rows, both[:HEAD])
-        transposed(out, heads[1], rows, both[HEAD:])
-
-
-def project_key_value(me, own, other, gain, shards):
+        for j, head in zip((i, i + 1), heads):
+            weights = jnp.concatenate([shards[j][2 * HEAD :, :], shards[j][:HEAD, :]], axis=0)
+            both = lax.dot_general(weights, normed[...], CONTRACT, preferred_element_type=jnp.float32)
+            transposed(out, head, rows, both[:HEAD])
+            query = both[HEAD:] * (HEAD**-0.5 * LOG2E)
+            transposed(staged, lax.rem(head + 8 - me[Z], 8), 0, query)
+    copies = [pltpu.make_async_copy(staged.at[d], pieces[d], sems.at[d]) for d in range(8)]
+    for copy in copies:
+        copy.start()
+    for copy in copies:
+        copy.wait()
+
+
+def project_qkv(me, own, other, gain, shards):
     rows, width = own.shape
+    piece = jax.ShapeDtypeStruct((rows, LANES), jnp.bfloat16)
     return pl.pallas_call(
-        key_value_kernel,
-        out_shape=[
-            jax.ShapeDtypeStruct((8, 2 * rows, LANES), jnp.bfloat16),
-            jax.ShapeDtypeStruct((2 * rows, width), jnp.bfloat16),
-        ],
-        in_specs=[SMEM] + [HBM] * 11,
-        out_specs=[VMEM] * 2,
+        project_kernel,
+        out_shape=[jax.ShapeDtypeStruct((8, 2 * rows, LANES), jnp.bfloat16)] + [piece] * 8,
+        in_specs=[SMEM, HBM, VMEM, HBM] + [VMEM] * 8,
+        out_specs=[VMEM] + [HBM] * 8,
         scratch_shapes=[
+            pltpu.VMEM((2 * rows, width), jnp.bfloat16),
+            pltpu.VMEM((8,) + piece.shape, jnp.bfloat16),
             pltpu.VMEM(own.shape, jnp.bfloat16),
             pltpu.VMEM(gain.shape, jnp.float32),
-            pltpu.VMEM(own.shape, jnp.bfloat16),
-            pltpu.VMEM((8,) + shards[0].shape, jnp.bfloat16),
-            pltpu.SemaphoreType.DMA((11,)),
+            pltpu.SemaphoreType.DMA((8,)),
+            pltpu.SemaphoreType.DMA((2,)),
         ],
-        compiler_params=pltpu.CompilerParams(vmem_limit_bytes=60 * 1024 * 1024),
-    )(me, own, gain, other, *shards)
-
-
-def query_kernel(me, normed, *refs):
-    near, far, outs, staged = refs[:4], refs[4], refs[5:13], refs[13]
-    shards = [ref[...] for ref in near] + [far[i * HEAD : (i + 1) * HEAD, :] for i in range(4)]
-    for i in range(0, 8, 2):
-        weights = jnp.concatenate([shards[i], shards[i + 1]], axis=0)
-        both = lax.dot_general(weights, normed[...], CONTRACT, preferred_element_type=jnp.float32)
-        both = both * (HEAD**-0.5 * LOG2E)
-        transposed(staged, lax.rem(shard_head(me, i) + 8 - me[Z], 8), 0, both[:HEAD])
-        transposed(staged, lax.rem(shard_head(me, i + 1) + 8 - me[Z], 8), 0, both[HEAD:])
-    for d in range(8):
-        outs[d][...] = staged[d]
-
-
-def project_query(me, normed, shards):
-    shape = (normed.shape[0] // 2, LANES)
-    return pl.pallas_call(
-        query_kernel,
-        out_shape=[jax.ShapeDtypeStruct(shape, jnp.bfloat16)] * 8,
-        in_specs=[SMEM] + [VMEM] * 6,
-        out_specs=[VMEM] * 8,
-        scratch_shapes=[pltpu.VMEM((8,) + shape, jnp.bfloat16)],
-        compiler_params=pltpu.CompilerParams(vmem_limit_bytes=16 * 1024 * 1024),
-    )(me, normed, *shards)
-
-
-def attend_kernel(me, start_ref, end_ref, in_ref, *refs):
-    parts_hbm, out_ref = refs[:8], refs[8]
-    keys, values, queries, scores, most_ref, parts_q, sems = refs[9:]
-    copies = [pltpu.make_async_copy(parts_hbm[d], parts_q.at[d], sems.at[d]) for d in range(8)]
+        compiler_params=pltpu.CompilerParams(vmem_limit_bytes=59 * 1024 * 1024),
+    )(me, own, other, gain, *shards)
+
+
+def attend_kernel(pieces, me, start_ref, end_ref, in_ref, before, *refs):
+    count = len(pieces)
+    parts_hbm, out_ref = refs[:count], refs[count]
+    keys, values, queries, scores, most_ref, parts_q, sems = refs[count + 1 :]
+    copies = [pltpu.make_async_copy(parts_hbm[d], parts_q.at[d], sems.at[d]) for d in range(count)]
     for copy in copies:
         copy.start()
+    out_ref[...] = before[...]
     sources = in_ref.shape[0]
     block = in_ref.shape[1] // 2
     low = low_lanes(block)
@@ -189,11 +171,13 @@
         return carry
 
     def origin(i):
-        d, side = i // 2, lax.rem(i, 2)
+        side, d = lax.rem(i, 2), pieces[0]
+        for j in range(1, count):
+            d = jnp.where(i // 2 == j, pieces[j], d)
         shard = jnp.where(side == 0, me[YL], 1 - me[YL])
         return 2 * lax.rem(me[Z] + 8 - d, 8) + shard
 
-    for i in range(2 * sources):
+    for i in range(2 * count):
         if i % 2 == 0:
             copies[i // 2].wait()
         mark = inside(column + (me[WINDOW] + origin(i) * block), start_ref, end_ref, place)
@@ -232,50 +216,67 @@
         finish(total, jnp.maximum(i - 1, 0))
         return carry
 
-    lax.fori_loop(0, 2 * sources, step, 0)
+    lax.fori_loop(0, 2 * count, step, 0)
     total = None
     for j in range(chunks):
         part = weigh(j, most_ref[0:1, :])
         total = part if total is None else total + part
-    finish(total, 2 * sources - 1)
-
-
-def attend(me, starts, ends, key_value, queries):
+    finish(total, 2 * count - 1)
+
+
+def attend(pieces, me, starts, ends, key_value, before, queries):
     sources, block = key_value.shape[0], key_value.shape[1] // 2
-    window = 2 * block * sources
+    window, count = 2 * block * sources, len(pieces)
     return pl.pallas_call(
-        attend_kernel,
+        functools.partial(attend_kernel, pieces),
         out_shape=jax.ShapeDtypeStruct((2 * sources, HEAD, block), jnp.bfloat16),
-        in_specs=[SMEM] * 3 + [VMEM] + [HBM] * 8,
+        in_specs=[SMEM] * 3 + [VMEM] * 2 + [HBM] * count,
         out_specs=VMEM,
         scratch_shapes=[
             pltpu.VMEM((window, LANES), jnp.bfloat16),
             pltpu.VMEM((window // KEY_CHUNK, HEAD + 16, KEY_CHUNK), jnp.bfloat16),
-            pltpu.VMEM((2 * sources, LANES, block), jnp.bfloat16),
-        ]
-        + [pltpu.VMEM((window, block), jnp.float32), pltpu.VMEM((8, block), jnp.float32)]
-        + [pltpu.VMEM((8, block, LANES), jnp.bfloat16), pltpu.SemaphoreType.DMA((8,))],
+            pltpu.VMEM((2 * count, LANES, block), jnp.bfloat16),
+            pltpu.VMEM((window, block), jnp.float32),
+            pltpu.VMEM((8, block), jnp.float32),
+            pltpu.VMEM((count, block, LANES), jnp.bfloat16),
+            pltpu.SemaphoreType.DMA((count,)),
+        ],
         compiler_params=pltpu.CompilerParams(vmem_limit_bytes=24 * 1024 * 1024),
-    )(me, starts, ends, key_value, *queries)
+    )(me, starts, ends, key_value, before, *queries)
+
+
+PIECE_COUNT = 4
+
+
+def copy_rows(source, target, sems):
+    step = source.shape[0] // PIECE_COUNT
+    at = [pl.ds(i * step, step) for i in range(PIECE_COUNT)]
+    copies = [pltpu.make_async_copy(source.at[a], target.at[a], sems.at[i]) for i, a in enumerate(at)]
+    for copy in copies:
+        copy.start()
+    return copies
+
+
+def wait_all(copies):
+    for copy in copies:
+        copy.wait()
 
 
 def gate_kernel(mixed, frames, gain, w_out_hbm, w_glu_hbm, residual_ref, gated_ref, *scratch):
     w_out, w_glu, attended, out_sem, glu_sem = scratch
-    out_copy = pltpu.make_async_copy(w_out_hbm, w_out, out_sem)
-    glu_copy = pltpu.make_async_copy(w_glu_hbm, w_glu, glu_sem)
-    out_copy.start()
-    glu_copy.start()
+    out_copies = copy_rows(w_out_hbm, w_out, out_sem)
+    glu_copies = copy_rows(w_glu_hbm, w_glu, glu_sem)
     heads = mixed.shape[0]
     for pair in range(heads // 2):
         flipped = jnp.concatenate([mixed[2 * pair], mixed[2 * pair + 1]], axis=0).astype(jnp.float32)
         attended[:, pair * LANES : (pair + 1) * LANES] = flipped.T.astype(jnp.bfloat16)
-    out_copy.wait()
+    wait_all(out_copies)
     projected = jnp.dot(attended[...], w_out[...], preferred_element_type=jnp.float32)
     residual = (frames[...].astype(jnp.float32) + projected).astype(jnp.bfloat16)
     residual_ref[...] = residual
     width = frames.shape[1]
     conv_in = normalize(residual.astype(jnp.float32), gain[0:1, :]).astype(jnp.bfloat16)
-    glu_copy.wait()
+    wait_all(glu_copies)
     step = 256
     for j in range(0, width, step):
         a = jnp.dot(conv_in, w_glu[:, j : j + step], preferred_element_type=jnp.float32)
@@ -294,8 +295,8 @@
             pltpu.VMEM(w_out.shape, jnp.bfloat16),
             pltpu.VMEM(w_glu.shape, jnp.bfloat16),
             pltpu.VMEM(frames.shape, jnp.bfloat16),
-            pltpu.SemaphoreType.DMA,
-            pltpu.SemaphoreType.DMA,
+            pltpu.SemaphoreType.DMA((PIECE_COUNT,)),
+            pltpu.SemaphoreType.DMA((PIECE_COUNT,)),
         ],
         compiler_params=pltpu.CompilerParams(vmem_limit_bytes=58 * 1024 * 1024),
     )(mixed, frames, gain, w_out, w_glu)
@@ -320,7 +321,8 @@
     return totals
 
 
-def inner_kernel(me, start_ref, end_ref, gated, weights, out, padded):
+def inner_kernel(me, start_ref, end_ref, gated_hbm, weights, out, padded, gated, sems):
+    wait_all(copy_rows(gated_hbm, gated, sems))
     rows, width = gated.shape
     for c in range(width // LANES):
         padded[c, :RIM] = jnp.zeros((RIM, LANES), jnp.float32)
@@ -353,19 +355,22 @@
     return pl.pallas_call(
         inner_kernel,
         out_shape=jax.ShapeDtypeStruct(gated.shape, jnp.float32),
-        in_specs=[SMEM] * 3 + [VMEM] * 2,
+        in_specs=[SMEM] * 3 + [HBM, VMEM],
         out_specs=VMEM,
-        scratch_shapes=[pltpu.VMEM((width // LANES, rows + 2 * RIM, LANES), jnp.float32)],
-        compiler_params=pltpu.CompilerParams(vmem_limit_bytes=16 * 1024 * 1024),
+        scratch_shapes=[
+            pltpu.VMEM((width // LANES, rows + 2 * RIM, LANES), jnp.float32),
+            pltpu.VMEM(gated.shape, jnp.bfloat16),
+            pltpu.SemaphoreType.DMA((PIECE_COUNT,)),
+        ],
+        compiler_params=pltpu.CompilerParams(vmem_limit_bytes=60 * 1024 * 1024),
     )(me, starts, ends, gated, weights)
 
 
 def last_kernel(
-    me, start_ref, end_ref, inner, left, right, residual, weights, gain, w_proj_hbm, out, *scratch
+    me, start_ref, end_ref, inner, left, right, residual_hbm, weights, gain, w_proj_hbm, out, *scratch
 ):
-    w_proj, total, edge, sem = scratch
-    copy = pltpu.make_async_copy(w_proj_hbm, w_proj, sem)
-    copy.start()
+    w_proj, residual, total, edge, sems, residual_sems = scratch
+    copies = copy_rows(w_proj_hbm, w_proj, sems) + copy_rows(residual_hbm, residual, residual_sems)
     rows, width = inner.shape
     total[...] = inner[...]
     count = weights.shape[0]
@@ -384,7 +389,7 @@
             total[row : row + ROWS, lanes] = total[row : row + ROWS, lanes] + part
     normed = normalize(total[...], gain[0:1, :])
     activated = (normed * jax.nn.sigmoid(normed)).astype(jnp.bfloat16)
-    copy.wait()
+    wait_all(copies)
     projected = jnp.dot(activated, w_proj[...], preferred_element_type=jnp.float32)
     out[...] = (residual[...].astype(jnp.float32) + projected).astype(jnp.bfloat16)
 
@@ -394,15 +399,17 @@
     return pl.pallas_call(
         last_kernel,
         out_shape=jax.ShapeDtypeStruct(residual.shape, jnp.bfloat16),
-        in_specs=[SMEM] * 3 + [VMEM] * 6 + [HBM],
+        in_specs=[SMEM] * 3 + [VMEM] * 3 + [HBM] + [VMEM] * 2 + [HBM],
         out_specs=VMEM,
         scratch_shapes=[
             pltpu.VMEM(w_proj.shape, jnp.bfloat16),
+            pltpu.VMEM(residual.shape, jnp.bfloat16),
             pltpu.VMEM(inner.shape, jnp.float32),
             pltpu.VMEM((width // LANES, 3 * RIM, LANES), jnp.float32),
-            pltpu.SemaphoreType.DMA,
+            pltpu.SemaphoreType.DMA((PIECE_COUNT,)),
+            pltpu.SemaphoreType.DMA((PIECE_COUNT,)),
         ],
-        compiler_params=pltpu.CompilerParams(vmem_limit_bytes=24 * 1024 * 1024),
+        compiler_params=pltpu.CompilerParams(vmem_limit_bytes=58 * 1024 * 1024),
     )(me, starts, ends, inner, left, right, residual, weights, gain, w_proj)
 
 
@@ -428,21 +435,20 @@
 
     swap = lambda x, yh, c, z, yl: (x, yh, 1 - c, z, yl)
     across = lambda x, yh, c, z, yl: (x, yh, c, z, 1 - yl)
-    near = [send(shard[HEAD:], route(o)) for o in OFFSETS]
+    near = [send(shard, route(o)) for o in OFFSETS]
     other_frames = send(local_frames, across)
     far = [send(piece, swap) for piece in near]
-    near_q = [send(shard[:HEAD], route(o)) for o in OFFSETS]
-    far_q = send(jnp.concatenate(near_q, axis=0), swap)
-    key_value, normed = project_key_value(me, local_frames, other_frames, attn_gain[None, :], near + far)
-    queries = project_query(me, normed, near_q + [far_q])
+    key_value, *queries = project_qkv(me, local_frames, other_frames, attn_gain[None, :], near + far)
     groups = [[2 * z + yl for z in range(8)] for yl in range(2)]
     key_value = lax.all_to_all(key_value, "blk", 0, 0, axis_index_groups=groups, tiled=True)
-    queries = list(queries)
     for d in SEND_ORDER:
         queries[d] = send(queries[d], lambda x, yh, c, z, yl: (x, yh, c, z + d, yl))
     ends = jnp.cumsum(utt_lengths)
     starts = ends - utt_lengths
-    mixed = attend(me, starts, ends, key_value, queries)
+    mixed = jnp.zeros((16, HEAD, frame_rows), jnp.bfloat16)
+    for pieces in PIECES:
+        ready = [queries[d] for d in pieces]
+        mixed = attend(pieces, me, starts, ends, key_value, mixed, ready)
     mixed = lax.all_to_all(mixed, "blk", 0, 0, tiled=True)
     residual, gated = gate(mixed, local_frames, conv_gain[None, :], w_out, w_glu)
 

time: 149 us -> 151 us (1.013)
  the two profiles are of different devices: /device:TPU:2 before, /device:TPU:6 now
where the time goes in v4:
time: 151 us
  starting transfers between devices  58.7 us (39%)
  Pallas kernels  48.2 us (32%)
  blocking collectives  21.3 us (14%)
  waiting for transfers between devices  19.6 us (13%)
  local copies, waits for them, and re-layouts  2.2 us (1%)
    ppermute x18, starting transfers between devices, send(): return lax.ppermute(value, ('blk', 'grp'), pairs)  50.1 us
    pallas_call x2, Pallas kernels, attend(): pl.pallas_call(functools.partial(attend_kernel, pieces), out_shape=jax.Sh...  21.4 us
    all_to_all x1, blocking collectives, body(): mixed = lax.all_to_all(mixed, 'blk', 0, 0, tiled=True)  21.3 us
    ppermute x18, waiting for transfers between devices, send(): return lax.ppermute(value, ('blk', 'grp'), pairs)  19.6 us
    pallas_call x1, Pallas kernels, project_qkv(): pl.pallas_call(project_kernel, out_shape=[jax.ShapeDtypeStruct((8, 2 * ro...  8.78 us
    all_to_all x1, starting transfers between devices, body(): lax.all_to_all(key_value, 'blk', 0, 0, axis_index_groups=groups, tiled=True)  8.61 us
    pallas_call x1, Pallas kernels, gate(): pl.pallas_call(gate_kernel, out_shape=[shape, shape], in_specs=[VMEM] * 3...  6.81 us
    pallas_call x1, Pallas kernels, convolve_inner(): pl.pallas_call(inner_kernel, out_shape=jax.ShapeDtypeStruct(gated.shape,...  6.6 us
  transfers between devices with their start and end apart: 19, of which 4 were waited for; matrix products, arithmetic and copies ran while one was open for 1% of the time, Pallas kernels for 11%

profile of v4, /device:TPU:6, one launch (start us, length us, event | category | flops | bytes accessed | tf_op | source)
XLA Modules:
  0.0 150.7 jit_solution(1675065259326040641)
XLA Ops:
  0.0 1.6 %collective-permute-start.1 = (bf16[192,1024]{1,0:T(8,128)(2,1)}, bf16[192,1024]{1,0:T(8,128)(2,1)S(1)}, u32[]{:S(2)}, u32[]{:S(2)}) collective-permute-start(bf16[192,1024]{1,0:T(8,128)(2,1)} %bitcast.25), channel_id=1, source_target_pairs={{0,0},{1,18},{2,3},{3,17},{4,4},{5,22},{6,7},{7,21},{8,8},{9,26},{... | collective-permute-start | bytes 1179656 | tf_op jit(solution)/shard_map/ppermute | solution.py:45
  1.6 0.8 collective-permute-start.2
  2.5 2.4 %collective-permute-start.3 = (bf16[192,1024]{1,0:T(8,128)(2,1)}, bf16[192,1024]{1,0:T(8,128)(2,1)S(1)}, u32[]{:S(2)}, u32[]{:S(2)}) collective-permute-start(bf16[192,1024]{1,0:T(8,128)(2,1)} %bitcast.27), channel_id=1, source_target_pairs={{0,4},{1,22},{2,7},{3,21},{4,8},{5,26},{6,11},{7,25},{8,12},{9,30}... | collective-permute-start | bytes 1179656 | tf_op jit(solution)/shard_map/ppermute | solution.py:45
  4.9 0.4 collective-permute-start.4
  5.3 2.4 %collective-permute-start = (bf16[256,1024]{1,0:T(8,128)(2,1)}, bf16[256,1024]{1,0:T(8,128)(2,1)S(1)}, u32[]{:S(2)}, u32[]{:S(2)}) collective-permute-start(bf16[256,1024]{1,0:T(8,128)(2,1)} %bitcast.19), channel_id=1, source_target_pairs={{0,16},{1,17},{2,18},{3,19},{4,20},{5,21},{6,22},{7,23},{8,24},{9,... | collective-permute-start | bytes 1572872 | tf_op jit(solution)/shard_map/ppermute | solution.py:45
  7.7 13.9 %collective-permute-start.5 = (bf16[192,1024]{1,0:T(8,128)(2,1)S(1)}, bf16[192,1024]{1,0:T(8,128)(2,1)S(1)}, u32[]{:S(2)}, u32[]{:S(2)}) collective-permute-start(bf16[192,1024]{1,0:T(8,128)(2,1)S(1)} %collective-permute-done.1.refs_0_), channel_id=1, source_target_pairs={{0,1},{1,0},{2,3},{3,2},{4,5},{5,4},{6,7},{7,6},{8,9},{9,8},{10,11... | collective-permute-start | bytes 1179656 | tf_op jit(solution)/shard_map/ppermute | solution.py:45
  21.6 3.0 %collective-permute-start.6 = (bf16[192,1024]{1,0:T(8,128)(2,1)S(1)}, bf16[192,1024]{1,0:T(8,128)(2,1)S(1)}, u32[]{:S(2)}, u32[]{:S(2)}) collective-permute-start(bf16[192,1024]{1,0:T(8,128)(2,1)S(1)} %collective-permute-done.2.refs_1_), channel_id=1, source_target_pairs={{0,1},{1,0},{2,3},{3,2},{4,5},{5,4},{6,7},{7,6},{8,9},{9,8},{10,11... | collective-permute-start | bytes 1179656 | tf_op jit(solution)/shard_map/ppermute | solution.py:45
  24.7 0.4 collective-permute-start.8
  25.1 0.7 stack.27.me
  26.0 0.6 collective-permute-done.7.refs_6_
  26.5 0.7 collective-permute-done.8.refs_7_
  27.3 8.8 %shard_map.100 = (bf16[8,512,128]{2,1,0:T(8,128)(2,1)}, bf16[256,128]{1,0:T(8,128)(2,1)}, bf16[256,128]{1,0:T(8,128)(2,1)}, bf16[256,128]{1,0:T(8,128)(2,1)}, bf...) custom-call(s32[6]{0:T(128)} %stack.27.me, ...), custom_call_target="tpu_custom_call" | custom-call | tf_op jit(solution)/shard_map/pallas_call | solution.py:123
  36.2 8.6 %all-to-all-start = ((bf16[8,512,128]{2,1,0:T(8,128)(2,1)}), bf16[8,512,128]{2,1,0:T(8,128)(2,1)S(1)}, u32[]{:S(2)}, u32[]{:S(2)}) async-start(bf16[8,512,128]{2,1,0:T(8,128)(2,1)} %get-tuple-element.16), calls=%async_computation | async-start | bytes 2097152 | tf_op jit(solution)/shard_map/all_to_all | solution.py:443
  44.8 3.2 %collective-permute-start.10 = (bf16[256,128]{1,0:T(8,128)(2,1)S(1)}, bf16[256,128]{1,0:T(8,128)(2,1)S(1)}, u32[]{:S(2)}, u32[]{:S(2)}) collective-permute-start(bf16[256,128]{1,0:T(8,128)(2,1)S(1)} %copy-done.20), channel_id=1, source_target_pairs={{0,224},{1,225},{2,226},{3,227},{4,228},{5,229},{6,230},{7,231},{8... | collective-permute-start | bytes 196616 | tf_op jit(solution)/shard_map/ppermute | solution.py:45
  48.0 0.2 collective-permute-start.11
  48.3 0.2 reduce-window.9
  48.5 1.5 collective-permute-start.9
  50.0 2.5 %collective-permute-start.12 = (bf16[256,128]{1,0:T(8,128)(2,1)S(1)}, bf16[256,128]{1,0:T(8,128)(2,1)S(1)}, u32[]{:S(2)}, u32[]{:S(2)}) collective-permute-start(bf16[256,128]{1,0:T(8,128)(2,1)S(1)} %copy-done.17), channel_id=1, source_target_pairs={{0,192},{1,193},{2,194},{3,195},{4,196},{5,197},{6,198},{7,199},{8... | collective-permute-start | bytes 196616 | tf_op jit(solution)/shard_map/ppermute | solution.py:45
  52.5 2.5 %collective-permute-start.13 = (bf16[256,128]{1,0:T(8,128)(2,1)S(1)}, bf16[256,128]{1,0:T(8,128)(2,1)S(1)}, u32[]{:S(2)}, u32[]{:S(2)}) collective-permute-start(bf16[256,128]{1,0:T(8,128)(2,1)S(1)} %copy-done.16), channel_id=1, source_target_pairs={{0,96},{1,97},{2,98},{3,99},{4,100},{5,101},{6,102},{7,103},{8,104... | collective-permute-start | bytes 196616 | tf_op jit(solution)/shard_map/ppermute | solution.py:45
  55.0 18.2 %collective-permute-done.10.refs_2_ = bf16[256,128]{1,0:T(8,128)(2,1)S(1)} collective-permute-done((bf16[256,128]{1,0:T(8,128)(2,1)S(1)}, bf16[256,128]{1,0:T(8,128)(2,1)S(1)}, u32[]{:S(2)}, u32[]{:S(2)}) %collective-permute-start.10) | collective-permute-done | bytes 65568 | tf_op jit(solution)/shard_map/ppermute | solution.py:45
  73.2 3.1 %collective-permute-start.14 = (bf16[256,128]{1,0:T(8,128)(2,1)S(1)}, bf16[256,128]{1,0:T(8,128)(2,1)S(1)}, u32[]{:S(2)}, u32[]{:S(2)}) collective-permute-start(bf16[256,128]{1,0:T(8,128)(2,1)S(1)} %copy-done.15), channel_id=1, source_target_pairs={{0,160},{1,161},{2,162},{3,163},{4,164},{5,165},{6,166},{7,167},{8... | collective-permute-start | bytes 196616 | tf_op jit(solution)/shard_map/ppermute | solution.py:45
  76.3 2.2 %collective-permute-start.15 = (bf16[256,128]{1,0:T(8,128)(2,1)S(1)}, bf16[256,128]{1,0:T(8,128)(2,1)S(1)}, u32[]{:S(2)}, u32[]{:S(2)}) collective-permute-start(bf16[256,128]{1,0:T(8,128)(2,1)S(1)} %copy-done.14), channel_id=1, source_target_pairs={{0,128},{1,129},{2,130},{3,131},{4,132},{5,133},{6,134},{7,135},{8... | collective-permute-start | bytes 196616 | tf_op jit(solution)/shard_map/ppermute | solution.py:45
  78.5 10.7 %shard_map.101.before = bf16[16,64,256]{2,1,0:T(8,128)(2,1)S(1)} custom-call(s32[6]{0:T(128)S(1)} %copy-done.1, s32[8]{0:T(128)S(1)} %bitcast_subtract_fusion.start_ref, s32[8]{0:T(128)S(1)} %bitcast.15, bf16[8,512,128]{2,1,0:T(8,128)(2,1)S(1)} %all-to-all-done.in_ref, bf16[16,64,256]{2,1,0:T(8,128)(2,1)S(1)} %broadcast_in_dim.16.before, ...), custom_call_target="tpu_custom_call" | custom-call | tf_op jit(solution)/shard_map/pallas_call | solution.py:230
  89.3 10.7 %shard_map.102 = bf16[16,64,256]{2,1,0:T(8,128)(2,1)S(1)} custom-call(s32[6]{0:T(128)S(1)} %copy-done.1, s32[8]{0:T(128)S(1)} %bitcast_subtract_fusion.start_ref, s32[8]{0:T(128)S(1)} %bitcast.16, bf16[8,512,128]{2,1,0:T(8,128)(2,1)S(1)} %all-to-all-done.in_ref, bf16[16,64,256]{2,1,0:T(8,128)(2,1)S(1)} %shard_map.101.before, ...), custom_call_target="tpu_custom_call" | custom-call | tf_op jit(solution)/shard_map/pallas_call | solution.py:230
  100.0 21.3 %all_to_all.10.mixed = bf16[16,64,256]{2,1,0:T(8,128)(2,1)} all-to-all(bf16[16,64,256]{2,1,0:T(8,128)(2,1)S(1)} %shard_map.102), channel_id=1, replica_groups=mesh['blk'=16,'grp'=16] {'blk'}, dimensions={0} | all-to-all | bytes 1048576 | tf_op jit(solution)/shard_map/all_to_all | solution.py:452
  121.2 6.8 %shard_map.103 = (bf16[256,1024]{1,0:T(8,128)(2,1)}, bf16[256,1024]{1,0:T(8,128)(2,1)}) custom-call(bf16[16,64,256]{2,1,0:T(8,128)(2,1)} %all_to_all.10.mixed, bf16[256,1024]{1,0:T(8,128)(2,1)} %bitcast.21, f32[1,1024]{1,0:T(1,128)} %bitcast.23, bf16[1024,1024]{1,0:T(8,128)(2,1)} %w_out_hbm.1, bf16[1024,2048]{1,0:T(8,128)(2,1)} %w_glu_hbm.1), custom_call_target="tpu_custom_call" | custom-call | tf_op jit(solution)/shard_map/pallas_call | solution.py:289
  128.1 0.8 fusion
  128.8 2.5 %collective-permute-start.16 = (bf16[16,1024]{1,0:T(8,128)(2,1)S(1)}, bf16[16,1024]{1,0:T(8,128)(2,1)S(1)}, u32[]{:S(2)}, u32[]{:S(2)}) collective-permute-start(bf16[16,1024]{1,0:T(8,128)(2,1)S(1)} %get-tuple-element.28), channel_id=1, source_target_pairs={{0,16},{1,17},{2,18},{3,19},{4,20},{5,21},{6,22},{7,23},{8,24},{9,... | collective-permute-start | bytes 98312 | tf_op jit(solution)/shard_map/ppermute | solution.py:45
  131.3 7.3 %collective-permute-start.17 = (bf16[16,1024]{1,0:T(8,128)(2,1)S(1)}, bf16[16,1024]{1,0:T(8,128)(2,1)S(1)}, u32[]{:S(2)}, u32[]{:S(2)}) collective-permute-start(bf16[16,1024]{1,0:T(8,128)(2,1)S(1)} %get-tuple-element.27), channel_id=1, source_target_pairs={{1,240},{2,241},{3,242},{4,243},{5,244},{6,245},{7,246},{8,247},{9... | collective-permute-start | bytes 98312 | tf_op jit(solution)/shard_map/ppermute | solution.py:45
  138.6 6.6 %shard_map.104.inner = f32[256,1024]{1,0:T(8,128)} custom-call(s32[6]{0:T(128)} %stack.27.me, s32[8]{0:T(128)} %copy-done.3, s32[8]{0:T(128)} %bitcast.17, bf16[256,1024]{1,0:T(8,128)(2,1)} %get-tuple-element.25.gated_hbm, f32[31,1024]{1,0:T(8,128)} %weights.3), custom_call_target="tpu_custom_call" | custom-call | tf_op jit(solution)/shard_map/pallas_call | solution.py:355
  145.3 0.6 copy-done.12
  145.9 4.6 %shard_map.105 = bf16[256,1024]{1,0:T(8,128)(2,1)} custom-call(s32[6]{0:T(128)} %stack.27.me, s32[8]{0:T(128)} %copy-done.3, s32[8]{0:T(128)} %bitcast.18, f32[256,1024]{1,0:T(8,128)} %shard_map.104.inner, bf16[16,1024]{1,0:T(8,128)(2,1)} %copy-done.12, bf16[16,1024]{1,0:T(8,128)(2,1)} %copy-done.13, bf16[256,1024]{1,0:T(8,128)(2,1)} %get-tuple-element.26.residual_hbm, ...), custom_call_target="tpu_custom_call" | custom-call | tf_op jit(solution)/shard_map/pallas_call | solution.py:399
  (62 shorter events, 0.5 us)
Async XLA Ops:
  0.0 7.7 %collective-permute-start.1 = (bf16[192,1024]{1,0:T(8,128)(2,1)}, bf16[192,1024]{1,0:T(8,128)(2,1)S(1)}, u32[]{:S(2)}, u32[]{:S(2)}) collective-permute-start(bf16[192,1024]{1,0:T(8,128)(2,1)} %bitcast.25), channel_id=1, source_target_pairs={{0,0},{1,18},{2,3},{3,17},{4,4},{5,22},{6,7},{7,21},{8,8},{9,26},{... | collective-permute-start | bytes 1179656 | tf_op jit(solution)/shard_map/ppermute | solution.py:45
  1.6 20.0 %collective-permute-start.2 = (bf16[192,1024]{1,0:T(8,128)(2,1)}, bf16[192,1024]{1,0:T(8,128)(2,1)S(1)}, u32[]{:S(2)}, u32[]{:S(2)}) collective-permute-start(bf16[192,1024]{1,0:T(8,128)(2,1)} %bitcast.26), channel_id=1, source_target_pairs={{0,12},{1,30},{2,15},{3,29},{4,0},{5,18},{6,3},{7,17},{8,4},{9,22}... | collective-permute-start | bytes 1179656 | tf_op jit(solution)/shard_map/ppermute | solution.py:45
  2.5 22.2 %collective-permute-start.3 = (bf16[192,1024]{1,0:T(8,128)(2,1)}, bf16[192,1024]{1,0:T(8,128)(2,1)S(1)}, u32[]{:S(2)}, u32[]{:S(2)}) collective-permute-start(bf16[192,1024]{1,0:T(8,128)(2,1)} %bitcast.27), channel_id=1, source_target_pairs={{0,4},{1,22},{2,7},{3,21},{4,8},{5,26},{6,11},{7,25},{8,12},{9,30}... | collective-permute-start | bytes 1179656 | tf_op jit(solution)/shard_map/ppermute | solution.py:45
  4.9 19.8 %collective-permute-start.4 = (bf16[192,1024]{1,0:T(8,128)(2,1)}, bf16[192,1024]{1,0:T(8,128)(2,1)S(1)}, u32[]{:S(2)}, u32[]{:S(2)}) collective-permute-start(bf16[192,1024]{1,0:T(8,128)(2,1)} %bitcast.28), channel_id=1, source_target_pairs={{0,8},{1,26},{2,11},{3,25},{4,12},{5,30},{6,15},{7,29},{8,0},{9,18... | collective-permute-start | bytes 1179656 | tf_op jit(solution)/shard_map/ppermute | solution.py:45
  5.3 20.5 %collective-permute-start = (bf16[256,1024]{1,0:T(8,128)(2,1)}, bf16[256,1024]{1,0:T(8,128)(2,1)S(1)}, u32[]{:S(2)}, u32[]{:S(2)}) collective-permute-start(bf16[256,1024]{1,0:T(8,128)(2,1)} %bitcast.19), channel_id=1, source_target_pairs={{0,16},{1,17},{2,18},{3,19},{4,20},{5,21},{6,22},{7,23},{8,24},{9,... | collective-permute-start | bytes 1572872 | tf_op jit(solution)/shard_map/ppermute | solution.py:45
  7.7 19.5 %copy-start.5 = (bf16[192,1024]{1,0:T(8,128)(2,1)}, bf16[192,1024]{1,0:T(8,128)(2,1)S(1)}, u32[]{:S(2)}) copy-start(bf16[192,1024]{1,0:T(8,128)(2,1)S(1)} %collective-permute-done.1.refs_0_) | copy-start | bytes 1179652
  7.7 18.1 %collective-permute-start.5 = (bf16[192,1024]{1,0:T(8,128)(2,1)S(1)}, bf16[192,1024]{1,0:T(8,128)(2,1)S(1)}, u32[]{:S(2)}, u32[]{:S(2)}) collective-permute-start(bf16[192,1024]{1,0:T(8,128)(2,1)S(1)} %collective-permute-done.1.refs_0_), channel_id=1, source_target_pairs={{0,1},{1,0},{2,3},{3,2},{4,5},{5,4},{6,7},{7,6},{8,9},{9,8},{10,11... | collective-permute-start | bytes 1179656 | tf_op jit(solution)/shard_map/ppermute | solution.py:45
  21.6 4.4 %collective-permute-start.6 = (bf16[192,1024]{1,0:T(8,128)(2,1)S(1)}, bf16[192,1024]{1,0:T(8,128)(2,1)S(1)}, u32[]{:S(2)}, u32[]{:S(2)}) collective-permute-start(bf16[192,1024]{1,0:T(8,128)(2,1)S(1)} %collective-permute-done.2.refs_1_), channel_id=1, source_target_pairs={{0,1},{1,0},{2,3},{3,2},{4,5},{5,4},{6,7},{7,6},{8,9},{9,8},{10,11... | collective-permute-start | bytes 1179656 | tf_op jit(solution)/shard_map/ppermute | solution.py:45
  24.6 1.9 %collective-permute-start.7 = (bf16[192,1024]{1,0:T(8,128)(2,1)S(1)}, bf16[192,1024]{1,0:T(8,128)(2,1)S(1)}, u32[]{:S(2)}, u32[]{:S(2)}) collective-permute-start(bf16[192,1024]{1,0:T(8,128)(2,1)S(1)} %collective-permute-done.3.refs_2_), channel_id=1, source_target_pairs={{0,1},{1,0},{2,3},{3,2},{4,5},{5,4},{6,7},{7,6},{8,9},{9,8},{10,11... | collective-permute-start | bytes 1179656 | tf_op jit(solution)/shard_map/ppermute | solution.py:45
  24.7 2.5 %collective-permute-start.8 = (bf16[192,1024]{1,0:T(8,128)(2,1)S(1)}, bf16[192,1024]{1,0:T(8,128)(2,1)}, u32[]{:S(2)}, u32[]{:S(2)}) collective-permute-start(bf16[192,1024]{1,0:T(8,128)(2,1)S(1)} %collective-permute-done.4.refs_3_), channel_id=1, source_target_pairs={{0,1},{1,0},{2,3},{3,2},{4,5},{5,4},{6,7},{7,6},{8,9},{9,8},{10,11... | collective-permute-start | bytes 1179656 | tf_op jit(solution)/shard_map/ppermute | solution.py:45
  36.1 8.7 %copy-start.20 = (bf16[256,128]{1,0:T(8,128)(2,1)S(1)}, bf16[256,128]{1,0:T(8,128)(2,1)}, u32[]{:S(2)}) copy-start(bf16[256,128]{1,0:T(8,128)(2,1)} %get-tuple-element.19) | copy-start | bytes 196612
  36.1 11.9 %copy-start.19 = (bf16[256,128]{1,0:T(8,128)(2,1)S(1)}, bf16[256,128]{1,0:T(8,128)(2,1)}, u32[]{:S(2)}) copy-start(bf16[256,128]{1,0:T(8,128)(2,1)} %get-tuple-element.20) | copy-start | bytes 196612
  36.1 12.2 %copy-start.21 = (s32[8]{0:T(128)S(1)}, s32[8]{0:T(128)}, u32[]{:S(2)}) copy-start(s32[8]{0:T(128)} %param.11) | copy-start | bytes 100
  36.1 12.4 %copy-start.18 = (bf16[256,128]{1,0:T(8,128)(2,1)S(1)}, bf16[256,128]{1,0:T(8,128)(2,1)}, u32[]{:S(2)}) copy-start(bf16[256,128]{1,0:T(8,128)(2,1)} %get-tuple-element.18) | copy-start | bytes 196612
  36.1 13.8 %copy-start.17 = (bf16[256,128]{1,0:T(8,128)(2,1)S(1)}, bf16[256,128]{1,0:T(8,128)(2,1)}, u32[]{:S(2)}) copy-start(bf16[256,128]{1,0:T(8,128)(2,1)} %get-tuple-element.21) | copy-start | bytes 196612
  36.1 16.4 %copy-start.16 = (bf16[256,128]{1,0:T(8,128)(2,1)S(1)}, bf16[256,128]{1,0:T(8,128)(2,1)}, u32[]{:S(2)}) copy-start(bf16[256,128]{1,0:T(8,128)(2,1)} %get-tuple-element.22) | copy-start | bytes 196612
  36.1 37.0 %copy-start.15 = (bf16[256,128]{1,0:T(8,128)(2,1)S(1)}, bf16[256,128]{1,0:T(8,128)(2,1)}, u32[]{:S(2)}) copy-start(bf16[256,128]{1,0:T(8,128)(2,1)} %get-tuple-element.23) | copy-start | bytes 196612
  36.1 40.1 %copy-start.14 = (bf16[256,128]{1,0:T(8,128)(2,1)S(1)}, bf16[256,128]{1,0:T(8,128)(2,1)}, u32[]{:S(2)}) copy-start(bf16[256,128]{1,0:T(8,128)(2,1)} %get-tuple-element.24) | copy-start | bytes 196612
  36.2 42.3 %copy-start = (bf16[256,128]{1,0:T(8,128)(2,1)S(1)}, bf16[256,128]{1,0:T(8,128)(2,1)}, u32[]{:S(2)}) copy-start(bf16[256,128]{1,0:T(8,128)(2,1)} %get-tuple-element.17.refs_0_) | copy-start | bytes 196612
  36.2 42.3 %copy-start.1 = (s32[6]{0:T(128)S(1)}, s32[6]{0:T(128)}, u32[]{:S(2)}) copy-start(s32[6]{0:T(128)} %stack.27.me) | copy-start | bytes 76
  36.2 42.3 %all-to-all-start = ((bf16[8,512,128]{2,1,0:T(8,128)(2,1)}), bf16[8,512,128]{2,1,0:T(8,128)(2,1)S(1)}, u32[]{:S(2)}, u32[]{:S(2)}) async-start(bf16[8,512,128]{2,1,0:T(8,128)(2,1)} %get-tuple-element.16), calls=%async_computation | async-start | bytes 2097152 | tf_op jit(solution)/shard_map/all_to_all | solution.py:443
  44.8 28.4 %collective-permute-start.10 = (bf16[256,128]{1,0:T(8,128)(2,1)S(1)}, bf16[256,128]{1,0:T(8,128)(2,1)S(1)}, u32[]{:S(2)}, u32[]{:S(2)}) collective-permute-start(bf16[256,128]{1,0:T(8,128)(2,1)S(1)} %copy-done.20), channel_id=1, source_target_pairs={{0,224},{1,225},{2,226},{3,227},{4,228},{5,229},{6,230},{7,231},{8... | collective-permute-start | bytes 196616 | tf_op jit(solution)/shard_map/ppermute | solution.py:45
  48.0 28.2 %collective-permute-start.11 = (bf16[256,128]{1,0:T(8,128)(2,1)S(1)}, bf16[256,128]{1,0:T(8,128)(2,1)S(1)}, u32[]{:S(2)}, u32[]{:S(2)}) collective-permute-start(bf16[256,128]{1,0:T(8,128)(2,1)S(1)} %copy-done.19), channel_id=1, source_target_pairs={{0,64},{1,65},{2,66},{3,67},{4,68},{5,69},{6,70},{7,71},{8,72},{9,... | collective-permute-start | bytes 196616 | tf_op jit(solution)/shard_map/ppermute | solution.py:45
  48.5 51.5 %copy-start.2 = (s32[8,1]{0,1:T(1,128)}, s32[8,1]{0,1:T(1,128)S(1)}, u32[]{:S(2)}) copy-start(s32[8,1]{0,1:T(1,128)S(1)} %reduce-window.9) | copy-start | bytes 100
  48.5 30.0 %collective-permute-start.9 = (bf16[256,128]{1,0:T(8,128)(2,1)S(1)}, bf16[256,128]{1,0:T(8,128)(2,1)S(1)}, u32[]{:S(2)}, u32[]{:S(2)}) collective-permute-start(bf16[256,128]{1,0:T(8,128)(2,1)S(1)} %copy-done.18), channel_id=1, source_target_pairs={{0,32},{1,33},{2,34},{3,35},{4,36},{5,37},{6,38},{7,39},{8,40},{9,... | collective-permute-start | bytes 196616 | tf_op jit(solution)/shard_map/ppermute | solution.py:45
  50.0 39.3 %collective-permute-start.12 = (bf16[256,128]{1,0:T(8,128)(2,1)S(1)}, bf16[256,128]{1,0:T(8,128)(2,1)S(1)}, u32[]{:S(2)}, u32[]{:S(2)}) collective-permute-start(bf16[256,128]{1,0:T(8,128)(2,1)S(1)} %copy-done.17), channel_id=1, source_target_pairs={{0,192},{1,193},{2,194},{3,195},{4,196},{5,197},{6,198},{7,199},{8... | collective-permute-start | bytes 196616 | tf_op jit(solution)/shard_map/ppermute | solution.py:45
  52.5 36.7 %collective-permute-start.13 = (bf16[256,128]{1,0:T(8,128)(2,1)S(1)}, bf16[256,128]{1,0:T(8,128)(2,1)S(1)}, u32[]{:S(2)}, u32[]{:S(2)}) collective-permute-start(bf16[256,128]{1,0:T(8,128)(2,1)S(1)} %copy-done.16), channel_id=1, source_target_pairs={{0,96},{1,97},{2,98},{3,99},{4,100},{5,101},{6,102},{7,103},{8,104... | collective-permute-start | bytes 196616 | tf_op jit(solution)/shard_map/ppermute | solution.py:45
  73.2 16.1 %collective-permute-start.14 = (bf16[256,128]{1,0:T(8,128)(2,1)S(1)}, bf16[256,128]{1,0:T(8,128)(2,1)S(1)}, u32[]{:S(2)}, u32[]{:S(2)}) collective-permute-start(bf16[256,128]{1,0:T(8,128)(2,1)S(1)} %copy-done.15), channel_id=1, source_target_pairs={{0,160},{1,161},{2,162},{3,163},{4,164},{5,165},{6,166},{7,167},{8... | collective-permute-start | bytes 196616 | tf_op jit(solution)/shard_map/ppermute | solution.py:45
  76.3 13.0 %collective-permute-start.15 = (bf16[256,128]{1,0:T(8,128)(2,1)S(1)}, bf16[256,128]{1,0:T(8,128)(2,1)S(1)}, u32[]{:S(2)}, u32[]{:S(2)}) collective-permute-start(bf16[256,128]{1,0:T(8,128)(2,1)S(1)} %copy-done.14), channel_id=1, source_target_pairs={{0,128},{1,129},{2,130},{3,131},{4,132},{5,133},{6,134},{7,135},{8... | collective-permute-start | bytes 196616 | tf_op jit(solution)/shard_map/ppermute | solution.py:45
  78.4 21.5 %copy-start.3 = (s32[8]{0:T(128)}, s32[8]{0:T(128)S(1)}, u32[]{:S(2)}) copy-start(s32[8]{0:T(128)S(1)} %bitcast_subtract_fusion.start_ref) | copy-start | bytes 100
  128.8 16.4 %collective-permute-start.16 = (bf16[16,1024]{1,0:T(8,128)(2,1)S(1)}, bf16[16,1024]{1,0:T(8,128)(2,1)S(1)}, u32[]{:S(2)}, u32[]{:S(2)}) collective-permute-start(bf16[16,1024]{1,0:T(8,128)(2,1)S(1)} %get-tuple-element.28), channel_id=1, source_target_pairs={{0,16},{1,17},{2,18},{3,19},{4,20},{5,21},{6,22},{7,23},{8,24},{9,... | collective-permute-start | bytes 98312 | tf_op jit(solution)/shard_map/ppermute | solution.py:45
  131.3 13.9 %collective-permute-start.17 = (bf16[16,1024]{1,0:T(8,128)(2,1)S(1)}, bf16[16,1024]{1,0:T(8,128)(2,1)S(1)}, u32[]{:S(2)}, u32[]{:S(2)}) collective-permute-start(bf16[16,1024]{1,0:T(8,128)(2,1)S(1)} %get-tuple-element.27), channel_id=1, source_target_pairs={{1,240},{2,241},{3,242},{4,243},{5,244},{6,245},{7,246},{8,247},{9... | collective-permute-start | bytes 98312 | tf_op jit(solution)/shard_map/ppermute | solution.py:45
  (9 other events, 16.9 us)

commit v5 on v4

--- a/solution.py
+++ b/solution.py
@@ -15,7 +15,7 @@
 ROWS = 16
 OFFSETS = (0, 1, 3, 2)
 SEND_ORDER = (1, 7, 2, 6, 3, 5, 4)
-PIECES = ((0, 1, 7, 2), (6, 3, 5, 4))
+PIECES = ((0, 1, 7), (2, 6, 3, 5, 4))
 LOG2E = 1.4426950408889634
 
 epsilon = 1e-05
@@ -83,58 +83,66 @@
         out[index, at : at + HEAD] = flipped[:, j * LANES : (j + 1) * LANES].astype(jnp.bfloat16)
 
 
-def project_kernel(me, own_hbm, other_ref, gain_hbm, *refs):
-    shards, out, pieces = refs[:8], refs[8], refs[9:17]
-    normed, staged, own_ref, gain_ref, sems, in_sems = refs[17:]
-    pairs = ((gain_hbm, gain_ref), (own_hbm, own_ref))
-    copies = [pltpu.make_async_copy(a, b, in_sems.at[i]) for i, (a, b) in enumerate(pairs)]
-    for copy in copies:
-        copy.start()
-    copies[0].wait()
-    rows = own_ref.shape[0]
-    gain = gain_ref[0:1, :]
-    normed[rows:] = normalize(other_ref[...].astype(jnp.float32), gain).astype(jnp.bfloat16)
-    copies[1].wait()
-    normed[:rows] = normalize(own_ref[...].astype(jnp.float32), gain).astype(jnp.bfloat16)
+def norm_kernel(frames, gain, out):
+    out[...] = normalize(frames[...].astype(jnp.float32), gain[0:1, :]).astype(jnp.bfloat16)
+
+
+def norm(frames, gain):
+    return pl.pallas_call(
+        norm_kernel,
+        out_shape=jax.ShapeDtypeStruct(frames.shape, jnp.bfloat16),
+        in_specs=[VMEM] * 2,
+        out_specs=VMEM,
+        compiler_params=pltpu.CompilerParams(vmem_limit_bytes=8 * 1024 * 1024),
+    )(frames, gain)
+
+
+def key_value_kernel(me, own, other, *refs):
+    shards, out, both_rows = refs[:8], refs[8], refs[9]
+    rows = own.shape[0]
+    both_rows[:rows] = own[...]
+    both_rows[rows:] = other[...]
     low = low_lanes(rows)
     for i in range(0, 8, 2):
         heads = shard_head(me, i), shard_head(me, i + 1)
         weights = jnp.concatenate([shards[j][HEAD : 2 * HEAD, :] for j in (i, i + 1)], axis=0)
-        both = lax.dot_general(normed[...], weights, CONTRACT, preferred_element_type=jnp.float32)
-        own, other = both[:rows], both[rows:]
-        out[heads[0], :rows] = jnp.where(low, own, swap_lanes(other)).astype(jnp.bfloat16)
-        out[heads[1], :rows] = jnp.where(low, swap_lanes(own), other).astype(jnp.bfloat16)
-        for j, head in zip((i, i + 1), heads):
-            weights = jnp.concatenate([shards[j][2 * HEAD :, :], shards[j][:HEAD, :]], axis=0)
-            both = lax.dot_general(weights, normed[...], CONTRACT, preferred_element_type=jnp.float32)
-            transposed(out, head, rows, both[:HEAD])
-            query = both[HEAD:] * (HEAD**-0.5 * LOG2E)
-            transposed(staged, lax.rem(head + 8 - me[Z], 8), 0, query)
-    copies = [pltpu.make_async_copy(staged.at[d], pieces[d], sems.at[d]) for d in range(8)]
-    for copy in copies:
-        copy.start()
-    for copy in copies:
-        copy.wait()
-
-
-def project_qkv(me, own, other, gain, shards):
+        both = lax.dot_general(both_rows[...], weights, CONTRACT, preferred_element_type=jnp.float32)
+        mine, theirs = both[:rows], both[rows:]
+        out[heads[0], :rows] = jnp.where(low, mine, swap_lanes(theirs)).astype(jnp.bfloat16)
+        out[heads[1], :rows] = jnp.where(low, swap_lanes(mine), theirs).astype(jnp.bfloat16)
+        weights = jnp.concatenate([shards[j][2 * HEAD :, :] for j in (i, i + 1)], axis=0)
+        both = lax.dot_general(weights, both_rows[...], CONTRACT, preferred_element_type=jnp.float32)
+        transposed(out, heads[0], rows, both[:HEAD])
+        transposed(out, heads[1], rows, both[HEAD:])
+
+
+def query_kernel(me, own, other, *refs):
+    shards, pieces, both_rows, staged = refs[:8], refs[8:16], refs[16], refs[17]
+    rows = own.shape[0]
+    both_rows[:rows] = own[...]
+    both_rows[rows:] = other[...]
+    for i in range(0, 8, 2):
+        weights = jnp.concatenate([shards[j][:HEAD, :] for j in (i, i + 1)], axis=0)
+        both = lax.dot_general(weights, both_rows[...], CONTRACT, preferred_element_type=jnp.float32)
+        both = both * (HEAD**-0.5 * LOG2E)
+        for j in range(2):
+            piece = lax.rem(shard_head(me, i + j) + 8 - me[Z], 8)
+            transposed(staged, piece, 0, both[j * HEAD : (j + 1) * HEAD])
+    for d in range(8):
+        pieces[d][...] = staged[d]
+
+
+def project(kernel, shapes, staged, me, own, other, shards):
     rows, width = own.shape
-    piece = jax.ShapeDtypeStruct((rows, LANES), jnp.bfloat16)
-    return pl.pallas_call(
-        project_kernel,
-        out_shape=[jax.ShapeDtypeStruct((8, 2 * rows, LANES), jnp.bfloat16)] + [piece] * 8,
-        in_specs=[SMEM, HBM, VMEM, HBM] + [VMEM] * 8,
-        out_specs=[VMEM] + [HBM] * 8,
-        scratch_shapes=[
-            pltpu.VMEM((2 * rows, width), jnp.bfloat16),
-            pltpu.VMEM((8,) + piece.shape, jnp.bfloat16),
-            pltpu.VMEM(own.shape, jnp.bfloat16),
-            pltpu.VMEM(gain.shape, jnp.float32),
-            pltpu.SemaphoreType.DMA((8,)),
-            pltpu.SemaphoreType.DMA((2,)),
-        ],
-        compiler_params=pltpu.CompilerParams(vmem_limit_bytes=59 * 1024 * 1024),
-    )(me, own, other, gain, *shards)
+    return pl.pallas_call(
+        kernel,
+        out_shape=[jax.ShapeDtypeStruct(shape, jnp.bfloat16) for shape in shapes],
+        in_specs=[SMEM] + [VMEM] * 10,
+        out_specs=[VMEM] * len(shapes),
+        scratch_shapes=[pltpu.VMEM((2 * rows, width), jnp.bfloat16)]
+        + [pltpu.VMEM(shape, jnp.bfloat16) for shape in staged],
+        compiler_params=pltpu.CompilerParams(vmem_limit_bytes=16 * 1024 * 1024),
+    )(me, own, other, *shards)
 
 
 def attend_kernel(pieces, me, start_ref, end_ref, in_ref, before, *refs):
@@ -245,38 +253,23 @@
     )(me, starts, ends, key_value, before, *queries)
 
 
-PIECE_COUNT = 4
-
-
-def copy_rows(source, target, sems):
-    step = source.shape[0] // PIECE_COUNT
-    at = [pl.ds(i * step, step) for i in range(PIECE_COUNT)]
-    copies = [pltpu.make_async_copy(source.at[a], target.at[a], sems.at[i]) for i, a in enumerate(at)]
-    for copy in copies:
-        copy.start()
-    return copies
-
-
-def wait_all(copies):
-    for copy in copies:
-        copy.wait()
-
-
 def gate_kernel(mixed, frames, gain, w_out_hbm, w_glu_hbm, residual_ref, gated_ref, *scratch):
     w_out, w_glu, attended, out_sem, glu_sem = scratch
-    out_copies = copy_rows(w_out_hbm, w_out, out_sem)
-    glu_copies = copy_rows(w_glu_hbm, w_glu, glu_sem)
+    out_copy = pltpu.make_async_copy(w_out_hbm, w_out, out_sem)
+    glu_copy = pltpu.make_async_copy(w_glu_hbm, w_glu, glu_sem)
+    out_copy.start()
+    glu_copy.start()
     heads = mixed.shape[0]
     for pair in range(heads // 2):
         flipped = jnp.concatenate([mixed[2 * pair], mixed[2 * pair + 1]], axis=0).astype(jnp.float32)
         attended[:, pair * LANES : (pair + 1) * LANES] = flipped.T.astype(jnp.bfloat16)
-    wait_all(out_copies)
+    out_copy.wait()
     projected = jnp.dot(attended[...], w_out[...], preferred_element_type=jnp.float32)
     residual = (frames[...].astype(jnp.float32) + projected).astype(jnp.bfloat16)
     residual_ref[...] = residual
     width = frames.shape[1]
     conv_in = normalize(residual.astype(jnp.float32), gain[0:1, :]).astype(jnp.bfloat16)
-    wait_all(glu_copies)
+    glu_copy.wait()
     step = 256
     for j in range(0, width, step):
         a = jnp.dot(conv_in, w_glu[:, j : j + step], preferred_element_type=jnp.float32)
@@ -295,10 +288,10 @@
             pltpu.VMEM(w_out.shape, jnp.bfloat16),
             pltpu.VMEM(w_glu.shape, jnp.bfloat16),
             pltpu.VMEM(frames.shape, jnp.bfloat16),
-            pltpu.SemaphoreType.DMA((PIECE_COUNT,)),
-            pltpu.SemaphoreType.DMA((PIECE_COUNT,)),
+            pltpu.SemaphoreType.DMA,
+            pltpu.SemaphoreType.DMA,
         ],
-        compiler_params=pltpu.CompilerParams(vmem_limit_bytes=58 * 1024 * 1024),
+        compiler_params=pltpu.CompilerParams(vmem_limit_bytes=24 * 1024 * 1024),
     )(mixed, frames, gain, w_out, w_glu)
 
 
@@ -321,8 +314,7 @@
     return totals
 
 
-def inner_kernel(me, start_ref, end_ref, gated_hbm, weights, out, padded, gated, sems):
-    wait_all(copy_rows(gated_hbm, gated, sems))
+def inner_kernel(me, start_ref, end_ref, gated, weights, out, padded):
     rows, width = gated.shape
     for c in range(width // LANES):
         padded[c, :RIM] = jnp.zeros((RIM, LANES), jnp.float32)
@@ -355,22 +347,19 @@
     return pl.pallas_call(
         inner_kernel,
         out_shape=jax.ShapeDtypeStruct(gated.shape, jnp.float32),
-        in_specs=[SMEM] * 3 + [HBM, VMEM],
+        in_specs=[SMEM] * 3 + [VMEM] * 2,
         out_specs=VMEM,
-        scratch_shapes=[
-            pltpu.VMEM((width // LANES, rows + 2 * RIM, LANES), jnp.float32),
-            pltpu.VMEM(gated.shape, jnp.bfloat16),
-            pltpu.SemaphoreType.DMA((PIECE_COUNT,)),
-        ],
-        compiler_params=pltpu.CompilerParams(vmem_limit_bytes=60 * 1024 * 1024),
+        scratch_shapes=[pltpu.VMEM((width // LANES, rows + 2 * RIM, LANES), jnp.float32)],
+        compiler_params=pltpu.CompilerParams(vmem_limit_bytes=16 * 1024 * 1024),
     )(me, starts, ends, gated, weights)
 
 
 def last_kernel(
-    me, start_ref, end_ref, inner, left, right, residual_hbm, weights, gain, w_proj_hbm, out, *scratch
+    me, start_ref, end_ref, inner, left, right, residual, weights, gain, w_proj_hbm, out, *scratch
 ):
-    w_proj, residual, total, edge, sems, residual_sems = scratch
-    copies = copy_rows(w_proj_hbm, w_proj, sems) + copy_rows(residual_hbm, residual, residual_sems)
+    w_proj, total, edge, sem = scratch
+    copy = pltpu.make_async_copy(w_proj_hbm, w_proj, sem)
+    copy.start()
     rows, width = inner.shape
     total[...] = inner[...]
     count = weights.shape[0]
@@ -389,7 +378,7 @@
             total[row : row + ROWS, lanes] = total[row : row + ROWS, lanes] + part
     normed = normalize(total[...], gain[0:1, :])
     activated = (normed * jax.nn.sigmoid(normed)).astype(jnp.bfloat16)
-    wait_all(copies)
+    copy.wait()
     projected = jnp.dot(activated, w_proj[...], preferred_element_type=jnp.float32)
     out[...] = (residual[...].astype(jnp.float32) + projected).astype(jnp.bfloat16)
 
@@ -399,17 +388,15 @@
     return pl.pallas_call(
         last_kernel,
         out_shape=jax.ShapeDtypeStruct(residual.shape, jnp.bfloat16),
-        in_specs=[SMEM] * 3 + [VMEM] * 3 + [HBM] + [VMEM] * 2 + [HBM],
+        in_specs=[SMEM] * 3 + [VMEM] * 6 + [HBM],
         out_specs=VMEM,
         scratch_shapes=[
             pltpu.VMEM(w_proj.shape, jnp.bfloat16),
-            pltpu.VMEM(residual.shape, jnp.bfloat16),
             pltpu.VMEM(inner.shape, jnp.float32),
             pltpu.VMEM((width // LANES, 3 * RIM, LANES), jnp.float32),
-            pltpu.SemaphoreType.DMA((PIECE_COUNT,)),
-            pltpu.SemaphoreType.DMA((PIECE_COUNT,)),
+            pltpu.SemaphoreType.DMA,
         ],
-        compiler_params=pltpu.CompilerParams(vmem_limit_bytes=58 * 1024 * 1024),
+        compiler_params=pltpu.CompilerParams(vmem_limit_bytes=24 * 1024 * 1024),
     )(me, starts, ends, inner, left, right, residual, weights, gain, w_proj)
 
 
@@ -436,11 +423,16 @@
     swap = lambda x, yh, c, z, yl: (x, yh, 1 - c, z, yl)
     across = lambda x, yh, c, z, yl: (x, yh, c, z, 1 - yl)
     near = [send(shard, route(o)) for o in OFFSETS]
-    other_frames = send(local_frames, across)
+    own = norm(local_frames, attn_gain[None, :])
+    other = send(own, across)
     far = [send(piece, swap) for piece in near]
-    key_value, *queries = project_qkv(me, local_frames, other_frames, attn_gain[None, :], near + far)
+    stream = (me, own, other, near + far)
+    (key_value,) = project(key_value_kernel, [(8, 2 * frame_rows, LANES)], [], *stream)
+    piece = (frame_rows, LANES)
+    queries = project(query_kernel, [piece] * 8, [(8,) + piece], *stream)
     groups = [[2 * z + yl for z in range(8)] for yl in range(2)]
     key_value = lax.all_to_all(key_value, "blk", 0, 0, axis_index_groups=groups, tiled=True)
+    queries = list(queries)
     for d in SEND_ORDER:
         queries[d] = send(queries[d], lambda x, yh, c, z, yl: (x, yh, c, z + d, yl))
     ends = jnp.cumsum(utt_lengths)

time: 151 us -> 137 us (0.907)
  Pallas kernels: 48.2 us -> 39.8 us
  waiting for transfers between devices: 19.6 us -> 11.3 us
  local copies, waits for them, and re-layouts: 2.2 us -> 7.39 us
  starting transfers between devices: 58.7 us -> 56.4 us
    ppermute x18, waiting for transfers between devices: 19.6 us -> 11.3 us  [send(): return lax.ppermute(value, ('blk', 'grp'), pairs)]
    unnamed x44 -> x40, local copies, waits for them, and re-layouts: 0.71 us -> 7.25 us
    pallas_call x1, Pallas kernels: 6.81 us -> 2.92 us  [gate(): pl.pallas_call(gate_kernel, out_shape=[shape, shape], in_specs=[VMEM] * 3...]
    pallas_call x1, Pallas kernels: 6.6 us -> 4.1 us  [convolve_inner(): pl.pallas_call(inner_kernel, out_shape=jax.ShapeDtypeStruct(gated.shape,...]
    ppermute x18, starting transfers between devices: 50.1 us -> 47.9 us  [send(): return lax.ppermute(value, ('blk', 'grp'), pairs)]
    pallas_call x1, Pallas kernels: 4.63 us -> 2.87 us  [finish_block(): pl.pallas_call(last_kernel, out_shape=jax.ShapeDtypeStruct(residual.shape...]
    pallas_call x1 -> x3, Pallas kernels: 8.78 us -> 8.57 us  [the longest x2 8.21 us: project(): pl.pallas_call(kernel, out_shape=[jax.ShapeDtypeStruct(shape, jnp.bfloat1...]
  transfers between devices with their start and end apart: 19 -> 19, of which waited for: 4 -> 4; matrix products, arithmetic and copies ran while one was open for 1% -> 0% of each run, Pallas kernels for 11% -> 12%
where the time goes in v5:
time: 137 us; the launch traced here: 136 us
  starting transfers between devices  56.4 us (41%)
  Pallas kernels  39.8 us (29%)
  blocking collectives  20.6 us (15%)
  waiting for transfers between devices  11.3 us (8%)
  local copies, waits for them, and re-layouts  7.39 us (5%)
    ppermute x18, starting transfers between devices, send(): return lax.ppermute(value, ('blk', 'grp'), pairs)  47.9 us
    pallas_call x2, Pallas kernels, attend(): pl.pallas_call(functools.partial(attend_kernel, pieces), out_shape=jax.Sh...  21.3 us
    all_to_all x1, blocking collectives, body(): mixed = lax.all_to_all(mixed, 'blk', 0, 0, tiled=True)  20.6 us
    ppermute x18, waiting for transfers between devices, send(): return lax.ppermute(value, ('blk', 'grp'), pairs)  11.3 us
    all_to_all x1, starting transfers between devices, body(): lax.all_to_all(key_value, 'blk', 0, 0, axis_index_groups=groups, tiled=True)  8.48 us
    pallas_call x2, Pallas kernels, project(): pl.pallas_call(kernel, out_shape=[jax.ShapeDtypeStruct(shape, jnp.bfloat1...  8.21 us
    unnamed x40, local copies, waits for them, and re-layouts  7.25 us
    pallas_call x1, Pallas kernels, convolve_inner(): pl.pallas_call(inner_kernel, out_shape=jax.ShapeDtypeStruct(gated.shape,...  4.1 us
  transfers between devices with their start and end apart: 19, of which 4 were waited for; matrix products, arithmetic and copies ran while one was open for 0% of the time, Pallas kernels for 12%

profile of v5, /device:TPU:6, one launch (start us, length us, event | category | flops | bytes accessed | tf_op | source)
XLA Modules:
  0.0 136.0 jit_solution(14804651448140045709)
XLA Ops:
  0.0 1.6 %collective-permute-start.1 = (bf16[192,1024]{1,0:T(8,128)(2,1)}, bf16[192,1024]{1,0:T(8,128)(2,1)S(1)}, u32[]{:S(2)}, u32[]{:S(2)}) collective-permute-start(bf16[192,1024]{1,0:T(8,128)(2,1)} %bitcast.24), channel_id=1, source_target_pairs={{0,0},{1,18},{2,3},{3,17},{4,4},{5,22},{6,7},{7,21},{8,8},{9,26},{... | collective-permute-start | bytes 1179656 | tf_op jit(solution)/shard_map/ppermute | solution.py:45
  1.6 0.8 collective-permute-start.2
  2.5 2.4 %collective-permute-start.3 = (bf16[192,1024]{1,0:T(8,128)(2,1)}, bf16[192,1024]{1,0:T(8,128)(2,1)S(1)}, u32[]{:S(2)}, u32[]{:S(2)}) collective-permute-start(bf16[192,1024]{1,0:T(8,128)(2,1)} %bitcast.26), channel_id=1, source_target_pairs={{0,4},{1,22},{2,7},{3,21},{4,8},{5,26},{6,11},{7,25},{8,12},{9,30}... | collective-permute-start | bytes 1179656 | tf_op jit(solution)/shard_map/ppermute | solution.py:45
  5.3 1.0 copy-done.2
  6.3 0.7 copy-done.12
  7.4 2.5 %collective-permute-start = (bf16[256,1024]{1,0:T(8,128)(2,1)S(1)}, bf16[256,1024]{1,0:T(8,128)(2,1)S(1)}, u32[]{:S(2)}, u32[]{:S(2)}) collective-permute-start(bf16[256,1024]{1,0:T(8,128)(2,1)S(1)} %shard_map.100.own), channel_id=1, source_target_pairs={{0,16},{1,17},{2,18},{3,19},{4,20},{5,21},{6,22},{7,23},{8,24},{9,... | collective-permute-start | bytes 1572872 | tf_op jit(solution)/shard_map/ppermute | solution.py:45
  9.9 11.7 %collective-permute-start.5 = (bf16[192,1024]{1,0:T(8,128)(2,1)S(1)}, bf16[192,1024]{1,0:T(8,128)(2,1)S(1)}, u32[]{:S(2)}, u32[]{:S(2)}) collective-permute-start(bf16[192,1024]{1,0:T(8,128)(2,1)S(1)} %collective-permute-done.1.refs_0_), channel_id=1, source_target_pairs={{0,1},{1,0},{2,3},{3,2},{4,5},{5,4},{6,7},{7,6},{8,9},{9,8},{10,11... | collective-permute-start | bytes 1179656 | tf_op jit(solution)/shard_map/ppermute | solution.py:45
  21.6 3.0 %collective-permute-start.6 = (bf16[192,1024]{1,0:T(8,128)(2,1)S(1)}, bf16[192,1024]{1,0:T(8,128)(2,1)}, u32[]{:S(2)}, u32[]{:S(2)}) collective-permute-start(bf16[192,1024]{1,0:T(8,128)(2,1)S(1)} %collective-permute-done.2.refs_1_), channel_id=1, source_target_pairs={{0,1},{1,0},{2,3},{3,2},{4,5},{5,4},{6,7},{7,6},{8,9},{9,8},{10,11... | collective-permute-start | bytes 1179656 | tf_op jit(solution)/shard_map/ppermute | solution.py:45
  25.2 0.9 collective-permute-done.6.refs_5_
  27.2 4.8 %shard_map.101 = bf16[8,512,128]{2,1,0:T(8,128)(2,1)} custom-call(s32[6]{0:T(128)S(1)} %stack.27.me, bf16[256,1024]{1,0:T(8,128)(2,1)S(1)} %shard_map.100.own, bf16[256,1024]{1,0:T(8,128)(2,1)S(1)} %collective-permute-done.other, bf16[192,1024]{1,0:T(8,128)(2,1)S(1)} %collective-permute-done.1.refs_0_, bf16[192,1024]{1,0:T(8,128)(2,1)S(1)} %collective-permute-done.2.refs_1_, ...), custom_call_target="tpu_custom_call" | custom-call | tf_op jit(solution)/shard_map/pallas_call | solution.py:137
  32.0 8.5 %all-to-all-start = ((bf16[8,512,128]{2,1,0:T(8,128)(2,1)}), bf16[8,512,128]{2,1,0:T(8,128)(2,1)S(1)}, u32[]{:S(2)}, u32[]{:S(2)}) async-start(bf16[8,512,128]{2,1,0:T(8,128)(2,1)} %shard_map.101), calls=%async_computation | async-start | bytes 2097152 | tf_op jit(solution)/shard_map/all_to_all | solution.py:434
  40.5 1.0 copy-done.6
  41.5 1.0 copy-done.8
  42.5 1.0 copy-done.10
  43.5 3.4 %shard_map.102 = (bf16[256,128]{1,0:T(8,128)(2,1)S(1)}, bf16[256,128]{1,0:T(8,128)(2,1)}, bf16[256,128]{1,0:T(8,128)(2,1)S(1)}, bf16[256,128]{1,0:T(8,128)(2,1)S...) custom-call(s32[6]{0:T(128)S(1)} %stack.27.me, ...), custom_call_target="tpu_custom_call" | custom-call | tf_op jit(solution)/shard_map/pallas_call | solution.py:137
  46.9 0.6 copy-done.15
  48.8 0.6 copy-done.18
  49.4 3.2 %collective-permute-start.10 = (bf16[256,128]{1,0:T(8,128)(2,1)}, bf16[256,128]{1,0:T(8,128)(2,1)S(1)}, u32[]{:S(2)}, u32[]{:S(2)}) collective-permute-start(bf16[256,128]{1,0:T(8,128)(2,1)} %get-tuple-element.17), channel_id=1, source_target_pairs={{0,224},{1,225},{2,226},{3,227},{4,228},{5,229},{6,230},{7,231},{8... | collective-permute-start | bytes 196616 | tf_op jit(solution)/shard_map/ppermute | solution.py:45
  52.8 1.7 %collective-permute-start.11 = (bf16[256,128]{1,0:T(8,128)(2,1)}, bf16[256,128]{1,0:T(8,128)(2,1)S(1)}, u32[]{:S(2)}, u32[]{:S(2)}) collective-permute-start(bf16[256,128]{1,0:T(8,128)(2,1)} %copy-done.18), channel_id=1, source_target_pairs={{0,64},{1,65},{2,66},{3,67},{4,68},{5,69},{6,70},{7,71},{8,72},{9,... | collective-permute-start | bytes 196616 | tf_op jit(solution)/shard_map/ppermute | solution.py:45
  54.5 2.4 %collective-permute-start.12 = (bf16[256,128]{1,0:T(8,128)(2,1)}, bf16[256,128]{1,0:T(8,128)(2,1)S(1)}, u32[]{:S(2)}, u32[]{:S(2)}) collective-permute-start(bf16[256,128]{1,0:T(8,128)(2,1)} %copy-done.17), channel_id=1, source_target_pairs={{0,192},{1,193},{2,194},{3,195},{4,196},{5,197},{6,198},{7,199},{8... | collective-permute-start | bytes 196616 | tf_op jit(solution)/shard_map/ppermute | solution.py:45
  57.0 2.6 %collective-permute-start.13 = (bf16[256,128]{1,0:T(8,128)(2,1)}, bf16[256,128]{1,0:T(8,128)(2,1)S(1)}, u32[]{:S(2)}, u32[]{:S(2)}) collective-permute-start(bf16[256,128]{1,0:T(8,128)(2,1)} %copy-done.16), channel_id=1, source_target_pairs={{0,96},{1,97},{2,98},{3,99},{4,100},{5,101},{6,102},{7,103},{8,104... | collective-permute-start | bytes 196616 | tf_op jit(solution)/shard_map/ppermute | solution.py:45
  59.6 9.3 %collective-permute-done.10.refs_2_ = bf16[256,128]{1,0:T(8,128)(2,1)S(1)} collective-permute-done((bf16[256,128]{1,0:T(8,128)(2,1)}, bf16[256,128]{1,0:T(8,128)(2,1)S(1)}, u32[]{:S(2)}, u32[]{:S(2)}) %collective-permute-start.10) | collective-permute-done | bytes 65568 | tf_op jit(solution)/shard_map/ppermute | solution.py:45
  68.8 3.1 %collective-permute-start.14 = (bf16[256,128]{1,0:T(8,128)(2,1)}, bf16[256,128]{1,0:T(8,128)(2,1)S(1)}, u32[]{:S(2)}, u32[]{:S(2)}) collective-permute-start(bf16[256,128]{1,0:T(8,128)(2,1)} %copy-done.15), channel_id=1, source_target_pairs={{0,160},{1,161},{2,162},{3,163},{4,164},{5,165},{6,166},{7,167},{8... | collective-permute-start | bytes 196616 | tf_op jit(solution)/shard_map/ppermute | solution.py:45
  71.9 2.1 %collective-permute-start.15 = (bf16[256,128]{1,0:T(8,128)(2,1)S(1)}, bf16[256,128]{1,0:T(8,128)(2,1)S(1)}, u32[]{:S(2)}, u32[]{:S(2)}) collective-permute-start(bf16[256,128]{1,0:T(8,128)(2,1)S(1)} %get-tuple-element.22), channel_id=1, source_target_pairs={{0,128},{1,129},{2,130},{3,131},{4,132},{5,133},{6,134},{7,135},{8... | collective-permute-start | bytes 196616 | tf_op jit(solution)/shard_map/ppermute | solution.py:45
  74.1 8.6 %shard_map.103.before = bf16[16,64,256]{2,1,0:T(8,128)(2,1)S(1)} custom-call(s32[6]{0:T(128)S(1)} %stack.27.me, s32[8]{0:T(128)S(1)} %bitcast_subtract_fusion.start_ref, s32[8]{0:T(128)S(1)} %bitcast.17, bf16[8,512,128]{2,1,0:T(8,128)(2,1)S(1)} %all-to-all-done.in_ref, bf16[16,64,256]{2,1,0:T(8,128)(2,1)S(1)} %broadcast_in_dim.16.before, ...), custom_call_target="tpu_custom_call" | custom-call | tf_op jit(solution)/shard_map/pallas_call | solution.py:238
  82.7 12.8 %shard_map.104 = bf16[16,64,256]{2,1,0:T(8,128)(2,1)S(1)} custom-call(s32[6]{0:T(128)S(1)} %stack.27.me, s32[8]{0:T(128)S(1)} %bitcast_subtract_fusion.start_ref, s32[8]{0:T(128)S(1)} %bitcast.18, bf16[8,512,128]{2,1,0:T(8,128)(2,1)S(1)} %all-to-all-done.in_ref, bf16[16,64,256]{2,1,0:T(8,128)(2,1)S(1)} %shard_map.103.before, ...), custom_call_target="tpu_custom_call" | custom-call | tf_op jit(solution)/shard_map/pallas_call | solution.py:238
  95.5 20.6 %all_to_all.10.mixed = bf16[16,64,256]{2,1,0:T(8,128)(2,1)S(1)} all-to-all(bf16[16,64,256]{2,1,0:T(8,128)(2,1)S(1)} %shard_map.104), channel_id=1, replica_groups=mesh['blk'=16,'grp'=16] {'blk'}, dimensions={0} | all-to-all | bytes 1048576 | tf_op jit(solution)/shard_map/all_to_all | solution.py:444
  116.1 2.9 %shard_map.105 = (bf16[256,1024]{1,0:T(8,128)(2,1)S(1)}, bf16[256,1024]{1,0:T(8,128)(2,1)S(1)}) custom-call(bf16[16,64,256]{2,1,0:T(8,128)(2,1)S(1)} %all_to_all.10.mixed, bf16[256,1024]{1,0:T(8,128)(2,1)S(1)} %bitcast.16, f32[1,1024]{1,0:T(1,128)S(1)} %bitcast.22, bf16[1024,1024]{1,0:T(8,128)(2,1)S(1)} %copy-done.1, bf16[1024,2048]{1,0:T(8,128)(2,1)S(1)} %copy-done), custom_call_target="tpu_custom_call" | custom-call | tf_op jit(solution)/shard_map/pallas_call | solution.py:282
  119.1 2.2 %collective-permute-start.16 = (bf16[16,1024]{1,0:T(8,128)(2,1)S(1)}, bf16[16,1024]{1,0:T(8,128)(2,1)S(1)}, u32[]{:S(2)}, u32[]{:S(2)}) collective-permute-start(bf16[16,1024]{1,0:T(8,128)(2,1)S(1)} %get-tuple-element.26), channel_id=1, source_target_pairs={{0,16},{1,17},{2,18},{3,19},{4,20},{5,21},{6,22},{7,23},{8,24},{9,... | collective-permute-start | bytes 98312 | tf_op jit(solution)/shard_map/ppermute | solution.py:45
  121.3 7.6 %collective-permute-start.17 = (bf16[16,1024]{1,0:T(8,128)(2,1)S(1)}, bf16[16,1024]{1,0:T(8,128)(2,1)S(1)}, u32[]{:S(2)}, u32[]{:S(2)}) collective-permute-start(bf16[16,1024]{1,0:T(8,128)(2,1)S(1)} %get-tuple-element.25), channel_id=1, source_target_pairs={{1,240},{2,241},{3,242},{4,243},{5,244},{6,245},{7,246},{8,247},{9... | collective-permute-start | bytes 98312 | tf_op jit(solution)/shard_map/ppermute | solution.py:45
  128.9 4.1 %shard_map.106.inner = f32[256,1024]{1,0:T(8,128)S(1)} custom-call(s32[6]{0:T(128)S(1)} %stack.27.me, s32[8]{0:T(128)S(1)} %bitcast_subtract_fusion.start_ref, s32[8]{0:T(128)S(1)} %bitcast.19, bf16[256,1024]{1,0:T(8,128)(2,1)S(1)} %get-tuple-element.23.gated, f32[31,1024]{1,0:T(8,128)S(1)} %copy-done.11), custom_call_target="tpu_custom_call" | custom-call | tf_op jit(solution)/shard_map/pallas_call | solution.py:347
  133.0 2.9 %shard_map.107 = bf16[256,1024]{1,0:T(8,128)(2,1)} custom-call(s32[6]{0:T(128)S(1)} %stack.27.me, s32[8]{0:T(128)S(1)} %bitcast_subtract_fusion.start_ref, s32[8]{0:T(128)S(1)} %bitcast.20, f32[256,1024]{1,0:T(8,128)S(1)} %shard_map.106.inner, bf16[16,1024]{1,0:T(8,128)(2,1)S(1)} %collective-permute-done.16.left, ...), custom_call_target="tpu_custom_call" | custom-call | tf_op jit(solution)/shard_map/pallas_call | solution.py:388
  (60 shorter events, 4.1 us)
Async XLA Ops:
  0.0 9.9 %collective-permute-start.1 = (bf16[192,1024]{1,0:T(8,128)(2,1)}, bf16[192,1024]{1,0:T(8,128)(2,1)S(1)}, u32[]{:S(2)}, u32[]{:S(2)}) collective-permute-start(bf16[192,1024]{1,0:T(8,128)(2,1)} %bitcast.24), channel_id=1, source_target_pairs={{0,0},{1,18},{2,3},{3,17},{4,4},{5,22},{6,7},{7,21},{8,8},{9,26},{... | collective-permute-start | bytes 1179656 | tf_op jit(solution)/shard_map/ppermute | solution.py:45
  1.6 20.0 %collective-permute-start.2 = (bf16[192,1024]{1,0:T(8,128)(2,1)}, bf16[192,1024]{1,0:T(8,128)(2,1)S(1)}, u32[]{:S(2)}, u32[]{:S(2)}) collective-permute-start(bf16[192,1024]{1,0:T(8,128)(2,1)} %bitcast.25), channel_id=1, source_target_pairs={{0,12},{1,30},{2,15},{3,29},{4,0},{5,18},{6,3},{7,17},{8,4},{9,22}... | collective-permute-start | bytes 1179656 | tf_op jit(solution)/shard_map/ppermute | solution.py:45
  2.5 22.1 %collective-permute-start.3 = (bf16[192,1024]{1,0:T(8,128)(2,1)}, bf16[192,1024]{1,0:T(8,128)(2,1)S(1)}, u32[]{:S(2)}, u32[]{:S(2)}) collective-permute-start(bf16[192,1024]{1,0:T(8,128)(2,1)} %bitcast.26), channel_id=1, source_target_pairs={{0,4},{1,22},{2,7},{3,21},{4,8},{5,26},{6,11},{7,25},{8,12},{9,30}... | collective-permute-start | bytes 1179656 | tf_op jit(solution)/shard_map/ppermute | solution.py:45
  4.9 19.8 %collective-permute-start.4 = (bf16[192,1024]{1,0:T(8,128)(2,1)}, bf16[192,1024]{1,0:T(8,128)(2,1)S(1)}, u32[]{:S(2)}, u32[]{:S(2)}) collective-permute-start(bf16[192,1024]{1,0:T(8,128)(2,1)} %bitcast.27), channel_id=1, source_target_pairs={{0,8},{1,26},{2,11},{3,25},{4,12},{5,30},{6,15},{7,29},{8,0},{9,18... | collective-permute-start | bytes 1179656 | tf_op jit(solution)/shard_map/ppermute | solution.py:45
  5.3 1.0 copy-start.2
  7.4 17.8 %collective-permute-start = (bf16[256,1024]{1,0:T(8,128)(2,1)S(1)}, bf16[256,1024]{1,0:T(8,128)(2,1)S(1)}, u32[]{:S(2)}, u32[]{:S(2)}) collective-permute-start(bf16[256,1024]{1,0:T(8,128)(2,1)S(1)} %shard_map.100.own), channel_id=1, source_target_pairs={{0,16},{1,17},{2,18},{3,19},{4,20},{5,21},{6,22},{7,23},{8,24},{9,... | collective-permute-start | bytes 1572872 | tf_op jit(solution)/shard_map/ppermute | solution.py:45
  9.9 15.3 %collective-permute-start.5 = (bf16[192,1024]{1,0:T(8,128)(2,1)S(1)}, bf16[192,1024]{1,0:T(8,128)(2,1)S(1)}, u32[]{:S(2)}, u32[]{:S(2)}) collective-permute-start(bf16[192,1024]{1,0:T(8,128)(2,1)S(1)} %collective-permute-done.1.refs_0_), channel_id=1, source_target_pairs={{0,1},{1,0},{2,3},{3,2},{4,5},{5,4},{6,7},{7,6},{8,9},{9,8},{10,11... | collective-permute-start | bytes 1179656 | tf_op jit(solution)/shard_map/ppermute | solution.py:45
  21.6 4.5 %collective-permute-start.6 = (bf16[192,1024]{1,0:T(8,128)(2,1)S(1)}, bf16[192,1024]{1,0:T(8,128)(2,1)}, u32[]{:S(2)}, u32[]{:S(2)}) collective-permute-start(bf16[192,1024]{1,0:T(8,128)(2,1)S(1)} %collective-permute-done.2.refs_1_), channel_id=1, source_target_pairs={{0,1},{1,0},{2,3},{3,2},{4,5},{5,4},{6,7},{7,6},{8,9},{9,8},{10,11... | collective-permute-start | bytes 1179656 | tf_op jit(solution)/shard_map/ppermute | solution.py:45
  24.6 7.4 %copy-start.5 = (bf16[192,1024]{1,0:T(8,128)(2,1)}, bf16[192,1024]{1,0:T(8,128)(2,1)S(1)}, u32[]{:S(2)}) copy-start(bf16[192,1024]{1,0:T(8,128)(2,1)S(1)} %collective-permute-done.3.refs_2_) | copy-start | bytes 1179652
  24.6 2.0 %collective-permute-start.7 = (bf16[192,1024]{1,0:T(8,128)(2,1)S(1)}, bf16[192,1024]{1,0:T(8,128)(2,1)}, u32[]{:S(2)}, u32[]{:S(2)}) collective-permute-start(bf16[192,1024]{1,0:T(8,128)(2,1)S(1)} %collective-permute-done.3.refs_2_), channel_id=1, source_target_pairs={{0,1},{1,0},{2,3},{3,2},{4,5},{5,4},{6,7},{7,6},{8,9},{9,8},{10,11... | collective-permute-start | bytes 1179656 | tf_op jit(solution)/shard_map/ppermute | solution.py:45
  24.7 7.3 %copy-start.7 = (bf16[192,1024]{1,0:T(8,128)(2,1)}, bf16[192,1024]{1,0:T(8,128)(2,1)S(1)}, u32[]{:S(2)}) copy-start(bf16[192,1024]{1,0:T(8,128)(2,1)S(1)} %collective-permute-done.4.refs_3_) | copy-start | bytes 1179652
  24.7 2.5 %collective-permute-start.8 = (bf16[192,1024]{1,0:T(8,128)(2,1)S(1)}, bf16[192,1024]{1,0:T(8,128)(2,1)}, u32[]{:S(2)}, u32[]{:S(2)}) collective-permute-start(bf16[192,1024]{1,0:T(8,128)(2,1)S(1)} %collective-permute-done.4.refs_3_), channel_id=1, source_target_pairs={{0,1},{1,0},{2,3},{3,2},{4,5},{5,4},{6,7},{7,6},{8,9},{9,8},{10,11... | collective-permute-start | bytes 1179656 | tf_op jit(solution)/shard_map/ppermute | solution.py:45
  25.2 6.8 %copy-start.9 = (bf16[192,1024]{1,0:T(8,128)(2,1)}, bf16[192,1024]{1,0:T(8,128)(2,1)S(1)}, u32[]{:S(2)}) copy-start(bf16[192,1024]{1,0:T(8,128)(2,1)S(1)} %collective-permute-done.5.refs_4_) | copy-start | bytes 1179652
  32.0 42.0 %all-to-all-start = ((bf16[8,512,128]{2,1,0:T(8,128)(2,1)}), bf16[8,512,128]{2,1,0:T(8,128)(2,1)S(1)}, u32[]{:S(2)}, u32[]{:S(2)}) async-start(bf16[8,512,128]{2,1,0:T(8,128)(2,1)} %shard_map.101), calls=%async_computation | async-start | bytes 2097152 | tf_op jit(solution)/shard_map/all_to_all | solution.py:434
  40.5 1.0 copy-start.6
  43.5 9.2 %copy-start.19 = (s32[8]{0:T(128)S(1)}, s32[8]{0:T(128)}, u32[]{:S(2)}) copy-start(s32[8]{0:T(128)} %param.11) | copy-start | bytes 100
  43.5 72.6 %copy-start.3 = (bf16[1,256,1024]{2,1,0:T(8,128)(2,1)S(1)}, bf16[1,256,1024]{2,1,0:T(8,128)(2,1)}, u32[]{:S(2)}) copy-start(bf16[1,256,1024]{2,1,0:T(8,128)(2,1)} %param.10) | copy-start | bytes 1572868
  49.4 19.4 %collective-permute-start.10 = (bf16[256,128]{1,0:T(8,128)(2,1)}, bf16[256,128]{1,0:T(8,128)(2,1)S(1)}, u32[]{:S(2)}, u32[]{:S(2)}) collective-permute-start(bf16[256,128]{1,0:T(8,128)(2,1)} %get-tuple-element.17), channel_id=1, source_target_pairs={{0,224},{1,225},{2,226},{3,227},{4,228},{5,229},{6,230},{7,231},{8... | collective-permute-start | bytes 196616 | tf_op jit(solution)/shard_map/ppermute | solution.py:45
  52.6 19.3 %collective-permute-start.9 = (bf16[256,128]{1,0:T(8,128)(2,1)}, bf16[256,128]{1,0:T(8,128)(2,1)S(1)}, u32[]{:S(2)}, u32[]{:S(2)}) collective-permute-start(bf16[256,128]{1,0:T(8,128)(2,1)} %get-tuple-element.16), channel_id=1, source_target_pairs={{0,32},{1,33},{2,34},{3,35},{4,36},{5,37},{6,38},{7,39},{8,40},{9,... | collective-permute-start | bytes 196616 | tf_op jit(solution)/shard_map/ppermute | solution.py:45
  52.8 29.8 %collective-permute-start.11 = (bf16[256,128]{1,0:T(8,128)(2,1)}, bf16[256,128]{1,0:T(8,128)(2,1)S(1)}, u32[]{:S(2)}, u32[]{:S(2)}) collective-permute-start(bf16[256,128]{1,0:T(8,128)(2,1)} %copy-done.18), channel_id=1, source_target_pairs={{0,64},{1,65},{2,66},{3,67},{4,68},{5,69},{6,70},{7,71},{8,72},{9,... | collective-permute-start | bytes 196616 | tf_op jit(solution)/shard_map/ppermute | solution.py:45
  54.5 28.1 %collective-permute-start.12 = (bf16[256,128]{1,0:T(8,128)(2,1)}, bf16[256,128]{1,0:T(8,128)(2,1)S(1)}, u32[]{:S(2)}, u32[]{:S(2)}) collective-permute-start(bf16[256,128]{1,0:T(8,128)(2,1)} %copy-done.17), channel_id=1, source_target_pairs={{0,192},{1,193},{2,194},{3,195},{4,196},{5,197},{6,198},{7,199},{8... | collective-permute-start | bytes 196616 | tf_op jit(solution)/shard_map/ppermute | solution.py:45
  57.0 25.7 %collective-permute-start.13 = (bf16[256,128]{1,0:T(8,128)(2,1)}, bf16[256,128]{1,0:T(8,128)(2,1)S(1)}, u32[]{:S(2)}, u32[]{:S(2)}) collective-permute-start(bf16[256,128]{1,0:T(8,128)(2,1)} %copy-done.16), channel_id=1, source_target_pairs={{0,96},{1,97},{2,98},{3,99},{4,100},{5,101},{6,102},{7,103},{8,104... | collective-permute-start | bytes 196616 | tf_op jit(solution)/shard_map/ppermute | solution.py:45
  68.8 13.8 %collective-permute-start.14 = (bf16[256,128]{1,0:T(8,128)(2,1)}, bf16[256,128]{1,0:T(8,128)(2,1)S(1)}, u32[]{:S(2)}, u32[]{:S(2)}) collective-permute-start(bf16[256,128]{1,0:T(8,128)(2,1)} %copy-done.15), channel_id=1, source_target_pairs={{0,160},{1,161},{2,162},{3,163},{4,164},{5,165},{6,166},{7,167},{8... | collective-permute-start | bytes 196616 | tf_op jit(solution)/shard_map/ppermute | solution.py:45
  71.9 10.8 %collective-permute-start.15 = (bf16[256,128]{1,0:T(8,128)(2,1)S(1)}, bf16[256,128]{1,0:T(8,128)(2,1)S(1)}, u32[]{:S(2)}, u32[]{:S(2)}) collective-permute-start(bf16[256,128]{1,0:T(8,128)(2,1)S(1)} %get-tuple-element.22), channel_id=1, source_target_pairs={{0,128},{1,129},{2,130},{3,131},{4,132},{5,133},{6,134},{7,135},{8... | collective-permute-start | bytes 196616 | tf_op jit(solution)/shard_map/ppermute | solution.py:45
  74.0 42.1 %copy-start.1 = (bf16[1024,1024]{1,0:T(8,128)(2,1)S(1)}, bf16[1024,1024]{1,0:T(8,128)(2,1)}, u32[]{:S(2)}) copy-start(bf16[1024,1024]{1,0:T(8,128)(2,1)} %w_out_hbm.1) | copy-start | bytes 6291460
  74.1 42.0 %copy-start = (bf16[1024,2048]{1,0:T(8,128)(2,1)S(1)}, bf16[1024,2048]{1,0:T(8,128)(2,1)}, u32[]{:S(2)}) copy-start(bf16[1024,2048]{1,0:T(8,128)(2,1)} %w_glu_hbm.1) | copy-start | bytes 12582916
  82.6 33.4 %copy-start.13 = (f32[1024]{0:T(1024)S(1)}, f32[1024]{0:T(1024)}, u32[]{:S(2)}) copy-start(f32[1024]{0:T(1024)} %param.15) | copy-start | bytes 12292
  116.1 12.8 %copy-start.11 = (f32[31,1024]{1,0:T(8,128)S(1)}, f32[31,1024]{1,0:T(8,128)}, u32[]{:S(2)}) copy-start(f32[31,1024]{1,0:T(8,128)} %weights.3) | copy-start | bytes 380932
  116.1 16.9 %copy-start.4 = (bf16[1024,1024]{1,0:T(8,128)(2,1)S(1)}, bf16[1024,1024]{1,0:T(8,128)(2,1)}, u32[]{:S(2)}) copy-start(bf16[1024,1024]{1,0:T(8,128)(2,1)} %w_proj_hbm.1) | copy-start | bytes 6291460
  116.1 16.9 %copy-start.14 = (f32[1024]{0:T(1024)S(1)}, f32[1024]{0:T(1024)}, u32[]{:S(2)}) copy-start(f32[1024]{0:T(1024)} %param.18) | copy-start | bytes 12292
  119.1 13.9 %collective-permute-start.16 = (bf16[16,1024]{1,0:T(8,128)(2,1)S(1)}, bf16[16,1024]{1,0:T(8,128)(2,1)S(1)}, u32[]{:S(2)}, u32[]{:S(2)}) collective-permute-start(bf16[16,1024]{1,0:T(8,128)(2,1)S(1)} %get-tuple-element.26), channel_id=1, source_target_pairs={{0,16},{1,17},{2,18},{3,19},{4,20},{5,21},{6,22},{7,23},{8,24},{9,... | collective-permute-start | bytes 98312 | tf_op jit(solution)/shard_map/ppermute | solution.py:45
  121.3 11.7 %collective-permute-start.17 = (bf16[16,1024]{1,0:T(8,128)(2,1)S(1)}, bf16[16,1024]{1,0:T(8,128)(2,1)S(1)}, u32[]{:S(2)}, u32[]{:S(2)}) collective-permute-start(bf16[16,1024]{1,0:T(8,128)(2,1)S(1)} %get-tuple-element.25), channel_id=1, source_target_pairs={{1,240},{2,241},{3,242},{4,243},{5,244},{6,245},{7,246},{8,247},{9... | collective-permute-start | bytes 98312 | tf_op jit(solution)/shard_map/ppermute | solution.py:45
  (7 other events, 5.2 us)

commit v6 on v5

--- a/solution.py
+++ b/solution.py
@@ -98,22 +98,55 @@
 
 
 def key_value_kernel(me, own, other, *refs):
-    shards, out, both_rows = refs[:8], refs[8], refs[9]
+    near, far_hbm, out_hbm, stream, far, out, sems, out_sems = refs[:4], refs[4:8], *refs[8:]
+    copies = [pltpu.make_async_copy(far_hbm[i], far.at[i], sems.at[i]) for i in range(4)]
+    for copy in copies:
+        copy.start()
     rows = own.shape[0]
-    both_rows[:rows] = own[...]
-    both_rows[rows:] = other[...]
+    stream[:rows] = own[...]
+    stream[rows:] = other[...]
     low = low_lanes(rows)
-    for i in range(0, 8, 2):
-        heads = shard_head(me, i), shard_head(me, i + 1)
-        weights = jnp.concatenate([shards[j][HEAD : 2 * HEAD, :] for j in (i, i + 1)], axis=0)
-        both = lax.dot_general(both_rows[...], weights, CONTRACT, preferred_element_type=jnp.float32)
-        mine, theirs = both[:rows], both[rows:]
-        out[heads[0], :rows] = jnp.where(low, mine, swap_lanes(theirs)).astype(jnp.bfloat16)
-        out[heads[1], :rows] = jnp.where(low, swap_lanes(mine), theirs).astype(jnp.bfloat16)
-        weights = jnp.concatenate([shards[j][2 * HEAD :, :] for j in (i, i + 1)], axis=0)
-        both = lax.dot_general(weights, both_rows[...], CONTRACT, preferred_element_type=jnp.float32)
-        transposed(out, heads[0], rows, both[:HEAD])
-        transposed(out, heads[1], rows, both[HEAD:])
+    leaving = []
+    for first, part in ((0, near), (4, [far.at[i] for i in range(4)])):
+        if first:
+            for copy in copies:
+                copy.wait()
+        heads = [shard_head(me, first + j) for j in range(4)]
+        weights = jnp.concatenate([shard[HEAD : 2 * HEAD, :] for shard in part], axis=0)
+        both = lax.dot_general(stream[...], weights, CONTRACT, preferred_element_type=jnp.float32)
+        for j in (0, 2):
+            pair = both[:, j * HEAD : (j + 2) * HEAD]
+            mine, theirs = pair[:rows], pair[rows:]
+            out[first + j, :rows] = jnp.where(low, mine, swap_lanes(theirs)).astype(jnp.bfloat16)
+            out[first + j + 1, :rows] = jnp.where(low, swap_lanes(mine), theirs).astype(jnp.bfloat16)
+        weights = jnp.concatenate([shard[2 * HEAD :, :] for shard in part], axis=0)
+        both = lax.dot_general(weights, stream[...], CONTRACT, preferred_element_type=jnp.float32)
+        for j in range(4):
+            i = first + j
+            transposed(out, i, rows, both[j * HEAD : (j + 1) * HEAD])
+            leaving.append(pltpu.make_async_copy(out.at[i], out_hbm.at[heads[j]], out_sems.at[i]))
+            leaving[-1].start()
+    for copy in leaving:
+        copy.wait()
+
+
+def project_key_value(me, own, other, shards):
+    rows, width = own.shape
+    shape = (8, 2 * rows, LANES)
+    return pl.pallas_call(
+        key_value_kernel,
+        out_shape=jax.ShapeDtypeStruct(shape, jnp.bfloat16),
+        in_specs=[SMEM] + [VMEM] * 6 + [HBM] * 4,
+        out_specs=HBM,
+        scratch_shapes=[
+            pltpu.VMEM((2 * rows, width), jnp.bfloat16),
+            pltpu.VMEM((4,) + shards[0].shape, jnp.bfloat16),
+            pltpu.VMEM(shape, jnp.bfloat16),
+            pltpu.SemaphoreType.DMA((4,)),
+            pltpu.SemaphoreType.DMA((8,)),
+        ],
+        compiler_params=pltpu.CompilerParams(vmem_limit_bytes=16 * 1024 * 1024),
+    )(me, own, other, *shards)
 
 
 def query_kernel(me, own, other, *refs):
@@ -121,13 +154,12 @@
     rows = own.shape[0]
     both_rows[:rows] = own[...]
     both_rows[rows:] = other[...]
-    for i in range(0, 8, 2):
-        weights = jnp.concatenate([shards[j][:HEAD, :] for j in (i, i + 1)], axis=0)
-        both = lax.dot_general(weights, both_rows[...], CONTRACT, preferred_element_type=jnp.float32)
-        both = both * (HEAD**-0.5 * LOG2E)
-        for j in range(2):
-            piece = lax.rem(shard_head(me, i + j) + 8 - me[Z], 8)
-            transposed(staged, piece, 0, both[j * HEAD : (j + 1) * HEAD])
+    weights = jnp.concatenate([shard[:HEAD, :] for shard in shards], axis=0)
+    both = lax.dot_general(weights, both_rows[...], CONTRACT, preferred_element_type=jnp.float32)
+    both = both * (HEAD**-0.5 * LOG2E)
+    for i in range(8):
+        piece = lax.rem(shard_head(me, i) + 8 - me[Z], 8)
+        transposed(staged, piece, 0, both[i * HEAD : (i + 1) * HEAD])
     for d in range(8):
         pieces[d][...] = staged[d]
 
@@ -209,6 +241,19 @@
         mixed = total[:HEAD] / total[HEAD : HEAD + 1]
         out_ref[origin(i)] = mixed.astype(jnp.bfloat16)
 
+    def keep(j, part, best):
+        scores[j * KEY_CHUNK : (j + 1) * KEY_CHUNK, :] = part
+        part = jnp.max(part.reshape(KEY_CHUNK // 8, 8, block), axis=0)
+        return part if best is None else jnp.maximum(best, part)
+
+    def settle(best):
+        most_ref[...] = jnp.broadcast_to(jnp.max(best, axis=0, keepdims=True), (8, block))
+
+    best = None
+    for j in range(chunks):
+        best = keep(j, score(queries[0], j), best)
+    settle(best)
+
     def step(i, carry):
         query = queries[i]
         most = most_ref[0:1, :]
@@ -216,15 +261,12 @@
         for j in range(chunks):
             part = weigh(j, most)
             total = part if total is None else total + part
-            part = score(query, j)
-            scores[j * KEY_CHUNK : (j + 1) * KEY_CHUNK, :] = part
-            part = jnp.max(part.reshape(KEY_CHUNK // 8, 8, block), axis=0)
-            best = part if best is None else jnp.maximum(best, part)
-        most_ref[...] = jnp.broadcast_to(jnp.max(best, axis=0, keepdims=True), (8, block))
-        finish(total, jnp.maximum(i - 1, 0))
+            best = keep(j, score(query, j), best)
+        settle(best)
+        finish(total, i - 1)
         return carry
 
-    lax.fori_loop(0, 2 * count, step, 0)
+    lax.fori_loop(1, 2 * count, step, 0)
     total = None
     for j in range(chunks):
         part = weigh(j, most_ref[0:1, :])
@@ -427,7 +469,7 @@
     other = send(own, across)
     far = [send(piece, swap) for piece in near]
     stream = (me, own, other, near + far)
-    (key_value,) = project(key_value_kernel, [(8, 2 * frame_rows, LANES)], [], *stream)
+    key_value = project_key_value(*stream)
     piece = (frame_rows, LANES)
     queries = project(query_kernel, [piece] * 8, [(8,) + piece], *stream)
     groups = [[2 * z + yl for z in range(8)] for yl in range(2)]

time: 137 us -> 136 us (level)
  Pallas kernels: 39.8 us -> 38 us
    pallas_call x2 -> x1, Pallas kernels: 8.21 us -> 2.71 us  [project(): pl.pallas_call(kernel, out_shape=[jax.ShapeDtypeStruct(shape, jnp.bfloat1...]
    pallas_call x0 -> x1, Pallas kernels: none -> 3.96 us  [project_key_value(): pl.pallas_call(key_value_kernel, out_shape=jax.ShapeDtypeStruct(shape, jn...]
where the time goes in v6:
time: 136 us; the launch traced here: 135 us
  starting transfers between devices  56.4 us (41%)
  Pallas kernels  38 us (28%)
  blocking collectives  20.5 us (15%)
  waiting for transfers between devices  12 us (9%)
  local copies, waits for them, and re-layouts  7.39 us (5%)
    ppermute x18, starting transfers between devices, send(): return lax.ppermute(value, ('blk', 'grp'), pairs)  47.9 us
    pallas_call x2, Pallas kernels, attend(): pl.pallas_call(functools.partial(attend_kernel, pieces), out_shape=jax.Sh...  21.1 us
    all_to_all x1, blocking collectives, body(): mixed = lax.all_to_all(mixed, 'blk', 0, 0, tiled=True)  20.5 us
    ppermute x18, waiting for transfers between devices, send(): return lax.ppermute(value, ('blk', 'grp'), pairs)  12 us
    all_to_all x1, starting transfers between devices, body(): lax.all_to_all(key_value, 'blk', 0, 0, axis_index_groups=groups, tiled=True)  8.48 us
    unnamed x40, local copies, waits for them, and re-layouts  7.25 us
    pallas_call x1, Pallas kernels, convolve_inner(): pl.pallas_call(inner_kernel, out_shape=jax.ShapeDtypeStruct(gated.shape,...  4.1 us
    pallas_call x1, Pallas kernels, project_key_value(): pl.pallas_call(key_value_kernel, out_shape=jax.ShapeDtypeStruct(shape, jn...  3.96 us
  transfers between devices with their start and end apart: 19, of which 4 were waited for; matrix products, arithmetic and copies ran while one was open for 0% of the time, Pallas kernels for 12%

profile of v6, /device:TPU:6, one launch (start us, length us, event | category | flops | bytes accessed | tf_op | source)
XLA Modules:
  0.0 135.0 jit_solution(12425932707838488500)
XLA Ops:
  0.0 1.6 %collective-permute-start.1 = (bf16[192,1024]{1,0:T(8,128)(2,1)}, bf16[192,1024]{1,0:T(8,128)(2,1)S(1)}, u32[]{:S(2)}, u32[]{:S(2)}) collective-permute-start(bf16[192,1024]{1,0:T(8,128)(2,1)} %bitcast.24), channel_id=1, source_target_pairs={{0,0},{1,18},{2,3},{3,17},{4,4},{5,22},{6,7},{7,21},{8,8},{9,26},{... | collective-permute-start | bytes 1179656 | tf_op jit(solution)/shard_map/ppermute | solution.py:45
  1.6 0.8 collective-permute-start.2
  2.5 2.4 %collective-permute-start.3 = (bf16[192,1024]{1,0:T(8,128)(2,1)}, bf16[192,1024]{1,0:T(8,128)(2,1)S(1)}, u32[]{:S(2)}, u32[]{:S(2)}) collective-permute-start(bf16[192,1024]{1,0:T(8,128)(2,1)} %bitcast.26), channel_id=1, source_target_pairs={{0,4},{1,22},{2,7},{3,21},{4,8},{5,26},{6,11},{7,25},{8,12},{9,30}... | collective-permute-start | bytes 1179656 | tf_op jit(solution)/shard_map/ppermute | solution.py:45
  5.3 1.0 copy-done.2
  6.3 0.7 copy-done.12
  7.4 2.5 %collective-permute-start = (bf16[256,1024]{1,0:T(8,128)(2,1)S(1)}, bf16[256,1024]{1,0:T(8,128)(2,1)S(1)}, u32[]{:S(2)}, u32[]{:S(2)}) collective-permute-start(bf16[256,1024]{1,0:T(8,128)(2,1)S(1)} %shard_map.100.own), channel_id=1, source_target_pairs={{0,16},{1,17},{2,18},{3,19},{4,20},{5,21},{6,22},{7,23},{8,24},{9,... | collective-permute-start | bytes 1572872 | tf_op jit(solution)/shard_map/ppermute | solution.py:45
  9.9 11.7 %collective-permute-start.5 = (bf16[192,1024]{1,0:T(8,128)(2,1)S(1)}, bf16[192,1024]{1,0:T(8,128)(2,1)S(1)}, u32[]{:S(2)}, u32[]{:S(2)}) collective-permute-start(bf16[192,1024]{1,0:T(8,128)(2,1)S(1)} %collective-permute-done.1.refs_0_), channel_id=1, source_target_pairs={{0,1},{1,0},{2,3},{3,2},{4,5},{5,4},{6,7},{7,6},{8,9},{9,8},{10,11... | collective-permute-start | bytes 1179656 | tf_op jit(solution)/shard_map/ppermute | solution.py:45
  21.6 3.0 %collective-permute-start.6 = (bf16[192,1024]{1,0:T(8,128)(2,1)S(1)}, bf16[192,1024]{1,0:T(8,128)(2,1)}, u32[]{:S(2)}, u32[]{:S(2)}) collective-permute-start(bf16[192,1024]{1,0:T(8,128)(2,1)S(1)} %collective-permute-done.2.refs_1_), channel_id=1, source_target_pairs={{0,1},{1,0},{2,3},{3,2},{4,5},{5,4},{6,7},{7,6},{8,9},{9,8},{10,11... | collective-permute-start | bytes 1179656 | tf_op jit(solution)/shard_map/ppermute | solution.py:45
  25.2 0.9 collective-permute-done.6.refs_5_
  27.2 4.0 %shard_map.101 = bf16[8,512,128]{2,1,0:T(8,128)(2,1)} custom-call(s32[6]{0:T(128)S(1)} %stack.27.me, bf16[256,1024]{1,0:T(8,128)(2,1)S(1)} %shard_map.100.own, bf16[256,1024]{1,0:T(8,128)(2,1)S(1)} %collective-permute-done.other, bf16[192,1024]{1,0:T(8,128)(2,1)S(1)} %collective-permute-done.1.refs_0_, bf16[192,1024]{1,0:T(8,128)(2,1)S(1)} %collective-permute-done.2.refs_1_, ...), custom_call_target="tpu_custom_call" | custom-call | tf_op jit(solution)/shard_map/pallas_call | solution.py:136
  31.2 8.5 %all-to-all-start = ((bf16[8,512,128]{2,1,0:T(8,128)(2,1)}), bf16[8,512,128]{2,1,0:T(8,128)(2,1)S(1)}, u32[]{:S(2)}, u32[]{:S(2)}) async-start(bf16[8,512,128]{2,1,0:T(8,128)(2,1)} %shard_map.101), calls=%async_computation | async-start | bytes 2097152 | tf_op jit(solution)/shard_map/all_to_all | solution.py:476
  39.7 1.0 copy-done.6
  40.7 1.0 copy-done.8
  41.7 1.0 copy-done.10
  42.7 2.7 %shard_map.102 = (bf16[256,128]{1,0:T(8,128)(2,1)S(1)}, bf16[256,128]{1,0:T(8,128)(2,1)}, bf16[256,128]{1,0:T(8,128)(2,1)S(1)}, bf16[256,128]{1,0:T(8,128)(2,1)S...) custom-call(s32[6]{0:T(128)S(1)} %stack.27.me, ...), custom_call_target="tpu_custom_call" | custom-call | tf_op jit(solution)/shard_map/pallas_call | solution.py:169
  45.4 0.6 copy-done.15
  47.3 0.6 copy-done.18
  47.9 3.2 %collective-permute-start.10 = (bf16[256,128]{1,0:T(8,128)(2,1)}, bf16[256,128]{1,0:T(8,128)(2,1)S(1)}, u32[]{:S(2)}, u32[]{:S(2)}) collective-permute-start(bf16[256,128]{1,0:T(8,128)(2,1)} %get-tuple-element.17), channel_id=1, source_target_pairs={{0,224},{1,225},{2,226},{3,227},{4,228},{5,229},{6,230},{7,231},{8... | collective-permute-start | bytes 196616 | tf_op jit(solution)/shard_map/ppermute | solution.py:45
  51.3 1.7 %collective-permute-start.11 = (bf16[256,128]{1,0:T(8,128)(2,1)}, bf16[256,128]{1,0:T(8,128)(2,1)S(1)}, u32[]{:S(2)}, u32[]{:S(2)}) collective-permute-start(bf16[256,128]{1,0:T(8,128)(2,1)} %copy-done.18), channel_id=1, source_target_pairs={{0,64},{1,65},{2,66},{3,67},{4,68},{5,69},{6,70},{7,71},{8,72},{9,... | collective-permute-start | bytes 196616 | tf_op jit(solution)/shard_map/ppermute | solution.py:45
  53.0 2.4 %collective-permute-start.12 = (bf16[256,128]{1,0:T(8,128)(2,1)}, bf16[256,128]{1,0:T(8,128)(2,1)S(1)}, u32[]{:S(2)}, u32[]{:S(2)}) collective-permute-start(bf16[256,128]{1,0:T(8,128)(2,1)} %copy-done.17), channel_id=1, source_target_pairs={{0,192},{1,193},{2,194},{3,195},{4,196},{5,197},{6,198},{7,199},{8... | collective-permute-start | bytes 196616 | tf_op jit(solution)/shard_map/ppermute | solution.py:45
  55.4 2.6 %collective-permute-start.13 = (bf16[256,128]{1,0:T(8,128)(2,1)}, bf16[256,128]{1,0:T(8,128)(2,1)S(1)}, u32[]{:S(2)}, u32[]{:S(2)}) collective-permute-start(bf16[256,128]{1,0:T(8,128)(2,1)} %copy-done.16), channel_id=1, source_target_pairs={{0,96},{1,97},{2,98},{3,99},{4,100},{5,101},{6,102},{7,103},{8,104... | collective-permute-start | bytes 196616 | tf_op jit(solution)/shard_map/ppermute | solution.py:45
  58.1 10.0 %collective-permute-done.10.refs_2_ = bf16[256,128]{1,0:T(8,128)(2,1)S(1)} collective-permute-done((bf16[256,128]{1,0:T(8,128)(2,1)}, bf16[256,128]{1,0:T(8,128)(2,1)S(1)}, u32[]{:S(2)}, u32[]{:S(2)}) %collective-permute-start.10) | collective-permute-done | bytes 65568 | tf_op jit(solution)/shard_map/ppermute | solution.py:45
  68.1 3.1 %collective-permute-start.14 = (bf16[256,128]{1,0:T(8,128)(2,1)}, bf16[256,128]{1,0:T(8,128)(2,1)S(1)}, u32[]{:S(2)}, u32[]{:S(2)}) collective-permute-start(bf16[256,128]{1,0:T(8,128)(2,1)} %copy-done.15), channel_id=1, source_target_pairs={{0,160},{1,161},{2,162},{3,163},{4,164},{5,165},{6,166},{7,167},{8... | collective-permute-start | bytes 196616 | tf_op jit(solution)/shard_map/ppermute | solution.py:45
  71.2 2.1 %collective-permute-start.15 = (bf16[256,128]{1,0:T(8,128)(2,1)S(1)}, bf16[256,128]{1,0:T(8,128)(2,1)S(1)}, u32[]{:S(2)}, u32[]{:S(2)}) collective-permute-start(bf16[256,128]{1,0:T(8,128)(2,1)S(1)} %get-tuple-element.22), channel_id=1, source_target_pairs={{0,128},{1,129},{2,130},{3,131},{4,132},{5,133},{6,134},{7,135},{8... | collective-permute-start | bytes 196616 | tf_op jit(solution)/shard_map/ppermute | solution.py:45
  73.3 8.4 %shard_map.103.before = bf16[16,64,256]{2,1,0:T(8,128)(2,1)S(1)} custom-call(s32[6]{0:T(128)S(1)} %stack.27.me, s32[8]{0:T(128)S(1)} %bitcast_subtract_fusion.start_ref, s32[8]{0:T(128)S(1)} %bitcast.17, bf16[8,512,128]{2,1,0:T(8,128)(2,1)S(1)} %all-to-all-done.in_ref, bf16[16,64,256]{2,1,0:T(8,128)(2,1)S(1)} %broadcast_in_dim.16.before, ...), custom_call_target="tpu_custom_call" | custom-call | tf_op jit(solution)/shard_map/pallas_call | solution.py:280
  81.8 12.7 %shard_map.104 = bf16[16,64,256]{2,1,0:T(8,128)(2,1)S(1)} custom-call(s32[6]{0:T(128)S(1)} %stack.27.me, s32[8]{0:T(128)S(1)} %bitcast_subtract_fusion.start_ref, s32[8]{0:T(128)S(1)} %bitcast.18, bf16[8,512,128]{2,1,0:T(8,128)(2,1)S(1)} %all-to-all-done.in_ref, bf16[16,64,256]{2,1,0:T(8,128)(2,1)S(1)} %shard_map.103.before, ...), custom_call_target="tpu_custom_call" | custom-call | tf_op jit(solution)/shard_map/pallas_call | solution.py:280
  94.5 20.5 %all_to_all.10.mixed = bf16[16,64,256]{2,1,0:T(8,128)(2,1)S(1)} all-to-all(bf16[16,64,256]{2,1,0:T(8,128)(2,1)S(1)} %shard_map.104), channel_id=1, replica_groups=mesh['blk'=16,'grp'=16] {'blk'}, dimensions={0} | all-to-all | bytes 1048576 | tf_op jit(solution)/shard_map/all_to_all | solution.py:486
  115.1 2.9 %shard_map.105 = (bf16[256,1024]{1,0:T(8,128)(2,1)S(1)}, bf16[256,1024]{1,0:T(8,128)(2,1)S(1)}) custom-call(bf16[16,64,256]{2,1,0:T(8,128)(2,1)S(1)} %all_to_all.10.mixed, bf16[256,1024]{1,0:T(8,128)(2,1)S(1)} %bitcast.16, f32[1,1024]{1,0:T(1,128)S(1)} %bitcast.22, bf16[1024,1024]{1,0:T(8,128)(2,1)S(1)} %copy-done.1, bf16[1024,2048]{1,0:T(8,128)(2,1)S(1)} %copy-done), custom_call_target="tpu_custom_call" | custom-call | tf_op jit(solution)/shard_map/pallas_call | solution.py:324
  118.0 2.2 %collective-permute-start.16 = (bf16[16,1024]{1,0:T(8,128)(2,1)S(1)}, bf16[16,1024]{1,0:T(8,128)(2,1)S(1)}, u32[]{:S(2)}, u32[]{:S(2)}) collective-permute-start(bf16[16,1024]{1,0:T(8,128)(2,1)S(1)} %get-tuple-element.26), channel_id=1, source_target_pairs={{0,16},{1,17},{2,18},{3,19},{4,20},{5,21},{6,22},{7,23},{8,24},{9,... | collective-permute-start | bytes 98312 | tf_op jit(solution)/shard_map/ppermute | solution.py:45
  120.3 7.6 %collective-permute-start.17 = (bf16[16,1024]{1,0:T(8,128)(2,1)S(1)}, bf16[16,1024]{1,0:T(8,128)(2,1)S(1)}, u32[]{:S(2)}, u32[]{:S(2)}) collective-permute-start(bf16[16,1024]{1,0:T(8,128)(2,1)S(1)} %get-tuple-element.25), channel_id=1, source_target_pairs={{1,240},{2,241},{3,242},{4,243},{5,244},{6,245},{7,246},{8,247},{9... | collective-permute-start | bytes 98312 | tf_op jit(solution)/shard_map/ppermute | solution.py:45
  127.8 4.1 %shard_map.106.inner = f32[256,1024]{1,0:T(8,128)S(1)} custom-call(s32[6]{0:T(128)S(1)} %stack.27.me, s32[8]{0:T(128)S(1)} %bitcast_subtract_fusion.start_ref, s32[8]{0:T(128)S(1)} %bitcast.19, bf16[256,1024]{1,0:T(8,128)(2,1)S(1)} %get-tuple-element.23.gated, f32[31,1024]{1,0:T(8,128)S(1)} %copy-done.11), custom_call_target="tpu_custom_call" | custom-call | tf_op jit(solution)/shard_map/pallas_call | solution.py:389
  132.0 2.9 %shard_map.107 = bf16[256,1024]{1,0:T(8,128)(2,1)} custom-call(s32[6]{0:T(128)S(1)} %stack.27.me, s32[8]{0:T(128)S(1)} %bitcast_subtract_fusion.start_ref, s32[8]{0:T(128)S(1)} %bitcast.20, f32[256,1024]{1,0:T(8,128)S(1)} %shard_map.106.inner, bf16[16,1024]{1,0:T(8,128)(2,1)S(1)} %collective-permute-done.16.left, ...), custom_call_target="tpu_custom_call" | custom-call | tf_op jit(solution)/shard_map/pallas_call | solution.py:430
  (60 shorter events, 4.1 us)
Async XLA Ops:
  0.0 9.9 %collective-permute-start.1 = (bf16[192,1024]{1,0:T(8,128)(2,1)}, bf16[192,1024]{1,0:T(8,128)(2,1)S(1)}, u32[]{:S(2)}, u32[]{:S(2)}) collective-permute-start(bf16[192,1024]{1,0:T(8,128)(2,1)} %bitcast.24), channel_id=1, source_target_pairs={{0,0},{1,18},{2,3},{3,17},{4,4},{5,22},{6,7},{7,21},{8,8},{9,26},{... | collective-permute-start | bytes 1179656 | tf_op jit(solution)/shard_map/ppermute | solution.py:45
  1.6 20.0 %collective-permute-start.2 = (bf16[192,1024]{1,0:T(8,128)(2,1)}, bf16[192,1024]{1,0:T(8,128)(2,1)S(1)}, u32[]{:S(2)}, u32[]{:S(2)}) collective-permute-start(bf16[192,1024]{1,0:T(8,128)(2,1)} %bitcast.25), channel_id=1, source_target_pairs={{0,12},{1,30},{2,15},{3,29},{4,0},{5,18},{6,3},{7,17},{8,4},{9,22}... | collective-permute-start | bytes 1179656 | tf_op jit(solution)/shard_map/ppermute | solution.py:45
  2.5 22.1 %collective-permute-start.3 = (bf16[192,1024]{1,0:T(8,128)(2,1)}, bf16[192,1024]{1,0:T(8,128)(2,1)S(1)}, u32[]{:S(2)}, u32[]{:S(2)}) collective-permute-start(bf16[192,1024]{1,0:T(8,128)(2,1)} %bitcast.26), channel_id=1, source_target_pairs={{0,4},{1,22},{2,7},{3,21},{4,8},{5,26},{6,11},{7,25},{8,12},{9,30}... | collective-permute-start | bytes 1179656 | tf_op jit(solution)/shard_map/ppermute | solution.py:45
  4.9 19.8 %collective-permute-start.4 = (bf16[192,1024]{1,0:T(8,128)(2,1)}, bf16[192,1024]{1,0:T(8,128)(2,1)S(1)}, u32[]{:S(2)}, u32[]{:S(2)}) collective-permute-start(bf16[192,1024]{1,0:T(8,128)(2,1)} %bitcast.27), channel_id=1, source_target_pairs={{0,8},{1,26},{2,11},{3,25},{4,12},{5,30},{6,15},{7,29},{8,0},{9,18... | collective-permute-start | bytes 1179656 | tf_op jit(solution)/shard_map/ppermute | solution.py:45
  5.3 1.0 copy-start.2
  7.4 17.8 %collective-permute-start = (bf16[256,1024]{1,0:T(8,128)(2,1)S(1)}, bf16[256,1024]{1,0:T(8,128)(2,1)S(1)}, u32[]{:S(2)}, u32[]{:S(2)}) collective-permute-start(bf16[256,1024]{1,0:T(8,128)(2,1)S(1)} %shard_map.100.own), channel_id=1, source_target_pairs={{0,16},{1,17},{2,18},{3,19},{4,20},{5,21},{6,22},{7,23},{8,24},{9,... | collective-permute-start | bytes 1572872 | tf_op jit(solution)/shard_map/ppermute | solution.py:45
  9.9 15.3 %collective-permute-start.5 = (bf16[192,1024]{1,0:T(8,128)(2,1)S(1)}, bf16[192,1024]{1,0:T(8,128)(2,1)S(1)}, u32[]{:S(2)}, u32[]{:S(2)}) collective-permute-start(bf16[192,1024]{1,0:T(8,128)(2,1)S(1)} %collective-permute-done.1.refs_0_), channel_id=1, source_target_pairs={{0,1},{1,0},{2,3},{3,2},{4,5},{5,4},{6,7},{7,6},{8,9},{9,8},{10,11... | collective-permute-start | bytes 1179656 | tf_op jit(solution)/shard_map/ppermute | solution.py:45
  21.6 4.5 %collective-permute-start.6 = (bf16[192,1024]{1,0:T(8,128)(2,1)S(1)}, bf16[192,1024]{1,0:T(8,128)(2,1)}, u32[]{:S(2)}, u32[]{:S(2)}) collective-permute-start(bf16[192,1024]{1,0:T(8,128)(2,1)S(1)} %collective-permute-done.2.refs_1_), channel_id=1, source_target_pairs={{0,1},{1,0},{2,3},{3,2},{4,5},{5,4},{6,7},{7,6},{8,9},{9,8},{10,11... | collective-permute-start | bytes 1179656 | tf_op jit(solution)/shard_map/ppermute | solution.py:45
  24.6 6.6 %copy-start.5 = (bf16[192,1024]{1,0:T(8,128)(2,1)}, bf16[192,1024]{1,0:T(8,128)(2,1)S(1)}, u32[]{:S(2)}) copy-start(bf16[192,1024]{1,0:T(8,128)(2,1)S(1)} %collective-permute-done.3.refs_2_) | copy-start | bytes 1179652
  24.6 2.0 %collective-permute-start.7 = (bf16[192,1024]{1,0:T(8,128)(2,1)S(1)}, bf16[192,1024]{1,0:T(8,128)(2,1)}, u32[]{:S(2)}, u32[]{:S(2)}) collective-permute-start(bf16[192,1024]{1,0:T(8,128)(2,1)S(1)} %collective-permute-done.3.refs_2_), channel_id=1, source_target_pairs={{0,1},{1,0},{2,3},{3,2},{4,5},{5,4},{6,7},{7,6},{8,9},{9,8},{10,11... | collective-permute-start | bytes 1179656 | tf_op jit(solution)/shard_map/ppermute | solution.py:45
  24.7 6.5 %copy-start.7 = (bf16[192,1024]{1,0:T(8,128)(2,1)}, bf16[192,1024]{1,0:T(8,128)(2,1)S(1)}, u32[]{:S(2)}) copy-start(bf16[192,1024]{1,0:T(8,128)(2,1)S(1)} %collective-permute-done.4.refs_3_) | copy-start | bytes 1179652
  24.7 2.5 %collective-permute-start.8 = (bf16[192,1024]{1,0:T(8,128)(2,1)S(1)}, bf16[192,1024]{1,0:T(8,128)(2,1)}, u32[]{:S(2)}, u32[]{:S(2)}) collective-permute-start(bf16[192,1024]{1,0:T(8,128)(2,1)S(1)} %collective-permute-done.4.refs_3_), channel_id=1, source_target_pairs={{0,1},{1,0},{2,3},{3,2},{4,5},{5,4},{6,7},{7,6},{8,9},{9,8},{10,11... | collective-permute-start | bytes 1179656 | tf_op jit(solution)/shard_map/ppermute | solution.py:45
  25.2 6.0 %copy-start.9 = (bf16[192,1024]{1,0:T(8,128)(2,1)}, bf16[192,1024]{1,0:T(8,128)(2,1)S(1)}, u32[]{:S(2)}) copy-start(bf16[192,1024]{1,0:T(8,128)(2,1)S(1)} %collective-permute-done.5.refs_4_) | copy-start | bytes 1179652
  31.2 42.0 %all-to-all-start = ((bf16[8,512,128]{2,1,0:T(8,128)(2,1)}), bf16[8,512,128]{2,1,0:T(8,128)(2,1)S(1)}, u32[]{:S(2)}, u32[]{:S(2)}) async-start(bf16[8,512,128]{2,1,0:T(8,128)(2,1)} %shard_map.101), calls=%async_computation | async-start | bytes 2097152 | tf_op jit(solution)/shard_map/all_to_all | solution.py:476
  40.7 1.0 copy-start.8
  42.7 8.4 %copy-start.19 = (s32[8]{0:T(128)S(1)}, s32[8]{0:T(128)}, u32[]{:S(2)}) copy-start(s32[8]{0:T(128)} %param.11) | copy-start | bytes 100
  42.7 72.4 %copy-start.3 = (bf16[1,256,1024]{2,1,0:T(8,128)(2,1)S(1)}, bf16[1,256,1024]{2,1,0:T(8,128)(2,1)}, u32[]{:S(2)}) copy-start(bf16[1,256,1024]{2,1,0:T(8,128)(2,1)} %param.10) | copy-start | bytes 1572868
  47.9 20.2 %collective-permute-start.10 = (bf16[256,128]{1,0:T(8,128)(2,1)}, bf16[256,128]{1,0:T(8,128)(2,1)S(1)}, u32[]{:S(2)}, u32[]{:S(2)}) collective-permute-start(bf16[256,128]{1,0:T(8,128)(2,1)} %get-tuple-element.17), channel_id=1, source_target_pairs={{0,224},{1,225},{2,226},{3,227},{4,228},{5,229},{6,230},{7,231},{8... | collective-permute-start | bytes 196616 | tf_op jit(solution)/shard_map/ppermute | solution.py:45
  51.1 20.0 %collective-permute-start.9 = (bf16[256,128]{1,0:T(8,128)(2,1)}, bf16[256,128]{1,0:T(8,128)(2,1)S(1)}, u32[]{:S(2)}, u32[]{:S(2)}) collective-permute-start(bf16[256,128]{1,0:T(8,128)(2,1)} %get-tuple-element.16), channel_id=1, source_target_pairs={{0,32},{1,33},{2,34},{3,35},{4,36},{5,37},{6,38},{7,39},{8,40},{9,... | collective-permute-start | bytes 196616 | tf_op jit(solution)/shard_map/ppermute | solution.py:45
  51.3 30.4 %collective-permute-start.11 = (bf16[256,128]{1,0:T(8,128)(2,1)}, bf16[256,128]{1,0:T(8,128)(2,1)S(1)}, u32[]{:S(2)}, u32[]{:S(2)}) collective-permute-start(bf16[256,128]{1,0:T(8,128)(2,1)} %copy-done.18), channel_id=1, source_target_pairs={{0,64},{1,65},{2,66},{3,67},{4,68},{5,69},{6,70},{7,71},{8,72},{9,... | collective-permute-start | bytes 196616 | tf_op jit(solution)/shard_map/ppermute | solution.py:45
  53.0 28.7 %collective-permute-start.12 = (bf16[256,128]{1,0:T(8,128)(2,1)}, bf16[256,128]{1,0:T(8,128)(2,1)S(1)}, u32[]{:S(2)}, u32[]{:S(2)}) collective-permute-start(bf16[256,128]{1,0:T(8,128)(2,1)} %copy-done.17), channel_id=1, source_target_pairs={{0,192},{1,193},{2,194},{3,195},{4,196},{5,197},{6,198},{7,199},{8... | collective-permute-start | bytes 196616 | tf_op jit(solution)/shard_map/ppermute | solution.py:45
  55.4 26.3 %collective-permute-start.13 = (bf16[256,128]{1,0:T(8,128)(2,1)}, bf16[256,128]{1,0:T(8,128)(2,1)S(1)}, u32[]{:S(2)}, u32[]{:S(2)}) collective-permute-start(bf16[256,128]{1,0:T(8,128)(2,1)} %copy-done.16), channel_id=1, source_target_pairs={{0,96},{1,97},{2,98},{3,99},{4,100},{5,101},{6,102},{7,103},{8,104... | collective-permute-start | bytes 196616 | tf_op jit(solution)/shard_map/ppermute | solution.py:45
  68.1 13.7 %collective-permute-start.14 = (bf16[256,128]{1,0:T(8,128)(2,1)}, bf16[256,128]{1,0:T(8,128)(2,1)S(1)}, u32[]{:S(2)}, u32[]{:S(2)}) collective-permute-start(bf16[256,128]{1,0:T(8,128)(2,1)} %copy-done.15), channel_id=1, source_target_pairs={{0,160},{1,161},{2,162},{3,163},{4,164},{5,165},{6,166},{7,167},{8... | collective-permute-start | bytes 196616 | tf_op jit(solution)/shard_map/ppermute | solution.py:45
  71.2 10.6 %collective-permute-start.15 = (bf16[256,128]{1,0:T(8,128)(2,1)S(1)}, bf16[256,128]{1,0:T(8,128)(2,1)S(1)}, u32[]{:S(2)}, u32[]{:S(2)}) collective-permute-start(bf16[256,128]{1,0:T(8,128)(2,1)S(1)} %get-tuple-element.22), channel_id=1, source_target_pairs={{0,128},{1,129},{2,130},{3,131},{4,132},{5,133},{6,134},{7,135},{8... | collective-permute-start | bytes 196616 | tf_op jit(solution)/shard_map/ppermute | solution.py:45
  73.2 41.8 %copy-start.1 = (bf16[1024,1024]{1,0:T(8,128)(2,1)S(1)}, bf16[1024,1024]{1,0:T(8,128)(2,1)}, u32[]{:S(2)}) copy-start(bf16[1024,1024]{1,0:T(8,128)(2,1)} %w_out_hbm.1) | copy-start | bytes 6291460
  73.3 41.8 %copy-start = (bf16[1024,2048]{1,0:T(8,128)(2,1)S(1)}, bf16[1024,2048]{1,0:T(8,128)(2,1)}, u32[]{:S(2)}) copy-start(bf16[1024,2048]{1,0:T(8,128)(2,1)} %w_glu_hbm.1) | copy-start | bytes 12582916
  81.7 33.3 %copy-start.13 = (f32[1024]{0:T(1024)S(1)}, f32[1024]{0:T(1024)}, u32[]{:S(2)}) copy-start(f32[1024]{0:T(1024)} %param.15) | copy-start | bytes 12292
  115.1 12.8 %copy-start.11 = (f32[31,1024]{1,0:T(8,128)S(1)}, f32[31,1024]{1,0:T(8,128)}, u32[]{:S(2)}) copy-start(f32[31,1024]{1,0:T(8,128)} %weights.3) | copy-start | bytes 380932
  115.1 16.9 %copy-start.4 = (bf16[1024,1024]{1,0:T(8,128)(2,1)S(1)}, bf16[1024,1024]{1,0:T(8,128)(2,1)}, u32[]{:S(2)}) copy-start(bf16[1024,1024]{1,0:T(8,128)(2,1)} %w_proj_hbm.1) | copy-start | bytes 6291460
  115.1 16.9 %copy-start.14 = (f32[1024]{0:T(1024)S(1)}, f32[1024]{0:T(1024)}, u32[]{:S(2)}) copy-start(f32[1024]{0:T(1024)} %param.18) | copy-start | bytes 12292
  118.0 13.9 %collective-permute-start.16 = (bf16[16,1024]{1,0:T(8,128)(2,1)S(1)}, bf16[16,1024]{1,0:T(8,128)(2,1)S(1)}, u32[]{:S(2)}, u32[]{:S(2)}) collective-permute-start(bf16[16,1024]{1,0:T(8,128)(2,1)S(1)} %get-tuple-element.26), channel_id=1, source_target_pairs={{0,16},{1,17},{2,18},{3,19},{4,20},{5,21},{6,22},{7,23},{8,24},{9,... | collective-permute-start | bytes 98312 | tf_op jit(solution)/shard_map/ppermute | solution.py:45
  120.3 11.7 %collective-permute-start.17 = (bf16[16,1024]{1,0:T(8,128)(2,1)S(1)}, bf16[16,1024]{1,0:T(8,128)(2,1)S(1)}, u32[]{:S(2)}, u32[]{:S(2)}) collective-permute-start(bf16[16,1024]{1,0:T(8,128)(2,1)S(1)} %get-tuple-element.25), channel_id=1, source_target_pairs={{1,240},{2,241},{3,242},{4,243},{5,244},{6,245},{7,246},{8,247},{9... | collective-permute-start | bytes 98312 | tf_op jit(solution)/shard_map/ppermute | solution.py:45
  (7 other events, 5.2 us)

commit v7 on v6

--- a/solution.py
+++ b/solution.py
@@ -112,14 +112,14 @@
             for copy in copies:
                 copy.wait()
         heads = [shard_head(me, first + j) for j in range(4)]
-        weights = jnp.concatenate([shard[HEAD : 2 * HEAD, :] for shard in part], axis=0)
+        weights = jnp.concatenate([shard[:HEAD, :] for shard in part], axis=0)
         both = lax.dot_general(stream[...], weights, CONTRACT, preferred_element_type=jnp.float32)
         for j in (0, 2):
             pair = both[:, j * HEAD : (j + 2) * HEAD]
             mine, theirs = pair[:rows], pair[rows:]
             out[first + j, :rows] = jnp.where(low, mine, swap_lanes(theirs)).astype(jnp.bfloat16)
             out[first + j + 1, :rows] = jnp.where(low, swap_lanes(mine), theirs).astype(jnp.bfloat16)
-        weights = jnp.concatenate([shard[2 * HEAD :, :] for shard in part], axis=0)
+        weights = jnp.concatenate([shard[HEAD:, :] for shard in part], axis=0)
         both = lax.dot_general(weights, stream[...], CONTRACT, preferred_element_type=jnp.float32)
         for j in range(4):
             i = first + j
@@ -150,11 +150,11 @@
 
 
 def query_kernel(me, own, other, *refs):
-    shards, pieces, both_rows, staged = refs[:8], refs[8:16], refs[16], refs[17]
+    near, far, pieces, both_rows, staged = refs[:4], refs[4], refs[5:13], refs[13], refs[14]
     rows = own.shape[0]
     both_rows[:rows] = own[...]
     both_rows[rows:] = other[...]
-    weights = jnp.concatenate([shard[:HEAD, :] for shard in shards], axis=0)
+    weights = jnp.concatenate([ref[...] for ref in near] + [far[...]], axis=0)
     both = lax.dot_general(weights, both_rows[...], CONTRACT, preferred_element_type=jnp.float32)
     both = both * (HEAD**-0.5 * LOG2E)
     for i in range(8):
@@ -169,7 +169,7 @@
     return pl.pallas_call(
         kernel,
         out_shape=[jax.ShapeDtypeStruct(shape, jnp.bfloat16) for shape in shapes],
-        in_specs=[SMEM] + [VMEM] * 10,
+        in_specs=[SMEM] + [VMEM] * (2 + len(shards)),
         out_specs=[VMEM] * len(shapes),
         scratch_shapes=[pltpu.VMEM((2 * rows, width), jnp.bfloat16)]
         + [pltpu.VMEM(shape, jnp.bfloat16) for shape in staged],
@@ -464,14 +464,16 @@
 
     swap = lambda x, yh, c, z, yl: (x, yh, 1 - c, z, yl)
     across = lambda x, yh, c, z, yl: (x, yh, c, z, 1 - yl)
-    near = [send(shard, route(o)) for o in OFFSETS]
+    near = [send(shard[HEAD:], route(o)) for o in OFFSETS]
+    near_q = [send(shard[:HEAD], route(o)) for o in OFFSETS]
+    far_q = send(jnp.concatenate(near_q, axis=0), swap)
     own = norm(local_frames, attn_gain[None, :])
     other = send(own, across)
     far = [send(piece, swap) for piece in near]
-    stream = (me, own, other, near + far)
-    key_value = project_key_value(*stream)
+    stream = (me, own, other)
+    key_value = project_key_value(*stream, near + far)
     piece = (frame_rows, LANES)
-    queries = project(query_kernel, [piece] * 8, [(8,) + piece], *stream)
+    queries = project(query_kernel, [piece] * 8, [(8,) + piece], *stream, near_q + [far_q])
     groups = [[2 * z + yl for z in range(8)] for yl in range(2)]
     key_value = lax.all_to_all(key_value, "blk", 0, 0, axis_index_groups=groups, tiled=True)
     queries = list(queries)

time: 136 us -> 137 us (level)
  the two profiles are of different devices: /device:TPU:6 before, /device:TPU:1 now
where the time goes in v7:
time: 137 us; the launch traced here: 135 us
  starting transfers between devices  56.1 us (41%)
  Pallas kernels  35.7 us (26%)
  waiting for transfers between devices  21.5 us (16%)
  blocking collectives  17.3 us (13%)
  local copies, waits for them, and re-layouts  3.8 us (3%)
    ppermute x23, starting transfers between devices, send(): return lax.ppermute(value, ('blk', 'grp'), pairs)  47.9 us
    ppermute x23, waiting for transfers between devices, send(): return lax.ppermute(value, ('blk', 'grp'), pairs)  21.5 us
    pallas_call x2, Pallas kernels, attend(): pl.pallas_call(functools.partial(attend_kernel, pieces), out_shape=jax.Sh...  21.1 us
    all_to_all x1, blocking collectives, body(): mixed = lax.all_to_all(mixed, 'blk', 0, 0, tiled=True)  17.3 us
    all_to_all x1, starting transfers between devices, body(): lax.all_to_all(key_value, 'blk', 0, 0, axis_index_groups=groups, tiled=True)  8.2 us
    pallas_call x1, Pallas kernels, convolve_inner(): pl.pallas_call(inner_kernel, out_shape=jax.ShapeDtypeStruct(gated.shape,...  3.9 us
    pallas_call x1, Pallas kernels, project_key_value(): pl.pallas_call(key_value_kernel, out_shape=jax.ShapeDtypeStruct(shape, jn...  3.19 us
    pallas_call x1, Pallas kernels, gate(): pl.pallas_call(gate_kernel, out_shape=[shape, shape], in_specs=[VMEM] * 3...  2.92 us
  transfers between devices with their start and end apart: 24, of which 8 were waited for; matrix products, arithmetic and copies ran while one was open for 1% of the time, Pallas kernels for 10%

profile of v7, /device:TPU:1, one launch (start us, length us, event | category | flops | bytes accessed | tf_op | source)
XLA Modules:
  0.0 135.1 jit_solution(3857163961553779872)
XLA Ops:
  0.0 1.0 slice.22
  1.0 6.0 %collective-permute-start.1 = (bf16[128,1024]{1,0:T(8,128)(2,1)S(1)}, bf16[128,1024]{1,0:T(8,128)(2,1)S(1)}, u32[]{:S(2)}, u32[]{:S(2)}) collective-permute-start(bf16[128,1024]{1,0:T(8,128)(2,1)S(1)} %slice.22), channel_id=1, source_target_pairs={{0,0},{1,18},{2,3},{3,17},{4,4},{5,22},{6,7},{7,21},{8,8},{9,26},{... | collective-permute-start | bytes 786440 | tf_op jit(solution)/shard_map/ppermute | solution.py:45
  7.0 2.3 %collective-permute-start.2 = (bf16[128,1024]{1,0:T(8,128)(2,1)S(1)}, bf16[128,1024]{1,0:T(8,128)(2,1)S(1)}, u32[]{:S(2)}, u32[]{:S(2)}) collective-permute-start(bf16[128,1024]{1,0:T(8,128)(2,1)S(1)} %slice.22), channel_id=1, source_target_pairs={{0,12},{1,30},{2,15},{3,29},{4,0},{5,18},{6,3},{7,17},{8,4},{9,22}... | collective-permute-start | bytes 786440 | tf_op jit(solution)/shard_map/ppermute | solution.py:45
  9.3 1.0 copy-done.2
  11.9 1.3 collective-permute-start.3
  13.2 2.8 %collective-permute-start.4 = (bf16[128,1024]{1,0:T(8,128)(2,1)S(1)}, bf16[128,1024]{1,0:T(8,128)(2,1)S(1)}, u32[]{:S(2)}, u32[]{:S(2)}) collective-permute-start(bf16[128,1024]{1,0:T(8,128)(2,1)S(1)} %slice.22), channel_id=1, source_target_pairs={{0,8},{1,26},{2,11},{3,25},{4,12},{5,30},{6,15},{7,29},{8,0},{9,18... | collective-permute-start | bytes 786440 | tf_op jit(solution)/shard_map/ppermute | solution.py:45
  16.5 10.3 %collective-permute-done.3.refs_2_ = bf16[128,1024]{1,0:T(8,128)(2,1)S(1)} collective-permute-done((bf16[128,1024]{1,0:T(8,128)(2,1)S(1)}, bf16[128,1024]{1,0:T(8,128)(2,1)S(1)}, u32[]{:S(2)}, u32[]{:S(2)}) %collective-permute-start.3) | collective-permute-done | bytes 262176 | tf_op jit(solution)/shard_map/ppermute | solution.py:45
  27.4 0.9 collective-permute-done.7.refs_6_
  28.7 3.2 %shard_map.101 = bf16[8,512,128]{2,1,0:T(8,128)(2,1)} custom-call(s32[6]{0:T(128)S(1)} %stack.27.me, bf16[256,1024]{1,0:T(8,128)(2,1)S(1)} %shard_map.100.own, bf16[256,1024]{1,0:T(8,128)(2,1)S(1)} %collective-permute-done.other, bf16[128,1024]{1,0:T(8,128)(2,1)S(1)} %collective-permute-done.1.refs_0_, bf16[128,1024]{1,0:T(8,128)(2,1)S(1)} %collective-permute-done.2.refs_1_, ...), custom_call_target="tpu_custom_call" | custom-call | tf_op jit(solution)/shard_map/pallas_call | solution.py:136
  31.9 8.2 %all-to-all-start = ((bf16[8,512,128]{2,1,0:T(8,128)(2,1)}), bf16[8,512,128]{2,1,0:T(8,128)(2,1)S(1)}, u32[]{:S(2)}, u32[]{:S(2)}) async-start(bf16[8,512,128]{2,1,0:T(8,128)(2,1)} %shard_map.101), calls=%async_computation | async-start | bytes 2097152 | tf_op jit(solution)/shard_map/all_to_all | solution.py:478
  40.1 0.9 slice.23
  41.0 5.7 %collective-permute-start.9 = (bf16[64,1024]{1,0:T(8,128)(2,1)S(1)}, bf16[64,1024]{1,0:T(8,128)(2,1)S(1)}, u32[]{:S(2)}, u32[]{:S(2)}) collective-permute-start(bf16[64,1024]{1,0:T(8,128)(2,1)S(1)} %slice.23), channel_id=1, source_target_pairs={{0,0},{1,18},{2,3},{3,17},{4,4},{5,22},{6,7},{7,21},{8,8},{9,26},{... | collective-permute-start | bytes 393224 | tf_op jit(solution)/shard_map/ppermute | solution.py:45
  46.8 3.8 %collective-permute-start.11 = (bf16[64,1024]{1,0:T(8,128)(2,1)S(1)}, bf16[64,1024]{1,0:T(8,128)(2,1)S(1)}, u32[]{:S(2)}, u32[]{:S(2)}) collective-permute-start(bf16[64,1024]{1,0:T(8,128)(2,1)S(1)} %slice.23), channel_id=1, source_target_pairs={{0,4},{1,22},{2,7},{3,21},{4,8},{5,26},{6,11},{7,25},{8,12},{9,30}... | collective-permute-start | bytes 393224 | tf_op jit(solution)/shard_map/ppermute | solution.py:45
  51.4 2.2 %collective-permute-done.10.refs_1_ = bf16[64,1024]{1,0:T(8,128)(2,1)S(1)} collective-permute-done((bf16[64,1024]{1,0:T(8,128)(2,1)S(1)}, bf16[64,1024]{1,0:T(8,128)(2,1)S(1)}, u32[]{:S(2)}, u32[]{:S(2)}) %collective-permute-start.10) | collective-permute-done | bytes 131104 | tf_op jit(solution)/shard_map/ppermute | solution.py:45
  53.6 1.1 collective-permute-done.11.refs_2_
  54.7 4.0 %collective-permute-done.12.refs_3_ = bf16[64,1024]{1,0:T(8,128)(2,1)S(1)} collective-permute-done((bf16[64,1024]{1,0:T(8,128)(2,1)S(1)}, bf16[64,1024]{1,0:T(8,128)(2,1)S(1)}, u32[]{:S(2)}, u32[]{:S(2)}) %collective-permute-start.12) | collective-permute-done | bytes 131104 | tf_op jit(solution)/shard_map/ppermute | solution.py:45
  58.8 1.9 %collective-permute-done.13.refs_4_ = bf16[256,1024]{1,0:T(8,128)(2,1)S(1)} collective-permute-done((bf16[256,1024]{1,0:T(8,128)(2,1)S(1)}, bf16[256,1024]{1,0:T(8,128)(2,1)S(1)}, u32[]{:S(2)}, u32[]{:S(2)}) %collective-permute-start.13) | collective-permute-done | bytes 524320 | tf_op jit(solution)/shard_map/ppermute | solution.py:45
  60.7 1.3 shard_map.102
  62.0 1.8 %collective-permute-start.14 = (bf16[256,128]{1,0:T(8,128)(2,1)S(1)}, bf16[256,128]{1,0:T(8,128)(2,1)S(1)}, u32[]{:S(2)}, u32[]{:S(2)}) collective-permute-start(bf16[256,128]{1,0:T(8,128)(2,1)S(1)} %get-tuple-element.16), channel_id=1, source_target_pairs={{0,32},{1,33},{2,34},{3,35},{4,36},{5,37},{6,38},{7,39},{8,40},{9,... | collective-permute-start | bytes 196616 | tf_op jit(solution)/shard_map/ppermute | solution.py:45
  63.8 1.5 %collective-permute-start.15 = (bf16[256,128]{1,0:T(8,128)(2,1)S(1)}, bf16[256,128]{1,0:T(8,128)(2,1)S(1)}, u32[]{:S(2)}, u32[]{:S(2)}) collective-permute-start(bf16[256,128]{1,0:T(8,128)(2,1)S(1)} %get-tuple-element.17), channel_id=1, source_target_pairs={{0,224},{1,225},{2,226},{3,227},{4,228},{5,229},{6,230},{7,231},{8... | collective-permute-start | bytes 196616 | tf_op jit(solution)/shard_map/ppermute | solution.py:45
  66.4 2.7 %collective-permute-start.17 = (bf16[256,128]{1,0:T(8,128)(2,1)S(1)}, bf16[256,128]{1,0:T(8,128)(2,1)S(1)}, u32[]{:S(2)}, u32[]{:S(2)}) collective-permute-start(bf16[256,128]{1,0:T(8,128)(2,1)S(1)} %get-tuple-element.19), channel_id=1, source_target_pairs={{0,192},{1,193},{2,194},{3,195},{4,196},{5,197},{6,198},{7,199},{8... | collective-permute-start | bytes 196616 | tf_op jit(solution)/shard_map/ppermute | solution.py:45
  69.1 1.6 %collective-permute-start.18 = (bf16[256,128]{1,0:T(8,128)(2,1)S(1)}, bf16[256,128]{1,0:T(8,128)(2,1)S(1)}, u32[]{:S(2)}, u32[]{:S(2)}) collective-permute-start(bf16[256,128]{1,0:T(8,128)(2,1)S(1)} %get-tuple-element.20), channel_id=1, source_target_pairs={{0,96},{1,97},{2,98},{3,99},{4,100},{5,101},{6,102},{7,103},{8,104... | collective-permute-start | bytes 196616 | tf_op jit(solution)/shard_map/ppermute | solution.py:45
  70.7 2.8 %collective-permute-start.19 = (bf16[256,128]{1,0:T(8,128)(2,1)S(1)}, bf16[256,128]{1,0:T(8,128)(2,1)S(1)}, u32[]{:S(2)}, u32[]{:S(2)}) collective-permute-start(bf16[256,128]{1,0:T(8,128)(2,1)S(1)} %get-tuple-element.21), channel_id=1, source_target_pairs={{0,160},{1,161},{2,162},{3,163},{4,164},{5,165},{6,166},{7,167},{8... | collective-permute-start | bytes 196616 | tf_op jit(solution)/shard_map/ppermute | solution.py:45
  73.6 5.2 %collective-permute-start.20 = (bf16[256,128]{1,0:T(8,128)(2,1)S(1)}, bf16[256,128]{1,0:T(8,128)(2,1)S(1)}, u32[]{:S(2)}, u32[]{:S(2)}) collective-permute-start(bf16[256,128]{1,0:T(8,128)(2,1)S(1)} %get-tuple-element.22), channel_id=1, source_target_pairs={{0,128},{1,129},{2,130},{3,131},{4,132},{5,133},{6,134},{7,135},{8... | collective-permute-start | bytes 196616 | tf_op jit(solution)/shard_map/ppermute | solution.py:45
  78.9 8.4 %shard_map.103.before = bf16[16,64,256]{2,1,0:T(8,128)(2,1)S(1)} custom-call(s32[6]{0:T(128)S(1)} %stack.27.me, s32[8]{0:T(128)S(1)} %bitcast_subtract_fusion.start_ref, s32[8]{0:T(128)S(1)} %bitcast.17, bf16[8,512,128]{2,1,0:T(8,128)(2,1)S(1)} %all-to-all-done.in_ref, bf16[16,64,256]{2,1,0:T(8,128)(2,1)S(1)} %broadcast_in_dim.16.before, ...), custom_call_target="tpu_custom_call" | custom-call | tf_op jit(solution)/shard_map/pallas_call | solution.py:280
  87.4 12.7 %shard_map.104 = bf16[16,64,256]{2,1,0:T(8,128)(2,1)S(1)} custom-call(s32[6]{0:T(128)S(1)} %stack.27.me, s32[8]{0:T(128)S(1)} %bitcast_subtract_fusion.start_ref, s32[8]{0:T(128)S(1)} %bitcast.18, bf16[8,512,128]{2,1,0:T(8,128)(2,1)S(1)} %all-to-all-done.in_ref, bf16[16,64,256]{2,1,0:T(8,128)(2,1)S(1)} %shard_map.103.before, ...), custom_call_target="tpu_custom_call" | custom-call | tf_op jit(solution)/shard_map/pallas_call | solution.py:280
  100.1 17.3 %all_to_all.10.mixed = bf16[16,64,256]{2,1,0:T(8,128)(2,1)S(1)} all-to-all(bf16[16,64,256]{2,1,0:T(8,128)(2,1)S(1)} %shard_map.104), channel_id=1, replica_groups=mesh['blk'=16,'grp'=16] {'blk'}, dimensions={0} | all-to-all | bytes 1048576 | tf_op jit(solution)/shard_map/all_to_all | solution.py:488
  117.4 2.9 %shard_map.105 = (bf16[256,1024]{1,0:T(8,128)(2,1)S(1)}, bf16[256,1024]{1,0:T(8,128)(2,1)S(1)}) custom-call(bf16[16,64,256]{2,1,0:T(8,128)(2,1)S(1)} %all_to_all.10.mixed, bf16[256,1024]{1,0:T(8,128)(2,1)S(1)} %bitcast.16, f32[1,1024]{1,0:T(1,128)S(1)} %bitcast.22, bf16[1024,1024]{1,0:T(8,128)(2,1)S(1)} %copy-done.1, bf16[1024,2048]{1,0:T(8,128)(2,1)S(1)} %copy-done), custom_call_target="tpu_custom_call" | custom-call | tf_op jit(solution)/shard_map/pallas_call | solution.py:324
  120.4 1.9 %collective-permute-start.21 = (bf16[16,1024]{1,0:T(8,128)(2,1)S(1)}, bf16[16,1024]{1,0:T(8,128)(2,1)S(1)}, u32[]{:S(2)}, u32[]{:S(2)}) collective-permute-start(bf16[16,1024]{1,0:T(8,128)(2,1)S(1)} %get-tuple-element.26), channel_id=1, source_target_pairs={{0,16},{1,17},{2,18},{3,19},{4,20},{5,21},{6,22},{7,23},{8,24},{9,... | collective-permute-start | bytes 98312 | tf_op jit(solution)/shard_map/ppermute | solution.py:45
  122.3 5.7 %collective-permute-start.22 = (bf16[16,1024]{1,0:T(8,128)(2,1)S(1)}, bf16[16,1024]{1,0:T(8,128)(2,1)S(1)}, u32[]{:S(2)}, u32[]{:S(2)}) collective-permute-start(bf16[16,1024]{1,0:T(8,128)(2,1)S(1)} %get-tuple-element.25), channel_id=1, source_target_pairs={{1,240},{2,241},{3,242},{4,243},{5,244},{6,245},{7,246},{8,247},{9... | collective-permute-start | bytes 98312 | tf_op jit(solution)/shard_map/ppermute | solution.py:45
  128.1 3.9 %shard_map.106.inner = f32[256,1024]{1,0:T(8,128)S(1)} custom-call(s32[6]{0:T(128)S(1)} %stack.27.me, s32[8]{0:T(128)S(1)} %bitcast_subtract_fusion.start_ref, s32[8]{0:T(128)S(1)} %bitcast.19, bf16[256,1024]{1,0:T(8,128)(2,1)S(1)} %get-tuple-element.23.gated, f32[31,1024]{1,0:T(8,128)S(1)} %copy-done.5), custom_call_target="tpu_custom_call" | custom-call | tf_op jit(solution)/shard_map/pallas_call | solution.py:389
  132.0 2.9 %shard_map.107 = bf16[256,1024]{1,0:T(8,128)(2,1)} custom-call(s32[6]{0:T(128)S(1)} %stack.27.me, s32[8]{0:T(128)S(1)} %bitcast_subtract_fusion.start_ref, s32[8]{0:T(128)S(1)} %bitcast.20, f32[256,1024]{1,0:T(8,128)S(1)} %shard_map.106.inner, bf16[16,1024]{1,0:T(8,128)(2,1)S(1)} %collective-permute-done.21.left, ...), custom_call_target="tpu_custom_call" | custom-call | tf_op jit(solution)/shard_map/pallas_call | solution.py:430
  (53 shorter events, 5.2 us)
Async XLA Ops:
  1.0 15.0 %collective-permute-start.1 = (bf16[128,1024]{1,0:T(8,128)(2,1)S(1)}, bf16[128,1024]{1,0:T(8,128)(2,1)S(1)}, u32[]{:S(2)}, u32[]{:S(2)}) collective-permute-start(bf16[128,1024]{1,0:T(8,128)(2,1)S(1)} %slice.22), channel_id=1, source_target_pairs={{0,0},{1,18},{2,3},{3,17},{4,4},{5,22},{6,7},{7,21},{8,8},{9,26},{... | collective-permute-start | bytes 786440 | tf_op jit(solution)/shard_map/ppermute | solution.py:45
  7.0 9.0 %collective-permute-start.2 = (bf16[128,1024]{1,0:T(8,128)(2,1)S(1)}, bf16[128,1024]{1,0:T(8,128)(2,1)S(1)}, u32[]{:S(2)}, u32[]{:S(2)}) collective-permute-start(bf16[128,1024]{1,0:T(8,128)(2,1)S(1)} %slice.22), channel_id=1, source_target_pairs={{0,12},{1,30},{2,15},{3,29},{4,0},{5,18},{6,3},{7,17},{8,4},{9,22}... | collective-permute-start | bytes 786440 | tf_op jit(solution)/shard_map/ppermute | solution.py:45
  11.4 16.0 %collective-permute-start = (bf16[256,1024]{1,0:T(8,128)(2,1)S(1)}, bf16[256,1024]{1,0:T(8,128)(2,1)S(1)}, u32[]{:S(2)}, u32[]{:S(2)}) collective-permute-start(bf16[256,1024]{1,0:T(8,128)(2,1)S(1)} %shard_map.100.own), channel_id=1, source_target_pairs={{0,16},{1,17},{2,18},{3,19},{4,20},{5,21},{6,22},{7,23},{8,24},{9,... | collective-permute-start | bytes 1572872 | tf_op jit(solution)/shard_map/ppermute | solution.py:45
  11.9 14.9 %collective-permute-start.3 = (bf16[128,1024]{1,0:T(8,128)(2,1)S(1)}, bf16[128,1024]{1,0:T(8,128)(2,1)S(1)}, u32[]{:S(2)}, u32[]{:S(2)}) collective-permute-start(bf16[128,1024]{1,0:T(8,128)(2,1)S(1)} %slice.22), channel_id=1, source_target_pairs={{0,4},{1,22},{2,7},{3,21},{4,8},{5,26},{6,11},{7,25},{8,12},{9,30}... | collective-permute-start | bytes 786440 | tf_op jit(solution)/shard_map/ppermute | solution.py:45
  13.2 13.6 %collective-permute-start.4 = (bf16[128,1024]{1,0:T(8,128)(2,1)S(1)}, bf16[128,1024]{1,0:T(8,128)(2,1)S(1)}, u32[]{:S(2)}, u32[]{:S(2)}) collective-permute-start(bf16[128,1024]{1,0:T(8,128)(2,1)S(1)} %slice.22), channel_id=1, source_target_pairs={{0,8},{1,26},{2,11},{3,25},{4,12},{5,30},{6,15},{7,29},{8,0},{9,18... | collective-permute-start | bytes 786440 | tf_op jit(solution)/shard_map/ppermute | solution.py:45
  16.0 11.4 %collective-permute-start.5 = (bf16[128,1024]{1,0:T(8,128)(2,1)S(1)}, bf16[128,1024]{1,0:T(8,128)(2,1)S(1)}, u32[]{:S(2)}, u32[]{:S(2)}) collective-permute-start(bf16[128,1024]{1,0:T(8,128)(2,1)S(1)} %collective-permute-done.1.refs_0_), channel_id=1, source_target_pairs={{0,1},{1,0},{2,3},{3,2},{4,5},{5,4},{6,7},{7,6},{8,9},{9,8},{10,11... | collective-permute-start | bytes 786440 | tf_op jit(solution)/shard_map/ppermute | solution.py:45
  16.0 11.4 %collective-permute-start.6 = (bf16[128,1024]{1,0:T(8,128)(2,1)S(1)}, bf16[128,1024]{1,0:T(8,128)(2,1)S(1)}, u32[]{:S(2)}, u32[]{:S(2)}) collective-permute-start(bf16[128,1024]{1,0:T(8,128)(2,1)S(1)} %collective-permute-done.2.refs_1_), channel_id=1, source_target_pairs={{0,1},{1,0},{2,3},{3,2},{4,5},{5,4},{6,7},{7,6},{8,9},{9,8},{10,11... | collective-permute-start | bytes 786440 | tf_op jit(solution)/shard_map/ppermute | solution.py:45
  26.8 1.5 %collective-permute-start.7 = (bf16[128,1024]{1,0:T(8,128)(2,1)S(1)}, bf16[128,1024]{1,0:T(8,128)(2,1)S(1)}, u32[]{:S(2)}, u32[]{:S(2)}) collective-permute-start(bf16[128,1024]{1,0:T(8,128)(2,1)S(1)} %collective-permute-done.3.refs_2_), channel_id=1, source_target_pairs={{0,1},{1,0},{2,3},{3,2},{4,5},{5,4},{6,7},{7,6},{8,9},{9,8},{10,11... | collective-permute-start | bytes 786440 | tf_op jit(solution)/shard_map/ppermute | solution.py:45
  26.8 1.9 %collective-permute-start.8 = (bf16[128,1024]{1,0:T(8,128)(2,1)S(1)}, bf16[128,1024]{1,0:T(8,128)(2,1)S(1)}, u32[]{:S(2)}, u32[]{:S(2)}) collective-permute-start(bf16[128,1024]{1,0:T(8,128)(2,1)S(1)} %collective-permute-done.4.refs_3_), channel_id=1, source_target_pairs={{0,1},{1,0},{2,3},{3,2},{4,5},{5,4},{6,7},{7,6},{8,9},{9,8},{10,11... | collective-permute-start | bytes 786440 | tf_op jit(solution)/shard_map/ppermute | solution.py:45
  31.9 46.9 %all-to-all-start = ((bf16[8,512,128]{2,1,0:T(8,128)(2,1)}), bf16[8,512,128]{2,1,0:T(8,128)(2,1)S(1)}, u32[]{:S(2)}, u32[]{:S(2)}) async-start(bf16[8,512,128]{2,1,0:T(8,128)(2,1)} %shard_map.101), calls=%async_computation | async-start | bytes 2097152 | tf_op jit(solution)/shard_map/all_to_all | solution.py:478
  40.1 25.2 %copy-start.9 = (s32[8]{0:T(128)S(1)}, s32[8]{0:T(128)}, u32[]{:S(2)}) copy-start(s32[8]{0:T(128)} %param.11) | copy-start | bytes 100
  41.0 10.4 %collective-permute-start.9 = (bf16[64,1024]{1,0:T(8,128)(2,1)S(1)}, bf16[64,1024]{1,0:T(8,128)(2,1)S(1)}, u32[]{:S(2)}, u32[]{:S(2)}) collective-permute-start(bf16[64,1024]{1,0:T(8,128)(2,1)S(1)} %slice.23), channel_id=1, source_target_pairs={{0,0},{1,18},{2,3},{3,17},{4,4},{5,22},{6,7},{7,21},{8,8},{9,26},{... | collective-permute-start | bytes 393224 | tf_op jit(solution)/shard_map/ppermute | solution.py:45
  46.7 6.9 %collective-permute-start.10 = (bf16[64,1024]{1,0:T(8,128)(2,1)S(1)}, bf16[64,1024]{1,0:T(8,128)(2,1)S(1)}, u32[]{:S(2)}, u32[]{:S(2)}) collective-permute-start(bf16[64,1024]{1,0:T(8,128)(2,1)S(1)} %slice.23), channel_id=1, source_target_pairs={{0,12},{1,30},{2,15},{3,29},{4,0},{5,18},{6,3},{7,17},{8,4},{9,22}... | collective-permute-start | bytes 393224 | tf_op jit(solution)/shard_map/ppermute | solution.py:45
  46.8 7.9 %collective-permute-start.11 = (bf16[64,1024]{1,0:T(8,128)(2,1)S(1)}, bf16[64,1024]{1,0:T(8,128)(2,1)S(1)}, u32[]{:S(2)}, u32[]{:S(2)}) collective-permute-start(bf16[64,1024]{1,0:T(8,128)(2,1)S(1)} %slice.23), channel_id=1, source_target_pairs={{0,4},{1,22},{2,7},{3,21},{4,8},{5,26},{6,11},{7,25},{8,12},{9,30}... | collective-permute-start | bytes 393224 | tf_op jit(solution)/shard_map/ppermute | solution.py:45
  50.6 8.0 %collective-permute-start.12 = (bf16[64,1024]{1,0:T(8,128)(2,1)S(1)}, bf16[64,1024]{1,0:T(8,128)(2,1)S(1)}, u32[]{:S(2)}, u32[]{:S(2)}) collective-permute-start(bf16[64,1024]{1,0:T(8,128)(2,1)S(1)} %slice.23), channel_id=1, source_target_pairs={{0,8},{1,26},{2,11},{3,25},{4,12},{5,30},{6,15},{7,29},{8,0},{9,18... | collective-permute-start | bytes 393224 | tf_op jit(solution)/shard_map/ppermute | solution.py:45
  58.7 2.0 %collective-permute-start.13 = (bf16[256,1024]{1,0:T(8,128)(2,1)S(1)}, bf16[256,1024]{1,0:T(8,128)(2,1)S(1)}, u32[]{:S(2)}, u32[]{:S(2)}) collective-permute-start(bf16[256,1024]{1,0:T(8,128)(2,1)S(1)} %pad_maximum_fusion), channel_id=1, source_target_pairs={{0,1},{1,0},{2,3},{3,2},{4,5},{5,4},{6,7},{7,6},{8,9},{9,8},{10,11... | collective-permute-start | bytes 1572872 | tf_op jit(solution)/shard_map/ppermute | solution.py:45
  60.7 56.7 %copy-start.3 = (bf16[1,256,1024]{2,1,0:T(8,128)(2,1)S(1)}, bf16[1,256,1024]{2,1,0:T(8,128)(2,1)}, u32[]{:S(2)}) copy-start(bf16[1,256,1024]{2,1,0:T(8,128)(2,1)} %param.10) | copy-start | bytes 1572868
  62.0 8.7 %collective-permute-start.14 = (bf16[256,128]{1,0:T(8,128)(2,1)S(1)}, bf16[256,128]{1,0:T(8,128)(2,1)S(1)}, u32[]{:S(2)}, u32[]{:S(2)}) collective-permute-start(bf16[256,128]{1,0:T(8,128)(2,1)S(1)} %get-tuple-element.16), channel_id=1, source_target_pairs={{0,32},{1,33},{2,34},{3,35},{4,36},{5,37},{6,38},{7,39},{8,40},{9,... | collective-permute-start | bytes 196616 | tf_op jit(solution)/shard_map/ppermute | solution.py:45
  63.8 9.7 %collective-permute-start.15 = (bf16[256,128]{1,0:T(8,128)(2,1)S(1)}, bf16[256,128]{1,0:T(8,128)(2,1)S(1)}, u32[]{:S(2)}, u32[]{:S(2)}) collective-permute-start(bf16[256,128]{1,0:T(8,128)(2,1)S(1)} %get-tuple-element.17), channel_id=1, source_target_pairs={{0,224},{1,225},{2,226},{3,227},{4,228},{5,229},{6,230},{7,231},{8... | collective-permute-start | bytes 196616 | tf_op jit(solution)/shard_map/ppermute | solution.py:45
  65.5 21.8 %collective-permute-start.16 = (bf16[256,128]{1,0:T(8,128)(2,1)S(1)}, bf16[256,128]{1,0:T(8,128)(2,1)S(1)}, u32[]{:S(2)}, u32[]{:S(2)}) collective-permute-start(bf16[256,128]{1,0:T(8,128)(2,1)S(1)} %get-tuple-element.18), channel_id=1, source_target_pairs={{0,64},{1,65},{2,66},{3,67},{4,68},{5,69},{6,70},{7,71},{8,72},{9,... | collective-permute-start | bytes 196616 | tf_op jit(solution)/shard_map/ppermute | solution.py:45
  66.4 21.0 %collective-permute-start.17 = (bf16[256,128]{1,0:T(8,128)(2,1)S(1)}, bf16[256,128]{1,0:T(8,128)(2,1)S(1)}, u32[]{:S(2)}, u32[]{:S(2)}) collective-permute-start(bf16[256,128]{1,0:T(8,128)(2,1)S(1)} %get-tuple-element.19), channel_id=1, source_target_pairs={{0,192},{1,193},{2,194},{3,195},{4,196},{5,197},{6,198},{7,199},{8... | collective-permute-start | bytes 196616 | tf_op jit(solution)/shard_map/ppermute | solution.py:45
  69.1 18.3 %collective-permute-start.18 = (bf16[256,128]{1,0:T(8,128)(2,1)S(1)}, bf16[256,128]{1,0:T(8,128)(2,1)S(1)}, u32[]{:S(2)}, u32[]{:S(2)}) collective-permute-start(bf16[256,128]{1,0:T(8,128)(2,1)S(1)} %get-tuple-element.20), channel_id=1, source_target_pairs={{0,96},{1,97},{2,98},{3,99},{4,100},{5,101},{6,102},{7,103},{8,104... | collective-permute-start | bytes 196616 | tf_op jit(solution)/shard_map/ppermute | solution.py:45
  70.7 16.6 %collective-permute-start.19 = (bf16[256,128]{1,0:T(8,128)(2,1)S(1)}, bf16[256,128]{1,0:T(8,128)(2,1)S(1)}, u32[]{:S(2)}, u32[]{:S(2)}) collective-permute-start(bf16[256,128]{1,0:T(8,128)(2,1)S(1)} %get-tuple-element.21), channel_id=1, source_target_pairs={{0,160},{1,161},{2,162},{3,163},{4,164},{5,165},{6,166},{7,167},{8... | collective-permute-start | bytes 196616 | tf_op jit(solution)/shard_map/ppermute | solution.py:45
  73.6 13.8 %collective-permute-start.20 = (bf16[256,128]{1,0:T(8,128)(2,1)S(1)}, bf16[256,128]{1,0:T(8,128)(2,1)S(1)}, u32[]{:S(2)}, u32[]{:S(2)}) collective-permute-start(bf16[256,128]{1,0:T(8,128)(2,1)S(1)} %get-tuple-element.22), channel_id=1, source_target_pairs={{0,128},{1,129},{2,130},{3,131},{4,132},{5,133},{6,134},{7,135},{8... | collective-permute-start | bytes 196616 | tf_op jit(solution)/shard_map/ppermute | solution.py:45
  78.8 38.6 %copy-start.1 = (bf16[1024,1024]{1,0:T(8,128)(2,1)S(1)}, bf16[1024,1024]{1,0:T(8,128)(2,1)}, u32[]{:S(2)}) copy-start(bf16[1024,1024]{1,0:T(8,128)(2,1)} %w_out_hbm.1) | copy-start | bytes 6291460
  78.9 38.5 %copy-start = (bf16[1024,2048]{1,0:T(8,128)(2,1)S(1)}, bf16[1024,2048]{1,0:T(8,128)(2,1)}, u32[]{:S(2)}) copy-start(bf16[1024,2048]{1,0:T(8,128)(2,1)} %w_glu_hbm.1) | copy-start | bytes 12582916
  87.3 30.1 %copy-start.7 = (f32[1024]{0:T(1024)S(1)}, f32[1024]{0:T(1024)}, u32[]{:S(2)}) copy-start(f32[1024]{0:T(1024)} %param.15) | copy-start | bytes 12292
  117.4 10.7 %copy-start.5 = (f32[31,1024]{1,0:T(8,128)S(1)}, f32[31,1024]{1,0:T(8,128)}, u32[]{:S(2)}) copy-start(f32[31,1024]{1,0:T(8,128)} %weights.3) | copy-start | bytes 380932
  117.4 14.6 %copy-start.4 = (bf16[1024,1024]{1,0:T(8,128)(2,1)S(1)}, bf16[1024,1024]{1,0:T(8,128)(2,1)}, u32[]{:S(2)}) copy-start(bf16[1024,1024]{1,0:T(8,128)(2,1)} %w_proj_hbm.1) | copy-start | bytes 6291460
  117.4 14.6 %copy-start.8 = (f32[1024]{0:T(1024)S(1)}, f32[1024]{0:T(1024)}, u32[]{:S(2)}) copy-start(f32[1024]{0:T(1024)} %param.18) | copy-start | bytes 12292
  120.4 11.6 %collective-permute-start.21 = (bf16[16,1024]{1,0:T(8,128)(2,1)S(1)}, bf16[16,1024]{1,0:T(8,128)(2,1)S(1)}, u32[]{:S(2)}, u32[]{:S(2)}) collective-permute-start(bf16[16,1024]{1,0:T(8,128)(2,1)S(1)} %get-tuple-element.26), channel_id=1, source_target_pairs={{0,16},{1,17},{2,18},{3,19},{4,20},{5,21},{6,22},{7,23},{8,24},{9,... | collective-permute-start | bytes 98312 | tf_op jit(solution)/shard_map/ppermute | solution.py:45
  122.3 9.7 %collective-permute-start.22 = (bf16[16,1024]{1,0:T(8,128)(2,1)S(1)}, bf16[16,1024]{1,0:T(8,128)(2,1)S(1)}, u32[]{:S(2)}, u32[]{:S(2)}) collective-permute-start(bf16[16,1024]{1,0:T(8,128)(2,1)S(1)} %get-tuple-element.25), channel_id=1, source_target_pairs={{1,240},{2,241},{3,242},{4,243},{5,244},{6,245},{7,246},{8,247},{9... | collective-permute-start | bytes 98312 | tf_op jit(solution)/shard_map/ppermute | solution.py:45
  (2 other events, 1.7 us)
